TPU v7x, 32 devices: a whole 2x2x4 slice. The times are simulated.
32 devices in a mesh: rows: 8 (over y, x, core), hub: 4 (over z).
Axes of the slice: x: 2, y: 2, z: 4, core: 2. Of those that a mesh axis runs over, the one named last changes fastest.
Arguments:
- tail_blocks: float32 [2304, 128, 128], P(('rows', 'hub')), may hold values from -0.21875 to 0.21875
- tail_row: int32 [2304], P(('rows', 'hub')), may hold values from 0 to 15
- tail_owner: int32 [2304, 1], P(('rows', 'hub')), may hold values from 0 to 7; in each aligned block of 72 rows (0 to 71, 72 to 143, ...) at most 27 rows name the same one
- tail_slot: int32 [2304], P(('rows', 'hub')), may hold values from 0 to 63
- hub_blocks: float32 [768, 128, 128], P(('rows', 'hub')), may hold values from -0.21875 to 0.21875
- hub_row: int32 [768], P(('rows', 'hub')), may hold values from 0 to 15
- hub_col: int32 [768], P(('rows', 'hub')), may hold values from 0 to 127
- x_tail: float32 [2048, 128], P(('rows', 'hub')), may hold values from 0 to 0.5
- cost_tail: float32 [2048, 128], P(('rows', 'hub')), may hold values from -6 to 6
- upper_tail: float32 [2048, 128], P(('rows', 'hub')), may hold values from 0.5 to 2
- x_hub: float32 [128, 128], P('hub'), may hold values from 0 to 0.5
- cost_hub: float32 [128, 128], P('hub'), may hold values from -6 to 6
- upper_hub: float32 [128, 128], P('hub'), may hold values from 0.5 to 2
- duals: float32 [512, 128], P(('rows', 'hub')), may hold values from 0 to 1
- demand: float32 [512, 128], P(('rows', 'hub')), may hold values from -6 to 6
Outputs:
- x_tail_out: float32 [2048, 128], P(('rows', 'hub'))
- x_hub_out: float32 [128, 128], P('hub')
- duals_out: float32 [512, 128], P(('rows', 'hub'))
Inputs may be any that keep to these rules, and one draw needn't show every extreme that they name: `tail_owner`: among the blocks of one device no owner is named more than 27 times; on some device one owner is named exactly 27 times.
All inputs are finite; a program needn't handle non-finite values.
Results may differ from a plain program's by a relative error of at most 0.0001.
Values sent between devices are 32-bit elements; how exact they have to be, the bound alone decides.
No kernel may reach another device: no remote copies, remote signals or barrier semaphores. Data moves between devices by JAX's collectives and lax.ppermute only.
A program may use at most 64 MiB of HBM per device.

v0:
```python
import functools

import jax
import jax.numpy as jnp
from jax import lax
from jax.experimental import pallas as pl
from jax.experimental.pallas import tpu as pltpu
from jax.sharding import PartitionSpec as P


ITERS = 3

primal_step = 0.25
dual_step = 0.25

VMEM = pltpu.MemorySpace.VMEM
SMEM = pltpu.MemorySpace.SMEM
HBM = pltpu.MemorySpace.HBM


def eye_mask(width):
    rows = lax.broadcasted_iota(jnp.int32, (width, width), 0)
    return rows == lax.broadcasted_iota(jnp.int32, (width, width), 1)


def adjoint_terms(blocks, block_row, wide, out):
    def step(b, _):
        product = blocks[b] * wide[block_row[b]]
        out[pl.ds(b, 1), :] = jnp.sum(product, axis=0, keepdims=True)
        return 0

    lax.fori_loop(0, blocks.shape[0], step, 0, unroll=8)


def forward_sums(blocks, block_row, extra, start, sums):
    def step(b, _):
        sums[block_row[b]] += blocks[b] * extra[pl.ds(start + b, 1), :]
        return 0

    lax.fori_loop(0, blocks.shape[0], step, 0, unroll=4)


def fill_wide(duals, wide):
    width = duals.shape[1]
    eye = eye_mask(width)
    for r in range(wide.shape[0]):
        spread = jnp.where(eye, duals[r : r + 1, :], 0.0)
        wide[r] = jnp.broadcast_to(jnp.sum(spread, axis=1, keepdims=True), (width, width))


def split_bf16(values, count):
    parts = []
    for _ in range(count):
        parts.append(values.astype(jnp.bfloat16))
        values = values - parts[-1].astype(jnp.float32)
    return parts


def gathered_image(pieces, share, ids, keys, split):
    image = None
    for slot, source in enumerate(pieces):
        picked = [source[at : at + n, :] for at, n in share]
        values = picked[0] if len(picked) == 1 else jnp.concatenate(picked, axis=0)
        count = values.shape[0]
        tiles = -(-count // keys.shape[1])
        match = [keys == ids[slot * tiles + t : slot * tiles + t + 1, :] for t in range(tiles)]
        match = match[0] if tiles == 1 else jnp.concatenate(match, axis=1)
        match = jnp.where(match[:, :count], 1.0, 0.0).astype(jnp.bfloat16)
        for part in split_bf16(values, split):
            term = jnp.dot(match, part, preferred_element_type=jnp.float32)
            image = term if image is None else image + term
    return image


def first_terms(sizes, *refs):
    _, piece, tail_own = sizes
    ins, (payload, state) = refs[:12], refs[12:14]
    wide, blocks, hub_row, hub_col, owner, slot_of, duals, x_hub, cost_hub, upper_hub, sems = refs[14:]
    width = duals.shape[1]
    hub_n, tail_n = blocks.shape[0], owner.shape[0]
    targets = [hub_row, hub_col, owner, slot_of, blocks, duals, x_hub, cost_hub, upper_hub]
    targets += [state.at[pl.ds(i * tail_own, tail_own)] for i in range(3)]
    copies = [pltpu.make_async_copy(a, b, sems.at[i]) for i, (a, b) in enumerate(zip(ins, targets))]
    first = copies.pop(5)
    first.start()
    for copy in copies:
        copy.start()
    first.wait()
    fill_wide(duals, wide)
    for copy in copies:
        copy.wait()
    adjoint_terms(blocks, hub_row, wide, payload)
    mine = lax.axis_index("rows") * piece
    for which, source in enumerate((x_hub, cost_hub, upper_hub)):
        for i in range(piece):
            at = hub_n + which * piece + i
            payload[at : at + 1, :] = source[pl.ds(mine + i, 1), :]
    lane = lax.broadcasted_iota(jnp.int32, (1, width), 1)

    def id_row(count, value):
        row = jnp.full((1, width), -1, jnp.int32)
        for b in range(count):
            row = jnp.where(lane == b, value(b), row)
        return row.astype(jnp.float32)

    at = hub_n + 3 * piece
    payload[at : at + 1, :] = id_row(hub_n, lambda b: hub_col[b])
    payload[at + 1 :, :] = jnp.zeros((payload.shape[0] - at - 1, width), jnp.float32)
    at = 3 * tail_own
    state[at : at + 1, :] = id_row(tail_n, lambda b: owner[b] * tail_own + slot_of[b])
    state[at + 1 :, :] = jnp.zeros((state.shape[0] - at - 1, width), jnp.float32)


def choose(sources, apart, at):
    value = sources[0][at, :]
    for i in range(1, len(sources)):
        value = jnp.where(apart == i, sources[i][at, :], value)
    return value


def slot_order(apart, slots):
    return (apart & 1) * (slots // 2) + (apart >> 1)


def pick_state(tail_own, owner, slot_of, *refs):
    states, (x, cost, upper, keys) = refs[:-4], refs[-4:]
    slots, width = len(states), x.shape[1]
    me = lax.axis_index("rows")

    def step(b, _):
        apart = slot_order(owner[b] ^ me, slots)
        for which, target in enumerate((x, cost, upper)):
            target[pl.ds(b, 1), :] = choose(states, apart, pl.ds(slot_of[b] + which * tail_own, 1))
        key = jnp.full((1, width), owner[b] * tail_own + slot_of[b], jnp.int32)
        keys[pl.ds(b, 1), :] = key.astype(jnp.float32)
        return 0

    lax.fori_loop(0, x.shape[0], step, 0, unroll=8)


def tail_begin(chunk, tail_row_in, blocks_in, duals, out, blocks, wide, tail_row, sems):
    row_copy = pltpu.make_async_copy(tail_row_in, tail_row, sems.at[blocks.shape[0] // chunk])
    row_copy.start()
    copies = []
    for i in range(0, blocks.shape[0], chunk):
        part = pl.ds(i, chunk)
        copies.append(pltpu.make_async_copy(blocks_in.at[part], blocks.at[part], sems.at[i // chunk]))
        copies[-1].start()
    fill_wide(duals, wide)
    row_copy.wait()
    for i, copy in enumerate(copies):
        copy.wait()

        def step(b, _):
            product = blocks[b] * wide[tail_row[b]]
            out[pl.ds(b, 1), :] = jnp.sum(product, axis=0, keepdims=True)
            return 0

        lax.fori_loop(i * chunk, (i + 1) * chunk, step, 0, unroll=4)


def tail_adjoint(tail_row, tail_blocks, wide, tail_out):
    adjoint_terms(tail_blocks, tail_row, wide, tail_out)


def gathered_ids(sizes, states, pieces, ids):
    tail_n, tail_own, hub_n, hub_devs, piece, each = sizes
    slots, width = len(pieces), ids.shape[1]
    tiles = ids.shape[0] // slots
    hub_base = float(slots * tail_own)
    lane = lax.broadcasted_iota(jnp.int32, (1, width), 1)
    for slot in range(slots):
        merged = [jnp.full((1, width), -1.0, jnp.float32)] * tiles
        rows = [(0, tail_n, states[slot][3 * tail_own : 3 * tail_own + 1, :])]
        for z in range(hub_devs):
            at = tail_n + z * each + hub_n + 3 * piece
            rows.append((tail_n + z * hub_n, hub_n, pieces[slot][at : at + 1, :] + hub_base))
        for start, count, row in rows:
            row = pltpu.roll(row, start % width, 1) if start % width else row
            for t in range(tiles):
                here = (lane >= start - t * width) & (lane < start + count - t * width)
                merged[t] = jnp.where(here, row, merged[t])
        for t in range(tiles):
            ids[slot * tiles + t : slot * tiles + t + 1, :] = merged[t]


def share_of(tail_n, hub_n, hub_devs, each):
    if each == hub_n:
        return [(0, tail_n + hub_devs * hub_n)]
    return [(0, tail_n)] + [(tail_n + z * each, hub_n) for z in range(hub_devs)]


def primal_update(image, x, cost, upper):
    x_new = jnp.minimum(jnp.maximum(x - primal_step * (cost - image), 0.0), upper)
    return x_new, 2.0 * x_new - x


def step_kernel(first, last, sizes, *refs):
    tail_n, tail_own, hub_n, hub_own, hub_devs, piece, each, slots = sizes
    refs = list(refs)
    take = lambda n: [refs.pop(0) for _ in range(n)]
    tail_row, hub_row = take(2)
    if first:
        (hub_col,) = take(1)
    tail_blocks, hub_blocks, duals, demand = take(4)
    pieces = take(slots)
    if first:
        states = take(slots)
        picked = take(4)
    else:
        x_in, cost, upper, keys, ids = take(5)
    (duals_out,) = take(1)
    if not last:
        hub_out, wide, x_out = take(3)
    if first:
        cost, upper, keys, ids = take(4)
        x_in = x_out
    sums, extra = take(2)
    width = duals.shape[1]

    if first:
        for target, source in zip((x_in, cost, upper, keys), picked):
            target[:tail_n, :] = source[...]
        me, my_hub = lax.axis_index("rows"), lax.axis_index("hub")

        def pick(b, _):
            col = hub_col[b]
            local = col % hub_own
            apart = slot_order((local // piece) ^ me, slots)
            place = tail_n + ((col // hub_own) ^ my_hub) * each + hub_n + local % piece
            at = pl.ds(tail_n + b, 1)
            for which, target in enumerate((x_in, cost, upper)):
                target[at, :] = choose(pieces, apart, pl.ds(place + which * piece, 1))
            keys[at, :] = jnp.full((1, width), slots * tail_own + col, jnp.int32).astype(jnp.float32)
            return 0

        lax.fori_loop(0, hub_n, pick, 0, unroll=8)
        gathered_ids((tail_n, tail_own, hub_n, hub_devs, piece, each), states, pieces, ids)

    image = gathered_image(pieces, share_of(tail_n, hub_n, hub_devs, each), ids, keys[...], 2)
    x_new, extrapolated = primal_update(image, x_in[...], cost[...], upper[...])
    extra[...] = extrapolated
    if not last:
        x_out[...] = x_new

    eye = eye_mask(width)
    base = duals[...] + dual_step * demand[...]
    for r in range(sums.shape[0]):
        sums[r] = jnp.where(eye, (-1.0 / dual_step) * base[r : r + 1, :], 0.0)
    forward_sums(tail_blocks, tail_row, extra, 0, sums)
    forward_sums(hub_blocks, hub_row, extra, tail_n, sums)
    for r in range(sums.shape[0]):
        total = jnp.sum(sums[r], axis=1, keepdims=True)
        value = jnp.broadcast_to(jnp.maximum(-dual_step * total, 0.0), (width, width))
        if not last:
            wide[r] = value
        duals_out[r : r + 1, :] = jnp.sum(jnp.where(eye, value, 0.0), axis=0, keepdims=True)
    if not last:
        adjoint_terms(hub_blocks, hub_row, wide, hub_out)


def own_kernel(sizes, ids, *refs):
    tail_n, hub_n, hub_devs, each, slots = sizes
    pieces, (x_tail, cost_tail, upper_tail, x_hub, cost_hub, upper_hub, tail_out, hub_out) = refs[:slots], refs[slots:]
    tail_own, width = x_tail.shape
    hub_own = x_hub.shape[0]
    tail_key = lax.broadcasted_iota(jnp.int32, (tail_own, width), 0) + lax.axis_index("rows") * tail_own
    hub_key = lax.broadcasted_iota(jnp.int32, (hub_own, width), 0) + lax.axis_index("hub") * hub_own
    keys = jnp.concatenate([tail_key, hub_key + slots * tail_own], axis=0).astype(jnp.float32)
    image = gathered_image(pieces, share_of(tail_n, hub_n, hub_devs, each), ids, keys, 2)
    tail_out[...] = primal_update(image[:tail_own], x_tail[...], cost_tail[...], upper_tail[...])[0]
    hub_out[...] = primal_update(image[tail_own:], x_hub[...], cost_hub[...], upper_hub[...])[0]


def call(kernel, smem, vmem, outs, scratch, flops, hbm=(), room=32 << 20):
    spec = lambda space, items: [pl.BlockSpec(memory_space=space)] * len(items)
    return pl.pallas_call(
        kernel,
        out_shape=[jax.ShapeDtypeStruct(s, jnp.float32) for s in outs],
        in_specs=spec(HBM, hbm) + spec(SMEM, smem) + spec(VMEM, vmem),
        out_specs=spec(VMEM, outs),
        scratch_shapes=scratch,
        compiler_params=pltpu.CompilerParams(vmem_limit_bytes=(64 << 20) - room),
        cost_estimate=pl.CostEstimate(flops=flops, bytes_accessed=0, transcendentals=0),
    )(*hbm, *smem, *vmem)


def on_device(
    tail_blocks,
    tail_row,
    tail_owner,
    tail_slot,
    hub_blocks,
    hub_row,
    hub_col,
    x_tail,
    cost_tail,
    upper_tail,
    x_hub,
    cost_hub,
    upper_hub,
    duals,
    demand,
):
    row_devs = lax.axis_size("rows")
    hub_devs = lax.axis_size("hub")
    tail_n, width = tail_blocks.shape[0], tail_blocks.shape[2]
    hub_n = hub_blocks.shape[0]
    tail_own = x_tail.shape[0]
    hub_own = x_hub.shape[0]
    row_n = duals.shape[0]
    chips = row_devs // 2
    piece = hub_own // row_devs
    assert row_devs & (row_devs - 1) == 0 and hub_devs & (hub_devs - 1) == 0
    assert piece * row_devs == hub_own and tail_n <= width

    def swap(value, axis, mask):
        count = lax.axis_size(axis)
        return lax.ppermute(value, axis, [(i, i ^ mask) for i in range(count)])

    def over_rows(value):
        near = [value] + [swap(value, "rows", 2 * m) for m in range(1, chips)]
        return near + [swap(part, "rows", 1) for part in near]

    def over_hub(value):
        return [value] + [swap(value, "hub", m) for m in reversed(range(1, hub_devs))][::-1]

    owners = tail_owner[:, 0]
    each = hub_n + -(-(3 * piece + 1) // 8) * 8
    state_n = 3 * tail_own + 8
    f32, i32 = (lambda *s: pltpu.VMEM(s, jnp.float32)), (lambda *s: pltpu.SMEM(s, jnp.int32))
    dma = lambda n: pltpu.SemaphoreType.DMA((n,))
    work = 2 * width * width
    big = (row_n, width, width)

    payload, state = call(
        functools.partial(first_terms, (row_devs, piece, tail_own)),
        (),
        (),
        [(each, width), (state_n, width)],
        [f32(*big), f32(*hub_blocks.shape), i32(hub_n), i32(hub_n), i32(tail_n), i32(tail_n), f32(row_n, width)]
        + [f32(hub_own, width)] * 3
        + [dma(12)],
        hub_n * work,
        (hub_row, hub_col, owners, tail_slot, hub_blocks, duals, x_hub, cost_hub, upper_hub)
        + (x_tail, cost_tail, upper_tail),
        8 << 20,
    )
    states = over_rows(state)
    picked = call(
        functools.partial(pick_state, tail_own),
        (owners, tail_slot),
        tuple(states),
        [(tail_n, width)] * 4,
        [],
        tail_n * width * row_devs,
    )
    own = (x_tail, cost_tail, upper_tail, x_hub, cost_hub, upper_hub)
    share = tail_n + hub_devs * hub_n
    held = (tail_n + hub_n, width)
    for iteration in range(ITERS):
        first, last = iteration == 0, iteration == ITERS - 1
        if first:
            chunk = tail_n // 6 if tail_n % 24 == 0 else tail_n
            tail_terms, tail_held = call(
                functools.partial(tail_begin, chunk),
                (),
                (duals,),
                [(tail_n, width), tail_blocks.shape],
                [f32(*big), i32(tail_n), dma(tail_n // chunk + 1)],
                tail_n * work,
                (tail_row, tail_blocks),
                16 << 20,
            )
        else:
            (tail_terms,) = call(
                tail_adjoint, (tail_row,), (tail_held, wide), [(tail_n, width)], [], tail_n * work
            )
        parts = over_hub(payload)
        pieces = over_rows(jnp.concatenate([tail_terms] + parts, axis=0))
        step_each = each if first else hub_n
        vmem = (tail_held, hub_blocks, duals, demand, *pieces)
        vmem += (*states, *picked) if first else kept
        outs = [(row_n, width)]
        if not last:
            outs += [(hub_n, width), big, held]
        if first:
            outs += [held, held, held, (row_devs * -(-share // width), width)]
        duals, *out = call(
            functools.partial(
                step_kernel,
                first,
                last,
                (tail_n, tail_own, hub_n, hub_own, hub_devs, piece, step_each, row_devs),
            ),
            (tail_row, hub_row) + ((hub_col,) if first else ()),
            vmem,
            outs,
            [f32(*big), f32(*held)],
            (tail_n + hub_n) * work,
        )
        if not last:
            payload, wide, x_all, *rest = out
            kept = (x_all, *(rest if first else kept[1:]))
        x_tail_new, x_hub_new = call(
            functools.partial(own_kernel, (tail_n, hub_n, hub_devs, step_each, row_devs)),
            (),
            (kept[-1], *pieces, *own),
            [(tail_own, width), (hub_own, width)],
            [],
            (tail_own + hub_own) * share * row_devs * width,
        )
        own = (x_tail_new, *own[1:3], x_hub_new, *own[4:])
    return own[0], own[3], duals


def solution(mesh):
    both = ("rows", "hub")
    in_specs = (
        P(both, None, None),
        P(both),
        P(both, None),
        P(both),
        P(both, None, None),
        P(both),
        P(both),
        P(both, None),
        P(both, None),
        P(both, None),
        P("hub", None),
        P("hub", None),
        P("hub", None),
        P(both, None),
        P(both, None),
    )
    out_specs = (P(both, None), P("hub", None), P(both, None))

    return jax.shard_map(on_device, mesh=mesh, in_specs=in_specs, out_specs=out_specs, check_vma=False)
```

profile of v0, /device:TPU:0, one launch (start us, length us, event | category | flops | bytes accessed | tf_op | source)
XLA Modules:
  0.0 70.7 jit_solution(7706723964767410351)
XLA Ops:
  0.7 2.6 %shard_map.167 = (f32[40,128]{1,0:T(8,128)}, f32[200,128]{1,0:T(8,128)}) custom-call(s32[24]{0:T(128)} %refs_1_.7, s32[24]{0:T(128)} %refs_2_.1, s32[72]{0:T(128)} %bitcast.1, s32[72]{0:T(128)} %slot_of.1, f32[24,128,128]{2,1,0:T(8,128)} %refs_3_.5, f32[16,128]{1,0:T(8,128)} %refs_5_.5, f32[32,128]{1,0:T(8,128)} %refs_11_.3, f32[32,128]{1,0:T(8,128)} %refs_12_.5, ...), custom_call_target="tpu_custom_call" | custom-call | flops 786432 | tf_op jit(solution)/shard_map/pallas_call | solution.py:277
  3.3 5.1 %collective-permute-start.2 = (f32[40,128]{1,0:T(8,128)}, f32[40,128]{1,0:T(8,128)S(1)}, u32[]{:S(2)}, u32[]{:S(2)}) collective-permute-start(f32[40,128]{1,0:T(8,128)} %get-tuple-element.31), channel_id=1, source_target_pairs={{0,3},{1,2},{2,1},{3,0},{4,7},{5,6},{6,5},{7,4},{8,11},{9,10},{10,... | collective-permute-start | bytes 61448 | tf_op jit(solution)/shard_map/ppermute | solution.py:319
  8.4 0.0 collective-permute-start.1
  8.4 0.6 collective-permute-start
  9.1 2.6 %collective-permute-start.12 = (f32[200,128]{1,0:T(8,128)}, f32[200,128]{1,0:T(8,128)S(1)}, u32[]{:S(2)}, u32[]{:S(2)}) collective-permute-start(f32[200,128]{1,0:T(8,128)} %get-tuple-element.32.refs_0_.refs_15_), channel_id=1, source_target_pairs={{0,24},{4,28},{8,16},{12,20},{16,8},{20,12},{24,0},{28,4},{1,25},{... | collective-permute-start | bytes 307208 | tf_op jit(solution)/shard_map/ppermute | solution.py:319
  11.6 0.7 copy-done.7
  12.3 0.7 copy-done.10
  13.0 2.6 %shard_map.166 = (f32[72,128]{1,0:T(8,128)S(1)}, f32[72,128,128]{2,1,0:T(8,128)S(1)}) custom-call(s32[72]{0:T(128)S(1)} %copy-done.10, f32[72,128,128]{2,1,0:T(8,128)} %blocks_in.1, f32[16,128]{1,0:T(8,128)S(1)} %copy-done.7), custom_call_target="tpu_custom_call" | custom-call | flops 2359296 | tf_op jit(solution)/shard_map/pallas_call | solution.py:277
  15.6 0.6 collective-permute-start.11
  16.2 0.0 collective-permute-done.1
  16.2 0.4 collective-permute-start.10
  16.6 0.0 collective-permute-done.2
  16.6 2.7 %collective-permute-start.5 = (f32[232,128]{1,0:T(8,128)S(1)}, f32[232,128]{1,0:T(8,128)S(1)}, u32[]{:S(2)}, u32[]{:S(2)}) collective-permute-start(f32[232,128]{1,0:T(8,128)S(1)} %constant_dynamic-update-slice_fusion.refs_7_.refs_0_), channel_id=1, source_target_pairs={{0,24},{4,28},{8,16},{12,20},{16,8},{20,12},{24,0},{28,4},{1,25},{... | collective-permute-start | bytes 356360 | tf_op jit(solution)/shard_map/ppermute | solution.py:319
  19.3 0.5 collective-permute-start.4
  19.8 0.4 collective-permute-start.3
  20.2 0.5 collective-permute-done.11.refs_2_.refs_17_
  20.7 1.1 %collective-permute-done.10.refs_1_.refs_16_ = f32[200,128]{1,0:T(8,128)S(1)} collective-permute-done((f32[200,128]{1,0:T(8,128)S(1)}, f32[200,128]{1,0:T(8,128)S(1)}, u32[]{:S(2)}, u32[]{:S(2)}) %collective-permute-start.10) | collective-permute-done | bytes 102432 | tf_op jit(solution)/shard_map/ppermute | solution.py:319
  21.8 3.6 %collective-permute-done.5.refs_10_.refs_3_ = f32[232,128]{1,0:T(8,128)S(1)} collective-permute-done((f32[232,128]{1,0:T(8,128)S(1)}, f32[232,128]{1,0:T(8,128)S(1)}, u32[]{:S(2)}, u32[]{:S(2)}) %collective-permute-start.5) | collective-permute-done | bytes 118816 | tf_op jit(solution)/shard_map/ppermute | solution.py:319
  25.5 0.0 collective-permute-start.6
  25.5 0.7 collective-permute-done.4.refs_9_.refs_2_
  26.2 0.5 collective-permute-start.8
  26.7 0.1 collective-permute-start.7
  26.7 0.4 collective-permute-start.14
  27.2 1.0 %collective-permute-done.14.refs_5_.refs_20_ = f32[200,128]{1,0:T(8,128)S(1)} collective-permute-done((f32[200,128]{1,0:T(8,128)S(1)}, f32[200,128]{1,0:T(8,128)S(1)}, u32[]{:S(2)}, u32[]{:S(2)}) %collective-permute-start.14) | collective-permute-done | bytes 102432 | tf_op jit(solution)/shard_map/ppermute | solution.py:319
  28.2 2.0 %shard_map.168 = (f32[72,128]{1,0:T(8,128)S(1)}, f32[72,128]{1,0:T(8,128)S(1)}, f32[72,128]{1,0:T(8,128)S(1)}, f32[72,128]{1,0:T(8,128)S(1)}) custom-call(s32[72]{0:T(128)S(1)} %bitcast.2, s32[72]{0:T(128)S(1)} %copy-done.13, f32[200,128]{1,0:T(8,128)S(1)} %copy-done.3, f32[200,128]{1,0:T(8,128)S(1)} %collective-permute-done.10.refs_1_.refs_16_, ...), custom_call_target="tpu_custom_call" | custom-call | flops 73728 | tf_op jit(solution)/shard_map/pallas_call | solution.py:277
  30.2 3.0 %shard_map.169 = (f32[16,128]{1,0:T(8,128)S(1)}, f32[24,128]{1,0:T(8,128)S(1)}, f32[16,128,128]{2,1,0:T(8,128)S(1)}, f32[96,128]{1,0:T(8,128)S(1)}, f32[96,128]{...) custom-call(s32[72]{0:T(128)S(1)} %copy-done.10, s32[24]{0:T(128)S(1)} %copy-done.11, ...), custom_call_target="tpu_custom_call" | custom-call | flops 3145728 | tf_op jit(solution)/shard_map/pallas_call | solution.py:277
  33.2 3.7 %collective-permute-start.19 = (f32[24,128]{1,0:T(8,128)S(1)}, f32[24,128]{1,0:T(8,128)S(1)}, u32[]{:S(2)}, u32[]{:S(2)}) collective-permute-start(f32[24,128]{1,0:T(8,128)S(1)} %get-tuple-element.40), channel_id=1, source_target_pairs={{0,3},{1,2},{2,1},{3,0},{4,7},{5,6},{6,5},{7,4},{8,11},{9,10},{10,... | collective-permute-start | bytes 36872 | tf_op jit(solution)/shard_map/ppermute | solution.py:319
  36.9 0.8 %collective-permute-start.17 = (f32[24,128]{1,0:T(8,128)S(1)}, f32[24,128]{1,0:T(8,128)S(1)}, u32[]{:S(2)}, u32[]{:S(2)}) collective-permute-start(f32[24,128]{1,0:T(8,128)S(1)} %get-tuple-element.40), channel_id=1, source_target_pairs={{0,1},{1,0},{2,3},{3,2},{4,5},{5,4},{6,7},{7,6},{8,9},{9,8},{10,11... | collective-permute-start | bytes 36872 | tf_op jit(solution)/shard_map/ppermute | solution.py:319
  37.7 1.1 %shard_map.170 = f32[72,128]{1,0:T(8,128)S(1)} custom-call(s32[72]{0:T(128)S(1)} %copy-done.10, f32[72,128,128]{2,1,0:T(8,128)S(1)} %get-tuple-element.29.refs_3_.tail_blocks.refs_2_, f32[16,128,128]{2,1,0:T(8,128)S(1)} %get-tuple-element.39.wide), custom_call_target="tpu_custom_call" | custom-call | flops 2359296 | tf_op jit(solution)/shard_map/pallas_call | solution.py:277
  38.8 1.9 %collective-permute-done.17 = f32[24,128]{1,0:T(8,128)S(1)} collective-permute-done((f32[24,128]{1,0:T(8,128)S(1)}, f32[24,128]{1,0:T(8,128)S(1)}, u32[]{:S(2)}, u32[]{:S(2)}) %collective-permute-start.17) | collective-permute-done | bytes 12320 | tf_op jit(solution)/shard_map/ppermute | solution.py:319
  40.7 0.8 %collective-permute-done.18 = f32[24,128]{1,0:T(8,128)S(1)} collective-permute-done((f32[24,128]{1,0:T(8,128)S(1)}, f32[24,128]{1,0:T(8,128)S(1)}, u32[]{:S(2)}, u32[]{:S(2)}) %collective-permute-start.18) | collective-permute-done | bytes 12320 | tf_op jit(solution)/shard_map/ppermute | solution.py:319
  41.5 1.3 %collective-permute-start.22 = (f32[168,128]{1,0:T(8,128)S(1)}, f32[168,128]{1,0:T(8,128)S(1)}, u32[]{:S(2)}, u32[]{:S(2)}) collective-permute-start(f32[168,128]{1,0:T(8,128)S(1)} %constant_dynamic-update-slice_fusion.5.refs_6_.refs_0_), channel_id=1, source_target_pairs={{0,24},{4,28},{8,16},{12,20},{16,8},{20,12},{24,0},{28,4},{1,25},{... | collective-permute-start | bytes 258056 | tf_op jit(solution)/shard_map/ppermute | solution.py:319
  42.8 0.8 %collective-permute-start.21 = (f32[168,128]{1,0:T(8,128)S(1)}, f32[168,128]{1,0:T(8,128)S(1)}, u32[]{:S(2)}, u32[]{:S(2)}) collective-permute-start(f32[168,128]{1,0:T(8,128)S(1)} %constant_dynamic-update-slice_fusion.5.refs_6_.refs_0_), channel_id=1, source_target_pairs={{0,16},{4,20},{8,24},{12,28},{16,0},{20,4},{24,8},{28,12},{1,17},{... | collective-permute-start | bytes 258056 | tf_op jit(solution)/shard_map/ppermute | solution.py:319
  43.6 1.5 %collective-permute-start.20 = (f32[168,128]{1,0:T(8,128)S(1)}, f32[168,128]{1,0:T(8,128)S(1)}, u32[]{:S(2)}, u32[]{:S(2)}) collective-permute-start(f32[168,128]{1,0:T(8,128)S(1)} %constant_dynamic-update-slice_fusion.5.refs_6_.refs_0_), channel_id=1, source_target_pairs={{0,8},{4,12},{8,0},{12,4},{16,24},{20,28},{24,16},{28,20},{1,9},{5... | collective-permute-start | bytes 258056 | tf_op jit(solution)/shard_map/ppermute | solution.py:319
  45.1 2.0 %collective-permute-done.22.refs_9_.refs_3_ = f32[168,128]{1,0:T(8,128)S(1)} collective-permute-done((f32[168,128]{1,0:T(8,128)S(1)}, f32[168,128]{1,0:T(8,128)S(1)}, u32[]{:S(2)}, u32[]{:S(2)}) %collective-permute-start.22) | collective-permute-done | bytes 86048 | tf_op jit(solution)/shard_map/ppermute | solution.py:319
  47.0 0.9 %collective-permute-done.21.refs_8_.refs_2_ = f32[168,128]{1,0:T(8,128)S(1)} collective-permute-done((f32[168,128]{1,0:T(8,128)S(1)}, f32[168,128]{1,0:T(8,128)S(1)}, u32[]{:S(2)}, u32[]{:S(2)}) %collective-permute-start.21) | collective-permute-done | bytes 86048 | tf_op jit(solution)/shard_map/ppermute | solution.py:319
  47.9 0.2 collective-permute-done.20.refs_7_.refs_1_
  48.1 0.3 collective-permute-start.24
  48.4 0.8 %collective-permute-done.25.refs_12_.refs_6_ = f32[168,128]{1,0:T(8,128)S(1)} collective-permute-done((f32[168,128]{1,0:T(8,128)S(1)}, f32[168,128]{1,0:T(8,128)S(1)}, u32[]{:S(2)}, u32[]{:S(2)}) %collective-permute-start.25) | collective-permute-done | bytes 86048 | tf_op jit(solution)/shard_map/ppermute | solution.py:319
  49.2 0.2 collective-permute-done.24.refs_11_.refs_5_
  49.4 2.4 %shard_map.171 = (f32[16,128]{1,0:T(8,128)S(1)}, f32[24,128]{1,0:T(8,128)S(1)}, f32[16,128,128]{2,1,0:T(8,128)S(1)}, f32[96,128]{1,0:T(8,128)S(1)}) custom-call(s32[72]{0:T(128)S(1)} %copy-done.10, s32[24]{0:T(128)S(1)} %copy-done.11, f32[72,128,128]{2,1,0:T(8,128)S(1)} %get-tuple-element.29.refs_3_.tail_blocks.refs_2_, f32[24,128,128]{2,1,0:T(8,128)S(1)} %copy-done, ...), custom_call_target="tpu_custom_call" | custom-call | flops 3145728 | tf_op jit(solution)/shard_map/pallas_call | solution.py:277
  51.8 0.0 copy-start.1
  51.8 0.0 copy-start.2
  51.8 0.0 copy-start.4
  51.8 0.0 copy-start.5
  51.8 0.0 copy-start.6
  51.8 0.0 copy-start.9
  51.9 1.6 %collective-permute-start.29 = (f32[24,128]{1,0:T(8,128)S(1)}, f32[24,128]{1,0:T(8,128)S(1)}, u32[]{:S(2)}, u32[]{:S(2)}) collective-permute-start(f32[24,128]{1,0:T(8,128)S(1)} %get-tuple-element.46), channel_id=1, source_target_pairs={{0,3},{1,2},{2,1},{3,0},{4,7},{5,6},{6,5},{7,4},{8,11},{9,10},{10,... | collective-permute-start | bytes 36872 | tf_op jit(solution)/shard_map/ppermute | solution.py:319
  53.5 0.5 collective-permute-start.28
  54.0 2.3 %collective-permute-start.27 = (f32[24,128]{1,0:T(8,128)S(1)}, f32[24,128]{1,0:T(8,128)S(1)}, u32[]{:S(2)}, u32[]{:S(2)}) collective-permute-start(f32[24,128]{1,0:T(8,128)S(1)} %get-tuple-element.46), channel_id=1, source_target_pairs={{0,1},{1,0},{2,3},{3,2},{4,5},{5,4},{6,7},{7,6},{8,9},{9,8},{10,11... | collective-permute-start | bytes 36872 | tf_op jit(solution)/shard_map/ppermute | solution.py:319
  56.3 1.3 %shard_map.172 = f32[72,128]{1,0:T(8,128)S(1)} custom-call(s32[72]{0:T(128)S(1)} %copy-done.10, f32[72,128,128]{2,1,0:T(8,128)S(1)} %get-tuple-element.29.refs_3_.tail_blocks.refs_2_, f32[16,128,128]{2,1,0:T(8,128)S(1)} %get-tuple-element.45.wide), custom_call_target="tpu_custom_call" | custom-call | flops 2359296 | tf_op jit(solution)/shard_map/pallas_call | solution.py:277
  57.6 0.4 collective-permute-done.27
  58.0 0.1 collective-permute-done.28
  58.1 2.2 %collective-permute-start.32 = (f32[168,128]{1,0:T(8,128)S(1)}, f32[168,128]{1,0:T(8,128)S(1)}, u32[]{:S(2)}, u32[]{:S(2)}) collective-permute-start(f32[168,128]{1,0:T(8,128)S(1)} %constant_dynamic-update-slice_fusion.10.refs_0_.refs_6_), channel_id=1, source_target_pairs={{0,24},{4,28},{8,16},{12,20},{16,8},{20,12},{24,0},{28,4},{1,25},{... | collective-permute-start | bytes 258056 | tf_op jit(solution)/shard_map/ppermute | solution.py:319
  60.3 0.8 %collective-permute-start.31 = (f32[168,128]{1,0:T(8,128)S(1)}, f32[168,128]{1,0:T(8,128)S(1)}, u32[]{:S(2)}, u32[]{:S(2)}) collective-permute-start(f32[168,128]{1,0:T(8,128)S(1)} %constant_dynamic-update-slice_fusion.10.refs_0_.refs_6_), channel_id=1, source_target_pairs={{0,16},{4,20},{8,24},{12,28},{16,0},{20,4},{24,8},{28,12},{1,17},{... | collective-permute-start | bytes 258056 | tf_op jit(solution)/shard_map/ppermute | solution.py:319
  61.1 0.6 collective-permute-start.30
  61.7 2.6 %collective-permute-done.32.refs_3_.refs_9_ = f32[168,128]{1,0:T(8,128)S(1)} collective-permute-done((f32[168,128]{1,0:T(8,128)S(1)}, f32[168,128]{1,0:T(8,128)S(1)}, u32[]{:S(2)}, u32[]{:S(2)}) %collective-permute-start.32) | collective-permute-done | bytes 86048 | tf_op jit(solution)/shard_map/ppermute | solution.py:319
  64.3 0.7 %collective-permute-done.31.refs_2_.refs_8_ = f32[168,128]{1,0:T(8,128)S(1)} collective-permute-done((f32[168,128]{1,0:T(8,128)S(1)}, f32[168,128]{1,0:T(8,128)S(1)}, u32[]{:S(2)}, u32[]{:S(2)}) %collective-permute-start.31) | collective-permute-done | bytes 86048 | tf_op jit(solution)/shard_map/ppermute | solution.py:319
  65.0 0.6 collective-permute-done.30.refs_1_.refs_7_
  65.7 0.4 shard_map.173
  66.1 0.4 shard_map.174
  66.5 0.4 collective-permute-done.34.refs_5_.refs_11_
  66.9 2.8 %shard_map.176 = f32[16,128]{1,0:T(8,128)} custom-call(s32[72]{0:T(128)S(1)} %copy-done.10, s32[24]{0:T(128)S(1)} %copy-done.11, f32[72,128,128]{2,1,0:T(8,128)S(1)} %get-tuple-element.29.refs_3_.tail_blocks.refs_2_, f32[24,128,128]{2,1,0:T(8,128)S(1)} %copy-done, f32[16,128]{1,0:T(8,128)S(1)} %get-tuple-element.53.refs_4_, f32[16,128]{1,0:T(8,128)S(1)} %copy-done.8, ...), custom_call_target="tpu_custom_call" | custom-call | flops 3145728 | tf_op jit(solution)/shard_map/pallas_call | solution.py:277
  69.7 1.0 %shard_map.175 = (f32[64,128]{1,0:T(8,128)}, f32[32,128]{1,0:T(8,128)}) custom-call(f32[16,128]{1,0:T(8,128)S(1)} %get-tuple-element.37.refs_18_.ids, f32[168,128]{1,0:T(8,128)S(1)} %constant_dynamic-update-slice_fusion.10.refs_0_.refs_6_, f32[168,128]{1,0:T(8,128)S(1)} %collective-permute-done.30.refs_1_.refs_7_, ...), custom_call_target="tpu_custom_call" | custom-call | flops 16515072 | tf_op jit(solution)/shard_map/pallas_call | solution.py:277
  (68 shorter events, 0.2 us)
Async XLA Ops:
  0.6 29.6 %copy-start.11 = (s32[24]{0:T(128)S(1)}, s32[24]{0:T(128)}, u32[]{:S(2)}) copy-start(s32[24]{0:T(128)} %refs_1_.7) | copy-start | bytes 292
  0.6 29.6 %copy-start = (f32[24,128,128]{2,1,0:T(8,128)S(1)}, f32[24,128,128]{2,1,0:T(8,128)}, u32[]{:S(2)}) copy-start(f32[24,128,128]{2,1,0:T(8,128)} %refs_3_.5) | copy-start | bytes 4718596
  0.7 29.6 %copy-start.14 = (s32[24]{0:T(128)S(1)}, s32[24]{0:T(128)}, u32[]{:S(2)}) copy-start(s32[24]{0:T(128)} %refs_2_.1) | copy-start | bytes 292
  0.7 27.5 %copy-start.13 = (s32[72]{0:T(128)S(1)}, s32[72]{0:T(128)}, u32[]{:S(2)}) copy-start(s32[72]{0:T(128)} %slot_of.1) | copy-start | bytes 868
  0.7 27.5 %copy-start.12 = (s32[72,1]{0,1:T(1,128)S(1)}, s32[72,1]{0,1:T(1,128)}, u32[]{:S(2)}) copy-start(s32[72,1]{0,1:T(1,128)} %param.17) | copy-start | bytes 868
  0.7 29.5 %copy-start.8 = (f32[16,128]{1,0:T(8,128)S(1)}, f32[16,128]{1,0:T(8,128)}, u32[]{:S(2)}) copy-start(f32[16,128]{1,0:T(8,128)} %refs_5_.7) | copy-start | bytes 24580
  3.3 12.4 %copy-start.3 = (f32[200,128]{1,0:T(8,128)S(1)}, f32[200,128]{1,0:T(8,128)}, u32[]{:S(2)}) copy-start(f32[200,128]{1,0:T(8,128)} %get-tuple-element.32.refs_0_.refs_15_) | copy-start | bytes 307204
  3.3 13.3 %collective-permute-start.2 = (f32[40,128]{1,0:T(8,128)}, f32[40,128]{1,0:T(8,128)S(1)}, u32[]{:S(2)}, u32[]{:S(2)}) collective-permute-start(f32[40,128]{1,0:T(8,128)} %get-tuple-element.31), channel_id=1, source_target_pairs={{0,3},{1,2},{2,1},{3,0},{4,7},{5,6},{6,5},{7,4},{8,11},{9,10},{10,... | collective-permute-start | bytes 61448 | tf_op jit(solution)/shard_map/ppermute | solution.py:319
  8.4 7.8 %collective-permute-start.1 = (f32[40,128]{1,0:T(8,128)}, f32[40,128]{1,0:T(8,128)S(1)}, u32[]{:S(2)}, u32[]{:S(2)}) collective-permute-start(f32[40,128]{1,0:T(8,128)} %get-tuple-element.31), channel_id=1, source_target_pairs={{0,2},{1,3},{2,0},{3,1},{4,6},{5,7},{6,4},{7,5},{8,10},{9,11},{10,... | collective-permute-start | bytes 61448 | tf_op jit(solution)/shard_map/ppermute | solution.py:319
  8.4 7.2 %collective-permute-start = (f32[40,128]{1,0:T(8,128)}, f32[40,128]{1,0:T(8,128)S(1)}, u32[]{:S(2)}, u32[]{:S(2)}) collective-permute-start(f32[40,128]{1,0:T(8,128)} %get-tuple-element.31), channel_id=1, source_target_pairs={{0,1},{1,0},{2,3},{3,2},{4,5},{5,4},{6,7},{7,6},{8,9},{9,8},{10,11... | collective-permute-start | bytes 61448 | tf_op jit(solution)/shard_map/ppermute | solution.py:319
  9.0 10.2 %collective-permute-start.13 = (f32[200,128]{1,0:T(8,128)}, f32[200,128]{1,0:T(8,128)S(1)}, u32[]{:S(2)}, u32[]{:S(2)}) collective-permute-start(f32[200,128]{1,0:T(8,128)} %get-tuple-element.32.refs_0_.refs_15_), channel_id=1, source_target_pairs={{0,4},{4,0},{8,12},{12,8},{16,20},{20,16},{24,28},{28,24},{1,5},{5... | collective-permute-start | bytes 307208 | tf_op jit(solution)/shard_map/ppermute | solution.py:319
  9.1 10.7 %collective-permute-start.12 = (f32[200,128]{1,0:T(8,128)}, f32[200,128]{1,0:T(8,128)S(1)}, u32[]{:S(2)}, u32[]{:S(2)}) collective-permute-start(f32[200,128]{1,0:T(8,128)} %get-tuple-element.32.refs_0_.refs_15_), channel_id=1, source_target_pairs={{0,24},{4,28},{8,16},{12,20},{16,8},{20,12},{24,0},{28,4},{1,25},{... | collective-permute-start | bytes 307208 | tf_op jit(solution)/shard_map/ppermute | solution.py:319
  11.6 0.7 copy-start.7
  12.3 0.7 copy-start.10
  13.0 2.6 %copy-start.15 = (f32[40,128]{1,0:T(8,128)S(1)}, f32[40,128]{1,0:T(8,128)}, u32[]{:S(2)}) copy-start(f32[40,128]{1,0:T(8,128)} %get-tuple-element.31) | copy-start | bytes 61444
  15.6 5.1 %collective-permute-start.11 = (f32[200,128]{1,0:T(8,128)S(1)}, f32[200,128]{1,0:T(8,128)S(1)}, u32[]{:S(2)}, u32[]{:S(2)}) collective-permute-start(f32[200,128]{1,0:T(8,128)S(1)} %copy-done.3), channel_id=1, source_target_pairs={{0,16},{4,20},{8,24},{12,28},{16,0},{20,4},{24,8},{28,12},{1,17},{... | collective-permute-start | bytes 307208 | tf_op jit(solution)/shard_map/ppermute | solution.py:319
  16.2 5.6 %collective-permute-start.10 = (f32[200,128]{1,0:T(8,128)S(1)}, f32[200,128]{1,0:T(8,128)S(1)}, u32[]{:S(2)}, u32[]{:S(2)}) collective-permute-start(f32[200,128]{1,0:T(8,128)S(1)} %copy-done.3), channel_id=1, source_target_pairs={{0,8},{4,12},{8,0},{12,4},{16,24},{20,28},{24,16},{28,20},{1,9},{5... | collective-permute-start | bytes 307208 | tf_op jit(solution)/shard_map/ppermute | solution.py:319
  16.6 8.9 %collective-permute-start.5 = (f32[232,128]{1,0:T(8,128)S(1)}, f32[232,128]{1,0:T(8,128)S(1)}, u32[]{:S(2)}, u32[]{:S(2)}) collective-permute-start(f32[232,128]{1,0:T(8,128)S(1)} %constant_dynamic-update-slice_fusion.refs_7_.refs_0_), channel_id=1, source_target_pairs={{0,24},{4,28},{8,16},{12,20},{16,8},{20,12},{24,0},{28,4},{1,25},{... | collective-permute-start | bytes 356360 | tf_op jit(solution)/shard_map/ppermute | solution.py:319
  19.3 6.9 %collective-permute-start.4 = (f32[232,128]{1,0:T(8,128)S(1)}, f32[232,128]{1,0:T(8,128)S(1)}, u32[]{:S(2)}, u32[]{:S(2)}) collective-permute-start(f32[232,128]{1,0:T(8,128)S(1)} %constant_dynamic-update-slice_fusion.refs_7_.refs_0_), channel_id=1, source_target_pairs={{0,16},{4,20},{8,24},{12,28},{16,0},{20,4},{24,8},{28,12},{1,17},{... | collective-permute-start | bytes 356360 | tf_op jit(solution)/shard_map/ppermute | solution.py:319
  19.8 6.4 %collective-permute-start.3 = (f32[232,128]{1,0:T(8,128)S(1)}, f32[232,128]{1,0:T(8,128)S(1)}, u32[]{:S(2)}, u32[]{:S(2)}) collective-permute-start(f32[232,128]{1,0:T(8,128)S(1)} %constant_dynamic-update-slice_fusion.refs_7_.refs_0_), channel_id=1, source_target_pairs={{0,8},{4,12},{8,0},{12,4},{16,24},{20,28},{24,16},{28,20},{1,9},{5... | collective-permute-start | bytes 356360 | tf_op jit(solution)/shard_map/ppermute | solution.py:319
  20.7 6.0 %collective-permute-start.16 = (f32[200,128]{1,0:T(8,128)S(1)}, f32[200,128]{1,0:T(8,128)S(1)}, u32[]{:S(2)}, u32[]{:S(2)}) collective-permute-start(f32[200,128]{1,0:T(8,128)S(1)} %collective-permute-done.12.refs_3_.refs_18_), channel_id=1, source_target_pairs={{0,4},{4,0},{8,12},{12,8},{16,20},{20,16},{24,28},{28,24},{1,5},{5... | collective-permute-start | bytes 307208 | tf_op jit(solution)/shard_map/ppermute | solution.py:319
  21.8 4.9 %collective-permute-start.15 = (f32[200,128]{1,0:T(8,128)S(1)}, f32[200,128]{1,0:T(8,128)S(1)}, u32[]{:S(2)}, u32[]{:S(2)}) collective-permute-start(f32[200,128]{1,0:T(8,128)S(1)} %collective-permute-done.11.refs_2_.refs_17_), channel_id=1, source_target_pairs={{0,4},{4,0},{8,12},{12,8},{16,20},{20,16},{24,28},{28,24},{1,5},{5... | collective-permute-start | bytes 307208 | tf_op jit(solution)/shard_map/ppermute | solution.py:319
  25.5 4.7 %collective-permute-start.6 = (f32[232,128]{1,0:T(8,128)S(1)}, f32[232,128]{1,0:T(8,128)S(1)}, u32[]{:S(2)}, u32[]{:S(2)}) collective-permute-start(f32[232,128]{1,0:T(8,128)S(1)} %constant_dynamic-update-slice_fusion.refs_7_.refs_0_), channel_id=1, source_target_pairs={{0,4},{4,0},{8,12},{12,8},{16,20},{20,16},{24,28},{28,24},{1,5},{5... | collective-permute-start | bytes 356360 | tf_op jit(solution)/shard_map/ppermute | solution.py:319
  26.2 4.0 %collective-permute-start.9 = (f32[232,128]{1,0:T(8,128)S(1)}, f32[232,128]{1,0:T(8,128)S(1)}, u32[]{:S(2)}, u32[]{:S(2)}) collective-permute-start(f32[232,128]{1,0:T(8,128)S(1)} %collective-permute-done.5.refs_10_.refs_3_), channel_id=1, source_target_pairs={{0,4},{4,0},{8,12},{12,8},{16,20},{20,16},{24,28},{28,24},{1,5},{5... | collective-permute-start | bytes 356360 | tf_op jit(solution)/shard_map/ppermute | solution.py:319
  26.2 4.0 %collective-permute-start.8 = (f32[232,128]{1,0:T(8,128)S(1)}, f32[232,128]{1,0:T(8,128)S(1)}, u32[]{:S(2)}, u32[]{:S(2)}) collective-permute-start(f32[232,128]{1,0:T(8,128)S(1)} %collective-permute-done.4.refs_9_.refs_2_), channel_id=1, source_target_pairs={{0,4},{4,0},{8,12},{12,8},{16,20},{20,16},{24,28},{28,24},{1,5},{5... | collective-permute-start | bytes 356360 | tf_op jit(solution)/shard_map/ppermute | solution.py:319
  26.7 3.5 %collective-permute-start.7 = (f32[232,128]{1,0:T(8,128)S(1)}, f32[232,128]{1,0:T(8,128)S(1)}, u32[]{:S(2)}, u32[]{:S(2)}) collective-permute-start(f32[232,128]{1,0:T(8,128)S(1)} %collective-permute-done.3.refs_8_.refs_1_), channel_id=1, source_target_pairs={{0,4},{4,0},{8,12},{12,8},{16,20},{20,16},{24,28},{28,24},{1,5},{5... | collective-permute-start | bytes 356360 | tf_op jit(solution)/shard_map/ppermute | solution.py:319
  26.7 1.4 %collective-permute-start.14 = (f32[200,128]{1,0:T(8,128)S(1)}, f32[200,128]{1,0:T(8,128)S(1)}, u32[]{:S(2)}, u32[]{:S(2)}) collective-permute-start(f32[200,128]{1,0:T(8,128)S(1)} %collective-permute-done.10.refs_1_.refs_16_), channel_id=1, source_target_pairs={{0,4},{4,0},{8,12},{12,8},{16,20},{20,16},{24,28},{28,24},{1,5},{5... | collective-permute-start | bytes 307208 | tf_op jit(solution)/shard_map/ppermute | solution.py:319
  33.2 8.3 %collective-permute-start.19 = (f32[24,128]{1,0:T(8,128)S(1)}, f32[24,128]{1,0:T(8,128)S(1)}, u32[]{:S(2)}, u32[]{:S(2)}) collective-permute-start(f32[24,128]{1,0:T(8,128)S(1)} %get-tuple-element.40), channel_id=1, source_target_pairs={{0,3},{1,2},{2,1},{3,0},{4,7},{5,6},{6,5},{7,4},{8,11},{9,10},{10,... | collective-permute-start | bytes 36872 | tf_op jit(solution)/shard_map/ppermute | solution.py:319
  36.9 4.6 %collective-permute-start.18 = (f32[24,128]{1,0:T(8,128)S(1)}, f32[24,128]{1,0:T(8,128)S(1)}, u32[]{:S(2)}, u32[]{:S(2)}) collective-permute-start(f32[24,128]{1,0:T(8,128)S(1)} %get-tuple-element.40), channel_id=1, source_target_pairs={{0,2},{1,3},{2,0},{3,1},{4,6},{5,7},{6,4},{7,5},{8,10},{9,11},{10,... | collective-permute-start | bytes 36872 | tf_op jit(solution)/shard_map/ppermute | solution.py:319
  36.9 3.8 %collective-permute-start.17 = (f32[24,128]{1,0:T(8,128)S(1)}, f32[24,128]{1,0:T(8,128)S(1)}, u32[]{:S(2)}, u32[]{:S(2)}) collective-permute-start(f32[24,128]{1,0:T(8,128)S(1)} %get-tuple-element.40), channel_id=1, source_target_pairs={{0,1},{1,0},{2,3},{3,2},{4,5},{5,4},{6,7},{7,6},{8,9},{9,8},{10,11... | collective-permute-start | bytes 36872 | tf_op jit(solution)/shard_map/ppermute | solution.py:319
  41.5 5.5 %collective-permute-start.22 = (f32[168,128]{1,0:T(8,128)S(1)}, f32[168,128]{1,0:T(8,128)S(1)}, u32[]{:S(2)}, u32[]{:S(2)}) collective-permute-start(f32[168,128]{1,0:T(8,128)S(1)} %constant_dynamic-update-slice_fusion.5.refs_6_.refs_0_), channel_id=1, source_target_pairs={{0,24},{4,28},{8,16},{12,20},{16,8},{20,12},{24,0},{28,4},{1,25},{... | collective-permute-start | bytes 258056 | tf_op jit(solution)/shard_map/ppermute | solution.py:319
  42.8 5.1 %collective-permute-start.21 = (f32[168,128]{1,0:T(8,128)S(1)}, f32[168,128]{1,0:T(8,128)S(1)}, u32[]{:S(2)}, u32[]{:S(2)}) collective-permute-start(f32[168,128]{1,0:T(8,128)S(1)} %constant_dynamic-update-slice_fusion.5.refs_6_.refs_0_), channel_id=1, source_target_pairs={{0,16},{4,20},{8,24},{12,28},{16,0},{20,4},{24,8},{28,12},{1,17},{... | collective-permute-start | bytes 258056 | tf_op jit(solution)/shard_map/ppermute | solution.py:319
  43.6 4.5 %collective-permute-start.20 = (f32[168,128]{1,0:T(8,128)S(1)}, f32[168,128]{1,0:T(8,128)S(1)}, u32[]{:S(2)}, u32[]{:S(2)}) collective-permute-start(f32[168,128]{1,0:T(8,128)S(1)} %constant_dynamic-update-slice_fusion.5.refs_6_.refs_0_), channel_id=1, source_target_pairs={{0,8},{4,12},{8,0},{12,4},{16,24},{20,28},{24,16},{28,20},{1,9},{5... | collective-permute-start | bytes 258056 | tf_op jit(solution)/shard_map/ppermute | solution.py:319
  45.1 3.3 %collective-permute-start.23 = (f32[168,128]{1,0:T(8,128)S(1)}, f32[168,128]{1,0:T(8,128)S(1)}, u32[]{:S(2)}, u32[]{:S(2)}) collective-permute-start(f32[168,128]{1,0:T(8,128)S(1)} %constant_dynamic-update-slice_fusion.5.refs_6_.refs_0_), channel_id=1, source_target_pairs={{0,4},{4,0},{8,12},{12,8},{16,20},{20,16},{24,28},{28,24},{1,5},{5... | collective-permute-start | bytes 258056 | tf_op jit(solution)/shard_map/ppermute | solution.py:319
  47.0 1.4 %collective-permute-start.26 = (f32[168,128]{1,0:T(8,128)S(1)}, f32[168,128]{1,0:T(8,128)S(1)}, u32[]{:S(2)}, u32[]{:S(2)}) collective-permute-start(f32[168,128]{1,0:T(8,128)S(1)} %collective-permute-done.22.refs_9_.refs_3_), channel_id=1, source_target_pairs={{0,4},{4,0},{8,12},{12,8},{16,20},{20,16},{24,28},{28,24},{1,5},{5... | collective-permute-start | bytes 258056 | tf_op jit(solution)/shard_map/ppermute | solution.py:319
  47.9 1.3 %collective-permute-start.25 = (f32[168,128]{1,0:T(8,128)S(1)}, f32[168,128]{1,0:T(8,128)S(1)}, u32[]{:S(2)}, u32[]{:S(2)}) collective-permute-start(f32[168,128]{1,0:T(8,128)S(1)} %collective-permute-done.21.refs_8_.refs_2_), channel_id=1, source_target_pairs={{0,4},{4,0},{8,12},{12,8},{16,20},{20,16},{24,28},{28,24},{1,5},{5... | collective-permute-start | bytes 258056 | tf_op jit(solution)/shard_map/ppermute | solution.py:319
  48.1 1.3 %collective-permute-start.24 = (f32[168,128]{1,0:T(8,128)S(1)}, f32[168,128]{1,0:T(8,128)S(1)}, u32[]{:S(2)}, u32[]{:S(2)}) collective-permute-start(f32[168,128]{1,0:T(8,128)S(1)} %collective-permute-done.20.refs_7_.refs_1_), channel_id=1, source_target_pairs={{0,4},{4,0},{8,12},{12,8},{16,20},{20,16},{24,28},{28,24},{1,5},{5... | collective-permute-start | bytes 258056 | tf_op jit(solution)/shard_map/ppermute | solution.py:319
  51.8 13.8 %copy-start.1 = (f32[64,128]{1,0:T(8,128)S(1)}, f32[64,128]{1,0:T(8,128)}, u32[]{:S(2)}) copy-start(f32[64,128]{1,0:T(8,128)} %refs_9_.7) | copy-start | bytes 98308
  51.8 13.8 %copy-start.2 = (f32[64,128]{1,0:T(8,128)S(1)}, f32[64,128]{1,0:T(8,128)}, u32[]{:S(2)}) copy-start(f32[64,128]{1,0:T(8,128)} %refs_10_.7) | copy-start | bytes 98308
  51.8 13.8 %copy-start.4 = (f32[32,128]{1,0:T(8,128)S(1)}, f32[32,128]{1,0:T(8,128)}, u32[]{:S(2)}) copy-start(f32[32,128]{1,0:T(8,128)} %refs_12_.5) | copy-start | bytes 49156
  51.8 13.8 %copy-start.5 = (f32[32,128]{1,0:T(8,128)S(1)}, f32[32,128]{1,0:T(8,128)}, u32[]{:S(2)}) copy-start(f32[32,128]{1,0:T(8,128)} %refs_13_.5) | copy-start | bytes 49156
  51.8 13.8 %copy-start.6 = (f32[64,128]{1,0:T(8,128)S(1)}, f32[64,128]{1,0:T(8,128)}, u32[]{:S(2)}) copy-start(f32[64,128]{1,0:T(8,128)} %refs_8_.3) | copy-start | bytes 98308
  51.8 13.8 %copy-start.9 = (f32[32,128]{1,0:T(8,128)S(1)}, f32[32,128]{1,0:T(8,128)}, u32[]{:S(2)}) copy-start(f32[32,128]{1,0:T(8,128)} %refs_11_.3) | copy-start | bytes 49156
  51.9 6.3 %collective-permute-start.29 = (f32[24,128]{1,0:T(8,128)S(1)}, f32[24,128]{1,0:T(8,128)S(1)}, u32[]{:S(2)}, u32[]{:S(2)}) collective-permute-start(f32[24,128]{1,0:T(8,128)S(1)} %get-tuple-element.46), channel_id=1, source_target_pairs={{0,3},{1,2},{2,1},{3,0},{4,7},{5,6},{6,5},{7,4},{8,11},{9,10},{10,... | collective-permute-start | bytes 36872 | tf_op jit(solution)/shard_map/ppermute | solution.py:319
  53.5 4.6 %collective-permute-start.28 = (f32[24,128]{1,0:T(8,128)S(1)}, f32[24,128]{1,0:T(8,128)S(1)}, u32[]{:S(2)}, u32[]{:S(2)}) collective-permute-start(f32[24,128]{1,0:T(8,128)S(1)} %get-tuple-element.46), channel_id=1, source_target_pairs={{0,2},{1,3},{2,0},{3,1},{4,6},{5,7},{6,4},{7,5},{8,10},{9,11},{10,... | collective-permute-start | bytes 36872 | tf_op jit(solution)/shard_map/ppermute | solution.py:319
  54.0 4.0 %collective-permute-start.27 = (f32[24,128]{1,0:T(8,128)S(1)}, f32[24,128]{1,0:T(8,128)S(1)}, u32[]{:S(2)}, u32[]{:S(2)}) collective-permute-start(f32[24,128]{1,0:T(8,128)S(1)} %get-tuple-element.46), channel_id=1, source_target_pairs={{0,1},{1,0},{2,3},{3,2},{4,5},{5,4},{6,7},{7,6},{8,9},{9,8},{10,11... | collective-permute-start | bytes 36872 | tf_op jit(solution)/shard_map/ppermute | solution.py:319
  58.1 6.2 %collective-permute-start.32 = (f32[168,128]{1,0:T(8,128)S(1)}, f32[168,128]{1,0:T(8,128)S(1)}, u32[]{:S(2)}, u32[]{:S(2)}) collective-permute-start(f32[168,128]{1,0:T(8,128)S(1)} %constant_dynamic-update-slice_fusion.10.refs_0_.refs_6_), channel_id=1, source_target_pairs={{0,24},{4,28},{8,16},{12,20},{16,8},{20,12},{24,0},{28,4},{1,25},{... | collective-permute-start | bytes 258056 | tf_op jit(solution)/shard_map/ppermute | solution.py:319
  60.3 4.7 %collective-permute-start.31 = (f32[168,128]{1,0:T(8,128)S(1)}, f32[168,128]{1,0:T(8,128)S(1)}, u32[]{:S(2)}, u32[]{:S(2)}) collective-permute-start(f32[168,128]{1,0:T(8,128)S(1)} %constant_dynamic-update-slice_fusion.10.refs_0_.refs_6_), channel_id=1, source_target_pairs={{0,16},{4,20},{8,24},{12,28},{16,0},{20,4},{24,8},{28,12},{1,17},{... | collective-permute-start | bytes 258056 | tf_op jit(solution)/shard_map/ppermute | solution.py:319
  61.1 4.5 %collective-permute-start.30 = (f32[168,128]{1,0:T(8,128)S(1)}, f32[168,128]{1,0:T(8,128)S(1)}, u32[]{:S(2)}, u32[]{:S(2)}) collective-permute-start(f32[168,128]{1,0:T(8,128)S(1)} %constant_dynamic-update-slice_fusion.10.refs_0_.refs_6_), channel_id=1, source_target_pairs={{0,8},{4,12},{8,0},{12,4},{16,24},{20,28},{24,16},{28,20},{1,9},{5... | collective-permute-start | bytes 258056 | tf_op jit(solution)/shard_map/ppermute | solution.py:319
  61.7 4.8 %collective-permute-start.33 = (f32[168,128]{1,0:T(8,128)S(1)}, f32[168,128]{1,0:T(8,128)S(1)}, u32[]{:S(2)}, u32[]{:S(2)}) collective-permute-start(f32[168,128]{1,0:T(8,128)S(1)} %constant_dynamic-update-slice_fusion.10.refs_0_.refs_6_), channel_id=1, source_target_pairs={{0,4},{4,0},{8,12},{12,8},{16,20},{20,16},{24,28},{28,24},{1,5},{5... | collective-permute-start | bytes 258056 | tf_op jit(solution)/shard_map/ppermute | solution.py:319
  64.3 2.2 %collective-permute-start.36 = (f32[168,128]{1,0:T(8,128)S(1)}, f32[168,128]{1,0:T(8,128)S(1)}, u32[]{:S(2)}, u32[]{:S(2)}) collective-permute-start(f32[168,128]{1,0:T(8,128)S(1)} %collective-permute-done.32.refs_3_.refs_9_), channel_id=1, source_target_pairs={{0,4},{4,0},{8,12},{12,8},{16,20},{20,16},{24,28},{28,24},{1,5},{5... | collective-permute-start | bytes 258056 | tf_op jit(solution)/shard_map/ppermute | solution.py:319
  65.0 1.4 %collective-permute-start.35 = (f32[168,128]{1,0:T(8,128)S(1)}, f32[168,128]{1,0:T(8,128)S(1)}, u32[]{:S(2)}, u32[]{:S(2)}) collective-permute-start(f32[168,128]{1,0:T(8,128)S(1)} %collective-permute-done.31.refs_2_.refs_8_), channel_id=1, source_target_pairs={{0,4},{4,0},{8,12},{12,8},{16,20},{20,16},{24,28},{28,24},{1,5},{5... | collective-permute-start | bytes 258056 | tf_op jit(solution)/shard_map/ppermute | solution.py:319
  65.6 1.3 %collective-permute-start.34 = (f32[168,128]{1,0:T(8,128)S(1)}, f32[168,128]{1,0:T(8,128)S(1)}, u32[]{:S(2)}, u32[]{:S(2)}) collective-permute-start(f32[168,128]{1,0:T(8,128)S(1)} %collective-permute-done.30.refs_1_.refs_7_), channel_id=1, source_target_pairs={{0,4},{4,0},{8,12},{12,8},{16,20},{20,16},{24,28},{28,24},{1,5},{5... | collective-permute-start | bytes 258056 | tf_op jit(solution)/shard_map/ppermute | solution.py:319
where the time goes:
time: 70.9 us; the launch traced here: 70.7 us
  starting transfers between devices  30.3 us (43%)
  Pallas kernels  19.4 us (27%)
  waiting for transfers between devices  18.5 us (26%)
  local copies, waits for them, and re-layouts  1.47 us (2%)
  between operations  1.03 us (1%)
    ppermute x37, starting transfers between devices, swap(): return lax.ppermute(value, axis, [(i, i ^ mask) for i in range(count)])  30.3 us
    pallas_call x11, Pallas kernels, call(): pl.pallas_call(kernel, out_shape=[jax.ShapeDtypeStruct(s, jnp.float32) fo...  19.4 us
    ppermute x37, waiting for transfers between devices, swap(): return lax.ppermute(value, axis, [(i, i ^ mask) for i in range(count)])  18.5 us
    unnamed x44, local copies, waits for them, and re-layouts  1.46 us
  transfers between devices with their start and end apart: 37, of which 18 were waited for; matrix products, arithmetic and copies ran while one was open for 0% of the time, Pallas kernels for 11%

commit v1 on v0

v1 whole, which is shorter than its diff:
```python
import functools

import jax
import jax.numpy as jnp
from jax import lax
from jax.experimental import pallas as pl
from jax.experimental.pallas import tpu as pltpu
from jax.sharding import PartitionSpec as P


ITERS = 3

PARTS = 4

primal_step = 0.25
dual_step = 0.25

SEED_FLOPS = 10**10

VMEM = pltpu.MemorySpace.VMEM


def eye_mask(width):
    rows = lax.broadcasted_iota(jnp.int32, (width, width), 0)
    return rows == lax.broadcasted_iota(jnp.int32, (width, width), 1)


def adjoint_terms(blocks, block_row, wide, out):
    def step(b, _):
        product = blocks[b] * wide[block_row[b]]
        out[pl.ds(b, 1), :] = jnp.sum(product, axis=0, keepdims=True)
        return 0

    lax.fori_loop(0, blocks.shape[0], step, 0, unroll=8)


def forward_sums(blocks, block_row, extra, start, sums):
    part = blocks.shape[1] // len(sums)

    def step(b, _):
        row = block_row[b]
        scale = extra[pl.ds(start + b, 1), :]
        for q, total in enumerate(sums):
            total[row] += blocks[b, q * part : (q + 1) * part, :] * scale
        return 0

    lax.fori_loop(0, blocks.shape[0], step, 0, unroll=4)


def fill_wide(duals, wide):
    width = duals.shape[1]
    eye = eye_mask(width)
    for r in range(wide.shape[0]):
        spread = jnp.where(eye, duals[r : r + 1, :], 0.0)
        wide[r] = jnp.broadcast_to(jnp.sum(spread, axis=1, keepdims=True), (width, width))


def split_bf16(values, count):
    parts = []
    for _ in range(count):
        parts.append(values.astype(jnp.bfloat16))
        values = values - parts[-1].astype(jnp.float32)
    return parts


def gathered_image(pieces, share, ids, keys, split):
    image = None
    for slot, source in enumerate(pieces):
        picked = [source[at : at + n, :] for at, n in share]
        values = picked[0] if len(picked) == 1 else jnp.concatenate(picked, axis=0)
        count = values.shape[0]
        tiles = -(-count // keys.shape[1])
        match = [keys == ids[slot * tiles + t : slot * tiles + t + 1, :] for t in range(tiles)]
        match = match[0] if tiles == 1 else jnp.concatenate(match, axis=1)
        match = jnp.where(match[:, :count], 1.0, 0.0).astype(jnp.bfloat16)
        for part in split_bf16(values, split):
            term = jnp.dot(match, part, preferred_element_type=jnp.float32)
            image = term if image is None else image + term
    return image


def to_smem(sources, targets, sems):
    copies = [pltpu.make_async_copy(a, b, sems.at[i]) for i, (a, b) in enumerate(zip(sources, targets))]
    for copy in copies:
        copy.start()
    return copies


def wait_all(copies):
    for copy in copies:
        copy.wait()


def seed(zeros):
    zeros[...] = jnp.zeros_like(zeros)


def first_terms(sizes, *refs):
    _, piece, tail_own = sizes
    indices, (zeros, blocks, duals), hub_own, tail_consts = refs[:4], refs[4:7], refs[7:10], refs[10:13]
    payload, wide, state, *scratch, sems = refs[13:]
    copies = to_smem(indices, scratch, sems)
    hub_row, hub_col, owner, slot_of = scratch
    width = duals.shape[1]
    hub_n, tail_n = blocks.shape[0], owner.shape[0]
    for which, source in enumerate(tail_consts):
        state[which * tail_own : (which + 1) * tail_own, :] = source[...]
    fill_wide(duals, wide)
    wait_all(copies)
    adjoint_terms(blocks, hub_row, wide, payload)
    mine = lax.axis_index("rows") * piece
    for which, source in enumerate(hub_own):
        for i in range(piece):
            at = hub_n + which * piece + i
            payload[at : at + 1, :] = source[pl.ds(mine + i, 1), :]
    lane = lax.broadcasted_iota(jnp.int32, (1, width), 1)

    def id_row(count, value):
        row = jnp.full((1, width), -1, jnp.int32)
        for b in range(count):
            row = jnp.where(lane == b, value(b), row)
        return row.astype(jnp.float32)

    at = hub_n + 3 * piece
    payload[at : at + 1, :] = id_row(hub_n, lambda b: hub_col[b])
    payload[at + 1 :, :] = zeros[: payload.shape[0] - at - 1, :]
    at = 3 * tail_own
    state[at : at + 1, :] = id_row(tail_n, lambda b: owner[b] * tail_own + slot_of[b])
    state[at + 1 :, :] = zeros[: state.shape[0] - at - 1, :]


def slot_order(apart, slots):
    return (apart & 1) * (slots // 2) + (apart >> 1)


def pick_rows(count, targets, keys, base, pool, where):
    def step(b, _):
        place, gap, key = where(b)
        for which, target in enumerate(targets):
            target[pl.ds(base + b, 1), :] = pool[pl.ds(place + which * gap, 1), :]
        keys[pl.ds(base + b, 1), :] = jnp.full((1, keys.shape[1]), key, jnp.int32).astype(jnp.float32)
        return 0

    lax.fori_loop(0, count, step, 0, unroll=8)


def pick_state(tail_own, *refs):
    indices, states, (x, cost, upper, keys, pool, owner, slot_of, sems) = refs[:2], refs[2:-8], refs[-8:]
    copies = to_smem(indices, (owner, slot_of), sems)
    slots, stride = len(states), 3 * tail_own
    for slot, source in enumerate(states):
        pool[slot * stride : (slot + 1) * stride, :] = source[:stride, :]
    me = lax.axis_index("rows")
    wait_all(copies)

    def where(b):
        place = slot_order(owner[b] ^ me, slots) * stride + slot_of[b]
        return place, tail_own, owner[b] * tail_own + slot_of[b]

    pick_rows(x.shape[0], (x, cost, upper), keys, 0, pool, where)


def tail_terms(own_sizes, row_in, blocks, wide, *refs):
    *own, row, sems = refs
    copies = to_smem((row_in,), (row,), sems)
    if own_sizes is None:
        (out,) = own
    else:
        out = own.pop(-3)
        own_step(own_sizes, *own)
    wait_all(copies)
    adjoint_terms(blocks, row, wide, out)


def gathered_ids(sizes, states, pieces, ids):
    tail_n, tail_own, hub_n, hub_devs, piece, each = sizes
    slots, width = len(pieces), ids.shape[1]
    tiles = ids.shape[0] // slots
    hub_base = float(slots * tail_own)
    lane = lax.broadcasted_iota(jnp.int32, (1, width), 1)
    for slot in range(slots):
        merged = [jnp.full((1, width), -1.0, jnp.float32)] * tiles
        rows = [(0, tail_n, states[slot][3 * tail_own : 3 * tail_own + 1, :])]
        for z in range(hub_devs):
            at = tail_n + z * each + hub_n + 3 * piece
            rows.append((tail_n + z * hub_n, hub_n, pieces[slot][at : at + 1, :] + hub_base))
        for start, count, row in rows:
            row = pltpu.roll(row, start % width, 1) if start % width else row
            for t in range(tiles):
                here = (lane >= start - t * width) & (lane < start + count - t * width)
                merged[t] = jnp.where(here, row, merged[t])
        for t in range(tiles):
            ids[slot * tiles + t : slot * tiles + t + 1, :] = merged[t]


def share_of(tail_n, hub_n, hub_devs, each):
    if each == hub_n:
        return [(0, tail_n + hub_devs * hub_n)]
    return [(0, tail_n)] + [(tail_n + z * each, hub_n) for z in range(hub_devs)]


def primal_update(image, x, cost, upper):
    x_new = jnp.minimum(jnp.maximum(x - primal_step * (cost - image), 0.0), upper)
    return x_new, 2.0 * x_new - x


def step_kernel(first, last, sizes, *refs):
    tail_n, tail_own, hub_n, hub_own, hub_devs, piece, each, slots = sizes
    refs = list(refs)
    take = lambda n: [refs.pop(0) for _ in range(n)]
    indices = take(3 if first else 2)
    tail_blocks, hub_blocks, duals, demand = take(4)
    pieces = take(slots)
    if first:
        states = take(slots)
        picked = take(4)
    else:
        x_in, cost, upper, keys, ids = take(5)
    if last:
        own = take(6)
    (duals_out,) = take(1)
    if last:
        own += take(2)
    else:
        hub_out, wide, x_out = take(3)
    if first:
        cost, upper, keys, ids = take(4)
        x_in = x_out
    scratch = take(len(indices))
    sems, extra = take(2)
    if first:
        (pool,) = take(1)
    sums = refs
    copies = to_smem(indices, scratch, sems)
    tail_row, hub_row = scratch[:2]
    width, part = duals.shape[1], duals.shape[1] // PARTS

    if first:
        for target, source in zip((x_in, cost, upper, keys), picked):
            target[:tail_n, :] = source[...]
        me, my_hub = lax.axis_index("rows"), lax.axis_index("hub")
        gathered_ids((tail_n, tail_own, hub_n, hub_devs, piece, each), states, pieces, ids)
        gap = each - hub_n
        for slot in range(slots):
            for z in range(hub_devs):
                to, at = (slot * hub_devs + z) * gap, tail_n + z * each + hub_n
                pool[to : to + gap, :] = pieces[slot][at : at + gap, :]
        wait_all(copies)
        hub_col = scratch[2]

        def where(b):
            col = hub_col[b]
            local = col % hub_own
            slot = slot_order((local // piece) ^ me, slots)
            place = (slot * hub_devs + ((col // hub_own) ^ my_hub)) * gap + local % piece
            return place, piece, slots * tail_own + col

        pick_rows(hub_n, (x_in, cost, upper), keys, tail_n, pool, where)

    image = gathered_image(pieces, share_of(tail_n, hub_n, hub_devs, each), ids, keys[...], 2)
    x_new, extrapolated = primal_update(image, x_in[...], cost[...], upper[...])
    extra[...] = extrapolated
    if not last:
        x_out[...] = x_new

    eye = eye_mask(width)
    base = duals[...] + dual_step * demand[...]
    for r in range(base.shape[0]):
        start = jnp.where(eye, (-1.0 / dual_step) * base[r : r + 1, :], 0.0)
        for q in range(PARTS):
            sums[q][r] = start[q * part : (q + 1) * part, :]
    if not first:
        wait_all(copies)
    forward_sums(tail_blocks, tail_row, extra, 0, sums)
    forward_sums(hub_blocks, hub_row, extra, tail_n, sums)
    for r in range(base.shape[0]):
        diagonal = jnp.zeros((1, width), jnp.float32)
        for q in range(PARTS):
            rows = slice(q * part, (q + 1) * part)
            total = jnp.sum(sums[q][r], axis=1, keepdims=True)
            value = jnp.broadcast_to(jnp.maximum(-dual_step * total, 0.0), (part, width))
            if not last:
                wide[r, rows, :] = value
            diagonal += jnp.sum(jnp.where(eye[rows, :], value, 0.0), axis=0, keepdims=True)
        duals_out[r : r + 1, :] = diagonal
    if last:
        own_step((tail_n, hub_n, hub_devs, each, slots), ids, *pieces, *own)
    else:
        adjoint_terms(hub_blocks, hub_row, wide, hub_out)


def own_step(sizes, ids, *refs):
    tail_n, hub_n, hub_devs, each, slots = sizes
    pieces, (x_tail, cost_tail, upper_tail, x_hub, cost_hub, upper_hub, tail_out, hub_out) = refs[:slots], refs[slots:]
    tail_own, width = x_tail.shape
    hub_own = x_hub.shape[0]
    tail_key = lax.broadcasted_iota(jnp.int32, (tail_own, width), 0) + lax.axis_index("rows") * tail_own
    hub_key = lax.broadcasted_iota(jnp.int32, (hub_own, width), 0) + lax.axis_index("hub") * hub_own
    keys = jnp.concatenate([tail_key, hub_key + slots * tail_own], axis=0).astype(jnp.float32)
    image = gathered_image(pieces, share_of(tail_n, hub_n, hub_devs, each), ids, keys, 2)
    tail_out[...] = primal_update(image[:tail_own], x_tail[...], cost_tail[...], upper_tail[...])[0]
    hub_out[...] = primal_update(image[tail_own:], x_hub[...], cost_hub[...], upper_hub[...])[0]


def call(kernel, ins, outs, scratch, flops):
    spec = lambda items: [pl.BlockSpec(memory_space=VMEM)] * len(items)
    return pl.pallas_call(
        kernel,
        out_shape=[jax.ShapeDtypeStruct(s, jnp.float32) for s in outs],
        in_specs=spec(ins),
        out_specs=spec(outs),
        scratch_shapes=scratch,
        compiler_params=pltpu.CompilerParams(vmem_limit_bytes=32 << 20),
        cost_estimate=pl.CostEstimate(flops=flops, bytes_accessed=0, transcendentals=0),
    )(*ins)


def on_device(
    tail_blocks,
    tail_row,
    tail_owner,
    tail_slot,
    hub_blocks,
    hub_row,
    hub_col,
    x_tail,
    cost_tail,
    upper_tail,
    x_hub,
    cost_hub,
    upper_hub,
    duals,
    demand,
):
    row_devs = lax.axis_size("rows")
    hub_devs = lax.axis_size("hub")
    tail_n, width = tail_blocks.shape[0], tail_blocks.shape[2]
    hub_n = hub_blocks.shape[0]
    tail_own = x_tail.shape[0]
    hub_own = x_hub.shape[0]
    row_n = duals.shape[0]
    chips = row_devs // 2
    piece = hub_own // row_devs
    assert row_devs & (row_devs - 1) == 0 and hub_devs & (hub_devs - 1) == 0
    assert piece * row_devs == hub_own and tail_n <= width

    def swap(value, axis, mask):
        count = lax.axis_size(axis)
        return lax.ppermute(value, axis, [(i, i ^ mask) for i in range(count)])

    def over_rows(value):
        near = [value] + [swap(value, "rows", 2 * m) for m in reversed(range(1, chips))][::-1]
        return near + [swap(part, "rows", 1) for part in near]

    def over_hub(value):
        return [value] + [swap(value, "hub", m) for m in reversed(range(1, hub_devs))][::-1]

    owners = tail_owner[:, 0]
    each = hub_n + -(-(3 * piece + 1) // 8) * 8
    state_n = 3 * tail_own + 8
    f32 = lambda *s: pltpu.VMEM(s, jnp.float32)
    ints = lambda *sizes: [pltpu.SMEM((n,), jnp.int32) for n in sizes] + [pltpu.SemaphoreType.DMA((len(sizes),))]
    work = 2 * width * width
    big = (row_n, width, width)

    (zeros,) = call(seed, (), [(8, width)], [], SEED_FLOPS)
    payload, wide, state = call(
        functools.partial(first_terms, (row_devs, piece, tail_own)),
        (hub_row, hub_col, owners, tail_slot, zeros, hub_blocks, duals)
        + (x_hub, cost_hub, upper_hub, x_tail, cost_tail, upper_tail),
        [(each, width), big, (state_n, width)],
        ints(hub_n, hub_n, tail_n, tail_n),
        hub_n * work,
    )
    states = over_rows(state)
    picked = call(
        functools.partial(pick_state, tail_own),
        (owners, tail_slot, *states),
        [(tail_n, width)] * 4,
        [f32(row_devs * 3 * tail_own, width)] + ints(tail_n, tail_n),
        tail_n * width * row_devs,
    )
    own = (x_tail, cost_tail, upper_tail, x_hub, cost_hub, upper_hub)
    own_outs = [(tail_own, width), (hub_own, width)]
    share = tail_n + hub_devs * hub_n
    held = (tail_n + hub_n, width)
    for iteration in range(ITERS):
        first, last = iteration == 0, iteration == ITERS - 1
        terms, *own_new = call(
            functools.partial(tail_terms, None if first else (tail_n, hub_n, hub_devs, step_each, row_devs)),
            (tail_row, tail_blocks, wide) + (() if first else (kept[-1], *pieces, *own)),
            [(tail_n, width)] + ([] if first else own_outs),
            ints(tail_n),
            tail_n * work,
        )
        if not first:
            own = (own_new[0], *own[1:3], own_new[1], *own[4:])
        parts = over_hub(payload)
        pieces = over_rows(jnp.concatenate([terms] + parts, axis=0))
        step_each = each if first else hub_n
        ins = (tail_row, hub_row) + (hub_col,) * first + (tail_blocks, hub_blocks, duals, demand, *pieces)
        ins += (*states, *picked) if first else kept
        ins += own if last else ()
        outs = [(row_n, width)] + (own_outs if last else [(hub_n, width), big, held])
        outs += [held, held, held, (row_devs * -(-share // width), width)] * first
        scratch = ints(tail_n, hub_n, *[hub_n] * first) + [f32(*held)]
        scratch += [f32(row_devs * hub_devs * (each - hub_n), width)] * first
        sizes = (tail_n, tail_own, hub_n, hub_own, hub_devs, piece, step_each, row_devs)
        duals, *out = call(
            functools.partial(step_kernel, first, last, sizes),
            ins,
            outs,
            scratch + [f32(row_n, width // PARTS, width)] * PARTS,
            (tail_n + hub_n) * work,
        )
        if last:
            return out[0], out[1], duals
        payload, wide, x_all, *rest = out
        kept = (x_all, *(rest if first else kept[1:]))


def solution(mesh):
    both = ("rows", "hub")
    in_specs = (
        P(both, None, None),
        P(both),
        P(both, None),
        P(both),
        P(both, None, None),
        P(both),
        P(both),
        P(both, None),
        P(both, None),
        P(both, None),
        P("hub", None),
        P("hub", None),
        P("hub", None),
        P(both, None),
        P(both, None),
    )
    out_specs = (P(both, None), P("hub", None), P(both, None))

    return jax.shard_map(on_device, mesh=mesh, in_specs=in_specs, out_specs=out_specs, check_vma=False)
```

time: 70.9 us -> 65.7 us (0.927)
  Pallas kernels: 19.4 us -> 13.7 us
  starting transfers between devices: 30.3 us -> 32 us
  waiting for transfers between devices: 18.5 us -> 17.4 us
    pallas_call x11 -> x9, Pallas kernels: 19.4 us -> 13.7 us  [call(): pl.pallas_call(kernel, out_shape=[jax.ShapeDtypeStruct(s, jnp.float32) fo...]
    ppermute x37, starting transfers between devices: 30.3 us -> 32 us  [swap(): return lax.ppermute(value, axis, [(i, i ^ mask) for i in range(count)])]
    ppermute x37, waiting for transfers between devices: 18.5 us -> 17.4 us  [swap(): return lax.ppermute(value, axis, [(i, i ^ mask) for i in range(count)])]
    unnamed x44 -> x42, local copies, waits for them, and re-layouts: 1.46 us -> 1.43 us
  transfers between devices with their start and end apart: 37 -> 37, of which waited for: 18 -> 19; matrix products, arithmetic and copies ran while one was open for 0% -> 0% of each run, Pallas kernels for 11% -> 7%
where the time goes in v1:
time: 65.7 us; the launch traced here: 65.5 us
  starting transfers between devices  32 us (49%)
  waiting for transfers between devices  17.4 us (26%)
  Pallas kernels  13.7 us (21%)
  local copies, waits for them, and re-layouts  1.43 us (2%)
  between operations  0.99 us (2%)
    ppermute x37, starting transfers between devices, swap(): return lax.ppermute(value, axis, [(i, i ^ mask) for i in range(count)])  32 us
    ppermute x37, waiting for transfers between devices, swap(): return lax.ppermute(value, axis, [(i, i ^ mask) for i in range(count)])  17.4 us
    pallas_call x9, Pallas kernels, call(): pl.pallas_call(kernel, out_shape=[jax.ShapeDtypeStruct(s, jnp.float32) fo...  13.7 us
    unnamed x42, local copies, waits for them, and re-layouts  1.43 us
  transfers between devices with their start and end apart: 37, of which 19 were waited for; matrix products, arithmetic and copies ran while one was open for 0% of the time, Pallas kernels for 7%

profile of v1, /device:TPU:0, one launch (start us, length us, event | category | flops | bytes accessed | tf_op | source)
XLA Modules:
  0.0 65.5 jit_solution(856793934117867886)
XLA Ops:
  0.8 0.0 copy-start.7
  0.8 0.6 copy-done.5
  1.4 0.0 copy-done.4
  1.4 0.1 copy-done.3
  1.4 0.0 copy-done.2
  1.4 0.7 %copy-done.1 = f32[24,128,128]{2,1,0:T(8,128)S(1)} copy-done((f32[24,128,128]{2,1,0:T(8,128)S(1)}, f32[24,128,128]{2,1,0:T(8,128)}, u32[]{:S(2)}) %copy-start.1) | copy-done | bytes 1572888
  2.2 1.2 %shard_map.167 = (f32[40,128]{1,0:T(8,128)S(1)}, f32[16,128,128]{2,1,0:T(8,128)S(1)}, f32[200,128]{1,0:T(8,128)S(1)}) custom-call(s32[24]{0:T(128)S(1)} %copy-done.11, s32[24]{0:T(128)S(1)} %copy-done.14, s32[72]{0:T(128)S(1)} %bitcast.1, s32[72]{0:T(128)S(1)} %copy-done.13, f32[8,128]{1,0:T(8,128)S(1)} %shard_map.166.refs_4_, ...), custom_call_target="tpu_custom_call" | custom-call | flops 786432 | tf_op jit(solution)/shard_map/pallas_call | solution.py:307
  3.3 5.1 %collective-permute-start.2 = (f32[40,128]{1,0:T(8,128)S(1)}, f32[40,128]{1,0:T(8,128)S(1)}, u32[]{:S(2)}, u32[]{:S(2)}) collective-permute-start(f32[40,128]{1,0:T(8,128)S(1)} %get-tuple-element.32), channel_id=1, source_target_pairs={{0,3},{1,2},{2,1},{3,0},{4,7},{5,6},{6,5},{7,4},{8,11},{9,10},{10,... | collective-permute-start | bytes 61448 | tf_op jit(solution)/shard_map/ppermute | solution.py:349
  8.5 0.0 collective-permute-start.1
  8.5 0.6 collective-permute-start
  9.1 0.0 collective-permute-start.13
  9.1 2.6 %collective-permute-start.12 = (f32[200,128]{1,0:T(8,128)S(1)}, f32[200,128]{1,0:T(8,128)S(1)}, u32[]{:S(2)}, u32[]{:S(2)}) collective-permute-start(f32[200,128]{1,0:T(8,128)S(1)} %get-tuple-element.33.refs_2_.refs_15_), channel_id=1, source_target_pairs={{0,24},{4,28},{8,16},{12,20},{16,8},{20,12},{24,0},{28,4},{1,25},{... | collective-permute-start | bytes 307208 | tf_op jit(solution)/shard_map/ppermute | solution.py:349
  11.7 1.3 %shard_map.168 = f32[72,128]{1,0:T(8,128)S(1)} custom-call(s32[72]{0:T(128)S(1)} %copy-done.10, f32[72,128,128]{2,1,0:T(8,128)S(1)} %copy-done, f32[16,128,128]{2,1,0:T(8,128)S(1)} %get-tuple-element.31.wide), custom_call_target="tpu_custom_call" | custom-call | flops 2359296 | tf_op jit(solution)/shard_map/pallas_call | solution.py:307
  13.0 0.0 collective-permute-done
  13.0 0.8 %collective-permute-start.11 = (f32[200,128]{1,0:T(8,128)S(1)}, f32[200,128]{1,0:T(8,128)S(1)}, u32[]{:S(2)}, u32[]{:S(2)}) collective-permute-start(f32[200,128]{1,0:T(8,128)S(1)} %get-tuple-element.33.refs_2_.refs_15_), channel_id=1, source_target_pairs={{0,16},{4,20},{8,24},{12,28},{16,0},{20,4},{24,8},{28,12},{1,17},{... | collective-permute-start | bytes 307208 | tf_op jit(solution)/shard_map/ppermute | solution.py:349
  13.8 1.5 %collective-permute-start.10 = (f32[200,128]{1,0:T(8,128)S(1)}, f32[200,128]{1,0:T(8,128)S(1)}, u32[]{:S(2)}, u32[]{:S(2)}) collective-permute-start(f32[200,128]{1,0:T(8,128)S(1)} %get-tuple-element.33.refs_2_.refs_15_), channel_id=1, source_target_pairs={{0,8},{4,12},{8,0},{12,4},{16,24},{20,28},{24,16},{28,20},{1,9},{5... | collective-permute-start | bytes 307208 | tf_op jit(solution)/shard_map/ppermute | solution.py:349
  15.3 1.4 %collective-permute-start.5 = (f32[232,128]{1,0:T(8,128)S(1)}, f32[232,128]{1,0:T(8,128)S(1)}, u32[]{:S(2)}, u32[]{:S(2)}) collective-permute-start(f32[232,128]{1,0:T(8,128)S(1)} %constant_dynamic-update-slice_fusion.refs_7_.refs_1_), channel_id=1, source_target_pairs={{0,24},{4,28},{8,16},{12,20},{16,8},{20,12},{24,0},{28,4},{1,25},{... | collective-permute-start | bytes 356360 | tf_op jit(solution)/shard_map/ppermute | solution.py:349
  16.7 0.0 collective-permute-done.13.refs_6_.refs_19_
  16.7 0.7 %collective-permute-start.4 = (f32[232,128]{1,0:T(8,128)S(1)}, f32[232,128]{1,0:T(8,128)S(1)}, u32[]{:S(2)}, u32[]{:S(2)}) collective-permute-start(f32[232,128]{1,0:T(8,128)S(1)} %constant_dynamic-update-slice_fusion.refs_7_.refs_1_), channel_id=1, source_target_pairs={{0,16},{4,20},{8,24},{12,28},{16,0},{20,4},{24,8},{28,12},{1,17},{... | collective-permute-start | bytes 356360 | tf_op jit(solution)/shard_map/ppermute | solution.py:349
  17.4 0.0 collective-permute-done.12.refs_5_.refs_18_
  17.4 1.5 %collective-permute-start.3 = (f32[232,128]{1,0:T(8,128)S(1)}, f32[232,128]{1,0:T(8,128)S(1)}, u32[]{:S(2)}, u32[]{:S(2)}) collective-permute-start(f32[232,128]{1,0:T(8,128)S(1)} %constant_dynamic-update-slice_fusion.refs_7_.refs_1_), channel_id=1, source_target_pairs={{0,8},{4,12},{8,0},{12,4},{16,24},{20,28},{24,16},{28,20},{1,9},{5... | collective-permute-start | bytes 356360 | tf_op jit(solution)/shard_map/ppermute | solution.py:349
  18.9 0.6 collective-permute-done.10.refs_3_.refs_16_
  19.4 0.0 collective-permute-start.15
  19.5 3.4 %collective-permute-done.5.refs_10_.refs_4_ = f32[232,128]{1,0:T(8,128)S(1)} collective-permute-done((f32[232,128]{1,0:T(8,128)S(1)}, f32[232,128]{1,0:T(8,128)S(1)}, u32[]{:S(2)}, u32[]{:S(2)}) %collective-permute-start.5) | collective-permute-done | bytes 118816 | tf_op jit(solution)/shard_map/ppermute | solution.py:349
  22.9 0.7 %collective-permute-done.4.refs_9_.refs_3_ = f32[232,128]{1,0:T(8,128)S(1)} collective-permute-done((f32[232,128]{1,0:T(8,128)S(1)}, f32[232,128]{1,0:T(8,128)S(1)}, u32[]{:S(2)}, u32[]{:S(2)}) %collective-permute-start.4) | collective-permute-done | bytes 118816 | tf_op jit(solution)/shard_map/ppermute | solution.py:349
  23.6 0.5 collective-permute-start.8
  24.1 0.1 collective-permute-start.7
  24.1 0.4 collective-permute-start.14
  24.6 1.0 %collective-permute-done.14.refs_7_.refs_20_ = f32[200,128]{1,0:T(8,128)S(1)} collective-permute-done((f32[200,128]{1,0:T(8,128)S(1)}, f32[200,128]{1,0:T(8,128)S(1)}, u32[]{:S(2)}, u32[]{:S(2)}) %collective-permute-start.14) | collective-permute-done | bytes 102432 | tf_op jit(solution)/shard_map/ppermute | solution.py:349
  25.5 0.9 %shard_map.169 = (f32[72,128]{1,0:T(8,128)S(1)}, f32[72,128]{1,0:T(8,128)S(1)}, f32[72,128]{1,0:T(8,128)S(1)}, f32[72,128]{1,0:T(8,128)S(1)}) custom-call(s32[72]{0:T(128)S(1)} %bitcast.2, s32[72]{0:T(128)S(1)} %copy-done.13, f32[200,128]{1,0:T(8,128)S(1)} %get-tuple-element.33.refs_2_.refs_15_, f32[200,128]{1,0:T(8,128)S(1)} %collective-permute-done.10.refs_3_.refs_16_, ...), custom_call_target="tpu_custom_call" | custom-call | flops 73728 | tf_op jit(solution)/shard_map/pallas_call | solution.py:307
  26.5 2.8 %shard_map.170 = (f32[16,128]{1,0:T(8,128)S(1)}, f32[24,128]{1,0:T(8,128)S(1)}, f32[16,128,128]{2,1,0:T(8,128)S(1)}, f32[96,128]{1,0:T(8,128)S(1)}, f32[96,128]{...) custom-call(s32[72]{0:T(128)S(1)} %copy-done.10, s32[24]{0:T(128)S(1)} %copy-done.11, ...), custom_call_target="tpu_custom_call" | custom-call | flops 3145728 | tf_op jit(solution)/shard_map/pallas_call | solution.py:307
  29.2 3.7 %collective-permute-start.19 = (f32[24,128]{1,0:T(8,128)S(1)}, f32[24,128]{1,0:T(8,128)S(1)}, u32[]{:S(2)}, u32[]{:S(2)}) collective-permute-start(f32[24,128]{1,0:T(8,128)S(1)} %get-tuple-element.42), channel_id=1, source_target_pairs={{0,3},{1,2},{2,1},{3,0},{4,7},{5,6},{6,5},{7,4},{8,11},{9,10},{10,... | collective-permute-start | bytes 36872 | tf_op jit(solution)/shard_map/ppermute | solution.py:349
  32.9 0.8 %collective-permute-start.17 = (f32[24,128]{1,0:T(8,128)S(1)}, f32[24,128]{1,0:T(8,128)S(1)}, u32[]{:S(2)}, u32[]{:S(2)}) collective-permute-start(f32[24,128]{1,0:T(8,128)S(1)} %get-tuple-element.42), channel_id=1, source_target_pairs={{0,1},{1,0},{2,3},{3,2},{4,5},{5,4},{6,7},{7,6},{8,9},{9,8},{10,11... | collective-permute-start | bytes 36872 | tf_op jit(solution)/shard_map/ppermute | solution.py:349
  33.7 1.3 %shard_map.171 = (f32[72,128]{1,0:T(8,128)S(1)}, f32[64,128]{1,0:T(8,128)S(1)}, f32[32,128]{1,0:T(8,128)S(1)}) custom-call(s32[72]{0:T(128)S(1)} %copy-done.10, f32[72,128,128]{2,1,0:T(8,128)S(1)} %copy-done, f32[16,128,128]{2,1,0:T(8,128)S(1)} %get-tuple-element.39.wide, f32[16,128]{1,0:T(8,128)S(1)} %get-tuple-element.40.refs_0_.refs_18_, ...), custom_call_target="tpu_custom_call" | custom-call | flops 2359296 | tf_op jit(solution)/shard_map/pallas_call | solution.py:307
  35.0 1.7 %collective-permute-done.17 = f32[24,128]{1,0:T(8,128)S(1)} collective-permute-done((f32[24,128]{1,0:T(8,128)S(1)}, f32[24,128]{1,0:T(8,128)S(1)}, u32[]{:S(2)}, u32[]{:S(2)}) %collective-permute-start.17) | collective-permute-done | bytes 12320 | tf_op jit(solution)/shard_map/ppermute | solution.py:349
  36.7 0.8 %collective-permute-done.18 = f32[24,128]{1,0:T(8,128)S(1)} collective-permute-done((f32[24,128]{1,0:T(8,128)S(1)}, f32[24,128]{1,0:T(8,128)S(1)}, u32[]{:S(2)}, u32[]{:S(2)}) %collective-permute-start.18) | collective-permute-done | bytes 12320 | tf_op jit(solution)/shard_map/ppermute | solution.py:349
  37.5 1.7 %collective-permute-start.22 = (f32[168,128]{1,0:T(8,128)S(1)}, f32[168,128]{1,0:T(8,128)S(1)}, u32[]{:S(2)}, u32[]{:S(2)}) collective-permute-start(f32[168,128]{1,0:T(8,128)S(1)} %constant_dynamic-update-slice_fusion.5.refs_6_.refs_1_), channel_id=1, source_target_pairs={{0,24},{4,28},{8,16},{12,20},{16,8},{20,12},{24,0},{28,4},{1,25},{... | collective-permute-start | bytes 258056 | tf_op jit(solution)/shard_map/ppermute | solution.py:349
  39.2 0.5 collective-permute-start.21
  39.7 1.3 %collective-permute-start.20 = (f32[168,128]{1,0:T(8,128)S(1)}, f32[168,128]{1,0:T(8,128)S(1)}, u32[]{:S(2)}, u32[]{:S(2)}) collective-permute-start(f32[168,128]{1,0:T(8,128)S(1)} %constant_dynamic-update-slice_fusion.5.refs_6_.refs_1_), channel_id=1, source_target_pairs={{0,8},{4,12},{8,0},{12,4},{16,24},{20,28},{24,16},{28,20},{1,9},{5... | collective-permute-start | bytes 258056 | tf_op jit(solution)/shard_map/ppermute | solution.py:349
  41.1 2.5 %collective-permute-done.22.refs_9_.refs_4_ = f32[168,128]{1,0:T(8,128)S(1)} collective-permute-done((f32[168,128]{1,0:T(8,128)S(1)}, f32[168,128]{1,0:T(8,128)S(1)}, u32[]{:S(2)}, u32[]{:S(2)}) %collective-permute-start.22) | collective-permute-done | bytes 86048 | tf_op jit(solution)/shard_map/ppermute | solution.py:349
  43.6 0.7 %collective-permute-done.21.refs_8_.refs_3_ = f32[168,128]{1,0:T(8,128)S(1)} collective-permute-done((f32[168,128]{1,0:T(8,128)S(1)}, f32[168,128]{1,0:T(8,128)S(1)}, u32[]{:S(2)}, u32[]{:S(2)}) %collective-permute-start.21) | collective-permute-done | bytes 86048 | tf_op jit(solution)/shard_map/ppermute | solution.py:349
  44.3 0.5 collective-permute-start.24
  44.8 0.1 collective-permute-done.26.refs_13_.refs_8_
  44.9 0.7 %collective-permute-done.25.refs_12_.refs_7_ = f32[168,128]{1,0:T(8,128)S(1)} collective-permute-done((f32[168,128]{1,0:T(8,128)S(1)}, f32[168,128]{1,0:T(8,128)S(1)}, u32[]{:S(2)}, u32[]{:S(2)}) %collective-permute-start.25) | collective-permute-done | bytes 86048 | tf_op jit(solution)/shard_map/ppermute | solution.py:349
  45.5 0.2 collective-permute-done.24.refs_11_.refs_6_
  45.7 2.1 %shard_map.172 = (f32[16,128]{1,0:T(8,128)S(1)}, f32[24,128]{1,0:T(8,128)S(1)}, f32[16,128,128]{2,1,0:T(8,128)S(1)}, f32[96,128]{1,0:T(8,128)S(1)}) custom-call(s32[72]{0:T(128)S(1)} %copy-done.10, s32[24]{0:T(128)S(1)} %copy-done.11, f32[72,128,128]{2,1,0:T(8,128)S(1)} %copy-done, f32[24,128,128]{2,1,0:T(8,128)S(1)} %copy-done.1, ...), custom_call_target="tpu_custom_call" | custom-call | flops 3145728 | tf_op jit(solution)/shard_map/pallas_call | solution.py:307
  47.8 1.6 %collective-permute-start.29 = (f32[24,128]{1,0:T(8,128)S(1)}, f32[24,128]{1,0:T(8,128)S(1)}, u32[]{:S(2)}, u32[]{:S(2)}) collective-permute-start(f32[24,128]{1,0:T(8,128)S(1)} %get-tuple-element.52), channel_id=1, source_target_pairs={{0,3},{1,2},{2,1},{3,0},{4,7},{5,6},{6,5},{7,4},{8,11},{9,10},{10,... | collective-permute-start | bytes 36872 | tf_op jit(solution)/shard_map/ppermute | solution.py:349
  49.4 0.5 collective-permute-start.28
  49.9 2.4 %collective-permute-start.27 = (f32[24,128]{1,0:T(8,128)S(1)}, f32[24,128]{1,0:T(8,128)S(1)}, u32[]{:S(2)}, u32[]{:S(2)}) collective-permute-start(f32[24,128]{1,0:T(8,128)S(1)} %get-tuple-element.52), channel_id=1, source_target_pairs={{0,1},{1,0},{2,3},{3,2},{4,5},{5,4},{6,7},{7,6},{8,9},{9,8},{10,11... | collective-permute-start | bytes 36872 | tf_op jit(solution)/shard_map/ppermute | solution.py:349
  52.3 1.3 %shard_map.173 = (f32[72,128]{1,0:T(8,128)S(1)}, f32[64,128]{1,0:T(8,128)S(1)}, f32[32,128]{1,0:T(8,128)S(1)}) custom-call(s32[72]{0:T(128)S(1)} %copy-done.10, f32[72,128,128]{2,1,0:T(8,128)S(1)} %copy-done, f32[16,128,128]{2,1,0:T(8,128)S(1)} %get-tuple-element.48.wide, f32[16,128]{1,0:T(8,128)S(1)} %get-tuple-element.40.refs_0_.refs_18_, ...), custom_call_target="tpu_custom_call" | custom-call | flops 2359296 | tf_op jit(solution)/shard_map/pallas_call | solution.py:307
  53.6 0.3 collective-permute-done.27
  54.0 0.1 collective-permute-done.28
  54.1 1.9 %collective-permute-start.32 = (f32[168,128]{1,0:T(8,128)S(1)}, f32[168,128]{1,0:T(8,128)S(1)}, u32[]{:S(2)}, u32[]{:S(2)}) collective-permute-start(f32[168,128]{1,0:T(8,128)S(1)} %constant_dynamic-update-slice_fusion.10.refs_6_), channel_id=1, source_target_pairs={{0,24},{4,28},{8,16},{12,20},{16,8},{20,12},{24,0},{28,4},{1,25},{... | collective-permute-start | bytes 258056 | tf_op jit(solution)/shard_map/ppermute | solution.py:349
  56.0 0.8 %collective-permute-start.31 = (f32[168,128]{1,0:T(8,128)S(1)}, f32[168,128]{1,0:T(8,128)S(1)}, u32[]{:S(2)}, u32[]{:S(2)}) collective-permute-start(f32[168,128]{1,0:T(8,128)S(1)} %constant_dynamic-update-slice_fusion.10.refs_6_), channel_id=1, source_target_pairs={{0,16},{4,20},{8,24},{12,28},{16,0},{20,4},{24,8},{28,12},{1,17},{... | collective-permute-start | bytes 258056 | tf_op jit(solution)/shard_map/ppermute | solution.py:349
  56.8 0.9 %collective-permute-start.30 = (f32[168,128]{1,0:T(8,128)S(1)}, f32[168,128]{1,0:T(8,128)S(1)}, u32[]{:S(2)}, u32[]{:S(2)}) collective-permute-start(f32[168,128]{1,0:T(8,128)S(1)} %constant_dynamic-update-slice_fusion.10.refs_6_), channel_id=1, source_target_pairs={{0,8},{4,12},{8,0},{12,4},{16,24},{20,28},{24,16},{28,20},{1,9},{5... | collective-permute-start | bytes 258056 | tf_op jit(solution)/shard_map/ppermute | solution.py:349
  57.6 2.8 %collective-permute-done.32.refs_9_ = f32[168,128]{1,0:T(8,128)S(1)} collective-permute-done((f32[168,128]{1,0:T(8,128)S(1)}, f32[168,128]{1,0:T(8,128)S(1)}, u32[]{:S(2)}, u32[]{:S(2)}) %collective-permute-start.32) | collective-permute-done | bytes 86048 | tf_op jit(solution)/shard_map/ppermute | solution.py:349
  60.5 0.5 collective-permute-done.31.refs_8_
  60.9 0.0 collective-permute-start.35
  61.0 0.3 collective-permute-done.30.refs_7_
  61.3 0.2 collective-permute-start.34
  61.4 0.3 collective-permute-done.36.refs_13_
  61.7 0.5 collective-permute-done.35.refs_12_
  62.2 0.3 collective-permute-done.34.refs_11_
  62.6 2.9 %shard_map.174 = (f32[16,128]{1,0:T(8,128)}, f32[64,128]{1,0:T(8,128)}, f32[32,128]{1,0:T(8,128)}) custom-call(s32[72]{0:T(128)S(1)} %copy-done.10, s32[24]{0:T(128)S(1)} %copy-done.11, f32[72,128,128]{2,1,0:T(8,128)S(1)} %copy-done, f32[24,128,128]{2,1,0:T(8,128)S(1)} %copy-done.1, f32[16,128]{1,0:T(8,128)S(1)} %get-tuple-element.47.refs_4_, ...), custom_call_target="tpu_custom_call" | custom-call | flops 3145728 | tf_op jit(solution)/shard_map/pallas_call | solution.py:307
  (64 shorter events, 0.2 us)
Async XLA Ops:
  0.6 0.7 %copy-start.5 = (f32[32,128]{1,0:T(8,128)S(1)}, f32[32,128]{1,0:T(8,128)}, u32[]{:S(2)}) copy-start(f32[32,128]{1,0:T(8,128)} %refs_24_.1) | copy-start | bytes 49156
  0.6 0.7 %copy-start.4 = (f32[32,128]{1,0:T(8,128)S(1)}, f32[32,128]{1,0:T(8,128)}, u32[]{:S(2)}) copy-start(f32[32,128]{1,0:T(8,128)} %refs_23_.1) | copy-start | bytes 49156
  0.7 0.8 %copy-start.3 = (f32[64,128]{1,0:T(8,128)S(1)}, f32[64,128]{1,0:T(8,128)}, u32[]{:S(2)}) copy-start(f32[64,128]{1,0:T(8,128)} %refs_21_.1) | copy-start | bytes 98308
  0.7 0.8 %copy-start.2 = (f32[64,128]{1,0:T(8,128)S(1)}, f32[64,128]{1,0:T(8,128)}, u32[]{:S(2)}) copy-start(f32[64,128]{1,0:T(8,128)} %refs_20_.1) | copy-start | bytes 98308
  0.7 0.8 %copy-start.11 = (s32[24]{0:T(128)S(1)}, s32[24]{0:T(128)}, u32[]{:S(2)}) copy-start(s32[24]{0:T(128)} %refs_1_.9) | copy-start | bytes 292
  0.7 1.4 %copy-start.1 = (f32[24,128,128]{2,1,0:T(8,128)S(1)}, f32[24,128,128]{2,1,0:T(8,128)}, u32[]{:S(2)}) copy-start(f32[24,128,128]{2,1,0:T(8,128)} %refs_3_.7) | copy-start | bytes 4718596
  0.7 1.4 %copy-start.9 = (f32[16,128]{1,0:T(8,128)S(1)}, f32[16,128]{1,0:T(8,128)}, u32[]{:S(2)}) copy-start(f32[16,128]{1,0:T(8,128)} %refs_5_.5) | copy-start | bytes 24580
  0.7 1.4 %copy-start.8 = (f32[32,128]{1,0:T(8,128)S(1)}, f32[32,128]{1,0:T(8,128)}, u32[]{:S(2)}) copy-start(f32[32,128]{1,0:T(8,128)} %refs_12_.3) | copy-start | bytes 49156
  0.7 1.4 %copy-start.6 = (f32[64,128]{1,0:T(8,128)S(1)}, f32[64,128]{1,0:T(8,128)}, u32[]{:S(2)}) copy-start(f32[64,128]{1,0:T(8,128)} %refs_9_.3) | copy-start | bytes 98308
  0.7 1.4 %copy-start.14 = (s32[24]{0:T(128)S(1)}, s32[24]{0:T(128)}, u32[]{:S(2)}) copy-start(s32[24]{0:T(128)} %refs_2_.3) | copy-start | bytes 292
  0.7 1.4 %copy-start.13 = (s32[72]{0:T(128)S(1)}, s32[72]{0:T(128)}, u32[]{:S(2)}) copy-start(s32[72]{0:T(128)} %refs_1_.6) | copy-start | bytes 868
  0.7 1.4 %copy-start.12 = (s32[72,1]{0,1:T(1,128)S(1)}, s32[72,1]{0,1:T(1,128)}, u32[]{:S(2)}) copy-start(s32[72,1]{0,1:T(1,128)} %param.17) | copy-start | bytes 868
  0.8 11.0 %copy-start.10 = (s32[72]{0:T(128)S(1)}, s32[72]{0:T(128)}, u32[]{:S(2)}) copy-start(s32[72]{0:T(128)} %refs_0_.7) | copy-start | bytes 868
  0.8 10.9 %copy-start = (f32[72,128,128]{2,1,0:T(8,128)S(1)}, f32[72,128,128]{2,1,0:T(8,128)}, u32[]{:S(2)}) copy-start(f32[72,128,128]{2,1,0:T(8,128)} %refs_2_.5) | copy-start | bytes 14155780
  0.8 25.7 %copy-start.7 = (f32[16,128]{1,0:T(8,128)S(1)}, f32[16,128]{1,0:T(8,128)}, u32[]{:S(2)}) copy-start(f32[16,128]{1,0:T(8,128)} %refs_5_.7) | copy-start | bytes 24580
  3.3 12.0 %collective-permute-start.2 = (f32[40,128]{1,0:T(8,128)S(1)}, f32[40,128]{1,0:T(8,128)S(1)}, u32[]{:S(2)}, u32[]{:S(2)}) collective-permute-start(f32[40,128]{1,0:T(8,128)S(1)} %get-tuple-element.32), channel_id=1, source_target_pairs={{0,3},{1,2},{2,1},{3,0},{4,7},{5,6},{6,5},{7,4},{8,11},{9,10},{10,... | collective-permute-start | bytes 61448 | tf_op jit(solution)/shard_map/ppermute | solution.py:349
  8.5 5.3 %collective-permute-start.1 = (f32[40,128]{1,0:T(8,128)S(1)}, f32[40,128]{1,0:T(8,128)S(1)}, u32[]{:S(2)}, u32[]{:S(2)}) collective-permute-start(f32[40,128]{1,0:T(8,128)S(1)} %get-tuple-element.32), channel_id=1, source_target_pairs={{0,2},{1,3},{2,0},{3,1},{4,6},{5,7},{6,4},{7,5},{8,10},{9,11},{10,... | collective-permute-start | bytes 61448 | tf_op jit(solution)/shard_map/ppermute | solution.py:349
  8.5 4.5 %collective-permute-start = (f32[40,128]{1,0:T(8,128)S(1)}, f32[40,128]{1,0:T(8,128)S(1)}, u32[]{:S(2)}, u32[]{:S(2)}) collective-permute-start(f32[40,128]{1,0:T(8,128)S(1)} %get-tuple-element.32), channel_id=1, source_target_pairs={{0,1},{1,0},{2,3},{3,2},{4,5},{5,4},{6,7},{7,6},{8,9},{9,8},{10,11... | collective-permute-start | bytes 61448 | tf_op jit(solution)/shard_map/ppermute | solution.py:349
  9.1 7.6 %collective-permute-start.13 = (f32[200,128]{1,0:T(8,128)S(1)}, f32[200,128]{1,0:T(8,128)S(1)}, u32[]{:S(2)}, u32[]{:S(2)}) collective-permute-start(f32[200,128]{1,0:T(8,128)S(1)} %get-tuple-element.33.refs_2_.refs_15_), channel_id=1, source_target_pairs={{0,4},{4,0},{8,12},{12,8},{16,20},{20,16},{24,28},{28,24},{1,5},{5... | collective-permute-start | bytes 307208 | tf_op jit(solution)/shard_map/ppermute | solution.py:349
  9.1 8.2 %collective-permute-start.12 = (f32[200,128]{1,0:T(8,128)S(1)}, f32[200,128]{1,0:T(8,128)S(1)}, u32[]{:S(2)}, u32[]{:S(2)}) collective-permute-start(f32[200,128]{1,0:T(8,128)S(1)} %get-tuple-element.33.refs_2_.refs_15_), channel_id=1, source_target_pairs={{0,24},{4,28},{8,16},{12,20},{16,8},{20,12},{24,0},{28,4},{1,25},{... | collective-permute-start | bytes 307208 | tf_op jit(solution)/shard_map/ppermute | solution.py:349
  13.0 5.8 %collective-permute-start.11 = (f32[200,128]{1,0:T(8,128)S(1)}, f32[200,128]{1,0:T(8,128)S(1)}, u32[]{:S(2)}, u32[]{:S(2)}) collective-permute-start(f32[200,128]{1,0:T(8,128)S(1)} %get-tuple-element.33.refs_2_.refs_15_), channel_id=1, source_target_pairs={{0,16},{4,20},{8,24},{12,28},{16,0},{20,4},{24,8},{28,12},{1,17},{... | collective-permute-start | bytes 307208 | tf_op jit(solution)/shard_map/ppermute | solution.py:349
  13.8 5.7 %collective-permute-start.10 = (f32[200,128]{1,0:T(8,128)S(1)}, f32[200,128]{1,0:T(8,128)S(1)}, u32[]{:S(2)}, u32[]{:S(2)}) collective-permute-start(f32[200,128]{1,0:T(8,128)S(1)} %get-tuple-element.33.refs_2_.refs_15_), channel_id=1, source_target_pairs={{0,8},{4,12},{8,0},{12,4},{16,24},{20,28},{24,16},{28,20},{1,9},{5... | collective-permute-start | bytes 307208 | tf_op jit(solution)/shard_map/ppermute | solution.py:349
  15.3 7.6 %collective-permute-start.5 = (f32[232,128]{1,0:T(8,128)S(1)}, f32[232,128]{1,0:T(8,128)S(1)}, u32[]{:S(2)}, u32[]{:S(2)}) collective-permute-start(f32[232,128]{1,0:T(8,128)S(1)} %constant_dynamic-update-slice_fusion.refs_7_.refs_1_), channel_id=1, source_target_pairs={{0,24},{4,28},{8,16},{12,20},{16,8},{20,12},{24,0},{28,4},{1,25},{... | collective-permute-start | bytes 356360 | tf_op jit(solution)/shard_map/ppermute | solution.py:349
  16.7 6.9 %collective-permute-start.4 = (f32[232,128]{1,0:T(8,128)S(1)}, f32[232,128]{1,0:T(8,128)S(1)}, u32[]{:S(2)}, u32[]{:S(2)}) collective-permute-start(f32[232,128]{1,0:T(8,128)S(1)} %constant_dynamic-update-slice_fusion.refs_7_.refs_1_), channel_id=1, source_target_pairs={{0,16},{4,20},{8,24},{12,28},{16,0},{20,4},{24,8},{28,12},{1,17},{... | collective-permute-start | bytes 356360 | tf_op jit(solution)/shard_map/ppermute | solution.py:349
  17.4 6.2 %collective-permute-start.3 = (f32[232,128]{1,0:T(8,128)S(1)}, f32[232,128]{1,0:T(8,128)S(1)}, u32[]{:S(2)}, u32[]{:S(2)}) collective-permute-start(f32[232,128]{1,0:T(8,128)S(1)} %constant_dynamic-update-slice_fusion.refs_7_.refs_1_), channel_id=1, source_target_pairs={{0,8},{4,12},{8,0},{12,4},{16,24},{20,28},{24,16},{28,20},{1,9},{5... | collective-permute-start | bytes 356360 | tf_op jit(solution)/shard_map/ppermute | solution.py:349
  18.9 5.2 %collective-permute-start.16 = (f32[200,128]{1,0:T(8,128)S(1)}, f32[200,128]{1,0:T(8,128)S(1)}, u32[]{:S(2)}, u32[]{:S(2)}) collective-permute-start(f32[200,128]{1,0:T(8,128)S(1)} %collective-permute-done.12.refs_5_.refs_18_), channel_id=1, source_target_pairs={{0,4},{4,0},{8,12},{12,8},{16,20},{20,16},{24,28},{28,24},{1,5},{5... | collective-permute-start | bytes 307208 | tf_op jit(solution)/shard_map/ppermute | solution.py:349
  19.4 4.7 %collective-permute-start.15 = (f32[200,128]{1,0:T(8,128)S(1)}, f32[200,128]{1,0:T(8,128)S(1)}, u32[]{:S(2)}, u32[]{:S(2)}) collective-permute-start(f32[200,128]{1,0:T(8,128)S(1)} %collective-permute-done.11.refs_4_.refs_17_), channel_id=1, source_target_pairs={{0,4},{4,0},{8,12},{12,8},{16,20},{20,16},{24,28},{28,24},{1,5},{5... | collective-permute-start | bytes 307208 | tf_op jit(solution)/shard_map/ppermute | solution.py:349
  22.9 3.6 %collective-permute-start.6 = (f32[232,128]{1,0:T(8,128)S(1)}, f32[232,128]{1,0:T(8,128)S(1)}, u32[]{:S(2)}, u32[]{:S(2)}) collective-permute-start(f32[232,128]{1,0:T(8,128)S(1)} %constant_dynamic-update-slice_fusion.refs_7_.refs_1_), channel_id=1, source_target_pairs={{0,4},{4,0},{8,12},{12,8},{16,20},{20,16},{24,28},{28,24},{1,5},{5... | collective-permute-start | bytes 356360 | tf_op jit(solution)/shard_map/ppermute | solution.py:349
  23.6 2.9 %collective-permute-start.9 = (f32[232,128]{1,0:T(8,128)S(1)}, f32[232,128]{1,0:T(8,128)S(1)}, u32[]{:S(2)}, u32[]{:S(2)}) collective-permute-start(f32[232,128]{1,0:T(8,128)S(1)} %collective-permute-done.5.refs_10_.refs_4_), channel_id=1, source_target_pairs={{0,4},{4,0},{8,12},{12,8},{16,20},{20,16},{24,28},{28,24},{1,5},{5... | collective-permute-start | bytes 356360 | tf_op jit(solution)/shard_map/ppermute | solution.py:349
  23.6 2.9 %collective-permute-start.8 = (f32[232,128]{1,0:T(8,128)S(1)}, f32[232,128]{1,0:T(8,128)S(1)}, u32[]{:S(2)}, u32[]{:S(2)}) collective-permute-start(f32[232,128]{1,0:T(8,128)S(1)} %collective-permute-done.4.refs_9_.refs_3_), channel_id=1, source_target_pairs={{0,4},{4,0},{8,12},{12,8},{16,20},{20,16},{24,28},{28,24},{1,5},{5... | collective-permute-start | bytes 356360 | tf_op jit(solution)/shard_map/ppermute | solution.py:349
  24.1 2.4 %collective-permute-start.7 = (f32[232,128]{1,0:T(8,128)S(1)}, f32[232,128]{1,0:T(8,128)S(1)}, u32[]{:S(2)}, u32[]{:S(2)}) collective-permute-start(f32[232,128]{1,0:T(8,128)S(1)} %collective-permute-done.3.refs_8_.refs_2_), channel_id=1, source_target_pairs={{0,4},{4,0},{8,12},{12,8},{16,20},{20,16},{24,28},{28,24},{1,5},{5... | collective-permute-start | bytes 356360 | tf_op jit(solution)/shard_map/ppermute | solution.py:349
  24.1 1.4 %collective-permute-start.14 = (f32[200,128]{1,0:T(8,128)S(1)}, f32[200,128]{1,0:T(8,128)S(1)}, u32[]{:S(2)}, u32[]{:S(2)}) collective-permute-start(f32[200,128]{1,0:T(8,128)S(1)} %collective-permute-done.10.refs_3_.refs_16_), channel_id=1, source_target_pairs={{0,4},{4,0},{8,12},{12,8},{16,20},{20,16},{24,28},{28,24},{1,5},{5... | collective-permute-start | bytes 307208 | tf_op jit(solution)/shard_map/ppermute | solution.py:349
  29.2 8.3 %collective-permute-start.19 = (f32[24,128]{1,0:T(8,128)S(1)}, f32[24,128]{1,0:T(8,128)S(1)}, u32[]{:S(2)}, u32[]{:S(2)}) collective-permute-start(f32[24,128]{1,0:T(8,128)S(1)} %get-tuple-element.42), channel_id=1, source_target_pairs={{0,3},{1,2},{2,1},{3,0},{4,7},{5,6},{6,5},{7,4},{8,11},{9,10},{10,... | collective-permute-start | bytes 36872 | tf_op jit(solution)/shard_map/ppermute | solution.py:349
  32.9 4.6 %collective-permute-start.18 = (f32[24,128]{1,0:T(8,128)S(1)}, f32[24,128]{1,0:T(8,128)S(1)}, u32[]{:S(2)}, u32[]{:S(2)}) collective-permute-start(f32[24,128]{1,0:T(8,128)S(1)} %get-tuple-element.42), channel_id=1, source_target_pairs={{0,2},{1,3},{2,0},{3,1},{4,6},{5,7},{6,4},{7,5},{8,10},{9,11},{10,... | collective-permute-start | bytes 36872 | tf_op jit(solution)/shard_map/ppermute | solution.py:349
  32.9 3.8 %collective-permute-start.17 = (f32[24,128]{1,0:T(8,128)S(1)}, f32[24,128]{1,0:T(8,128)S(1)}, u32[]{:S(2)}, u32[]{:S(2)}) collective-permute-start(f32[24,128]{1,0:T(8,128)S(1)} %get-tuple-element.42), channel_id=1, source_target_pairs={{0,1},{1,0},{2,3},{3,2},{4,5},{5,4},{6,7},{7,6},{8,9},{9,8},{10,11... | collective-permute-start | bytes 36872 | tf_op jit(solution)/shard_map/ppermute | solution.py:349
  37.5 6.1 %collective-permute-start.22 = (f32[168,128]{1,0:T(8,128)S(1)}, f32[168,128]{1,0:T(8,128)S(1)}, u32[]{:S(2)}, u32[]{:S(2)}) collective-permute-start(f32[168,128]{1,0:T(8,128)S(1)} %constant_dynamic-update-slice_fusion.5.refs_6_.refs_1_), channel_id=1, source_target_pairs={{0,24},{4,28},{8,16},{12,20},{16,8},{20,12},{24,0},{28,4},{1,25},{... | collective-permute-start | bytes 258056 | tf_op jit(solution)/shard_map/ppermute | solution.py:349
  39.2 5.0 %collective-permute-start.21 = (f32[168,128]{1,0:T(8,128)S(1)}, f32[168,128]{1,0:T(8,128)S(1)}, u32[]{:S(2)}, u32[]{:S(2)}) collective-permute-start(f32[168,128]{1,0:T(8,128)S(1)} %constant_dynamic-update-slice_fusion.5.refs_6_.refs_1_), channel_id=1, source_target_pairs={{0,16},{4,20},{8,24},{12,28},{16,0},{20,4},{24,8},{28,12},{1,17},{... | collective-permute-start | bytes 258056 | tf_op jit(solution)/shard_map/ppermute | solution.py:349
  39.7 4.5 %collective-permute-start.20 = (f32[168,128]{1,0:T(8,128)S(1)}, f32[168,128]{1,0:T(8,128)S(1)}, u32[]{:S(2)}, u32[]{:S(2)}) collective-permute-start(f32[168,128]{1,0:T(8,128)S(1)} %constant_dynamic-update-slice_fusion.5.refs_6_.refs_1_), channel_id=1, source_target_pairs={{0,8},{4,12},{8,0},{12,4},{16,24},{20,28},{24,16},{28,20},{1,9},{5... | collective-permute-start | bytes 258056 | tf_op jit(solution)/shard_map/ppermute | solution.py:349
  41.1 3.7 %collective-permute-start.23 = (f32[168,128]{1,0:T(8,128)S(1)}, f32[168,128]{1,0:T(8,128)S(1)}, u32[]{:S(2)}, u32[]{:S(2)}) collective-permute-start(f32[168,128]{1,0:T(8,128)S(1)} %constant_dynamic-update-slice_fusion.5.refs_6_.refs_1_), channel_id=1, source_target_pairs={{0,4},{4,0},{8,12},{12,8},{16,20},{20,16},{24,28},{28,24},{1,5},{5... | collective-permute-start | bytes 258056 | tf_op jit(solution)/shard_map/ppermute | solution.py:349
  43.6 1.3 %collective-permute-start.26 = (f32[168,128]{1,0:T(8,128)S(1)}, f32[168,128]{1,0:T(8,128)S(1)}, u32[]{:S(2)}, u32[]{:S(2)}) collective-permute-start(f32[168,128]{1,0:T(8,128)S(1)} %collective-permute-done.22.refs_9_.refs_4_), channel_id=1, source_target_pairs={{0,4},{4,0},{8,12},{12,8},{16,20},{20,16},{24,28},{28,24},{1,5},{5... | collective-permute-start | bytes 258056 | tf_op jit(solution)/shard_map/ppermute | solution.py:349
  44.2 1.3 %collective-permute-start.25 = (f32[168,128]{1,0:T(8,128)S(1)}, f32[168,128]{1,0:T(8,128)S(1)}, u32[]{:S(2)}, u32[]{:S(2)}) collective-permute-start(f32[168,128]{1,0:T(8,128)S(1)} %collective-permute-done.21.refs_8_.refs_3_), channel_id=1, source_target_pairs={{0,4},{4,0},{8,12},{12,8},{16,20},{20,16},{24,28},{28,24},{1,5},{5... | collective-permute-start | bytes 258056 | tf_op jit(solution)/shard_map/ppermute | solution.py:349
  44.3 1.4 %collective-permute-start.24 = (f32[168,128]{1,0:T(8,128)S(1)}, f32[168,128]{1,0:T(8,128)S(1)}, u32[]{:S(2)}, u32[]{:S(2)}) collective-permute-start(f32[168,128]{1,0:T(8,128)S(1)} %collective-permute-done.20.refs_7_.refs_2_), channel_id=1, source_target_pairs={{0,4},{4,0},{8,12},{12,8},{16,20},{20,16},{24,28},{28,24},{1,5},{5... | collective-permute-start | bytes 258056 | tf_op jit(solution)/shard_map/ppermute | solution.py:349
  47.8 6.3 %collective-permute-start.29 = (f32[24,128]{1,0:T(8,128)S(1)}, f32[24,128]{1,0:T(8,128)S(1)}, u32[]{:S(2)}, u32[]{:S(2)}) collective-permute-start(f32[24,128]{1,0:T(8,128)S(1)} %get-tuple-element.52), channel_id=1, source_target_pairs={{0,3},{1,2},{2,1},{3,0},{4,7},{5,6},{6,5},{7,4},{8,11},{9,10},{10,... | collective-permute-start | bytes 36872 | tf_op jit(solution)/shard_map/ppermute | solution.py:349
  49.4 4.7 %collective-permute-start.28 = (f32[24,128]{1,0:T(8,128)S(1)}, f32[24,128]{1,0:T(8,128)S(1)}, u32[]{:S(2)}, u32[]{:S(2)}) collective-permute-start(f32[24,128]{1,0:T(8,128)S(1)} %get-tuple-element.52), channel_id=1, source_target_pairs={{0,2},{1,3},{2,0},{3,1},{4,6},{5,7},{6,4},{7,5},{8,10},{9,11},{10,... | collective-permute-start | bytes 36872 | tf_op jit(solution)/shard_map/ppermute | solution.py:349
  49.9 4.1 %collective-permute-start.27 = (f32[24,128]{1,0:T(8,128)S(1)}, f32[24,128]{1,0:T(8,128)S(1)}, u32[]{:S(2)}, u32[]{:S(2)}) collective-permute-start(f32[24,128]{1,0:T(8,128)S(1)} %get-tuple-element.52), channel_id=1, source_target_pairs={{0,1},{1,0},{2,3},{3,2},{4,5},{5,4},{6,7},{7,6},{8,9},{9,8},{10,11... | collective-permute-start | bytes 36872 | tf_op jit(solution)/shard_map/ppermute | solution.py:349
  54.1 6.4 %collective-permute-start.32 = (f32[168,128]{1,0:T(8,128)S(1)}, f32[168,128]{1,0:T(8,128)S(1)}, u32[]{:S(2)}, u32[]{:S(2)}) collective-permute-start(f32[168,128]{1,0:T(8,128)S(1)} %constant_dynamic-update-slice_fusion.10.refs_6_), channel_id=1, source_target_pairs={{0,24},{4,28},{8,16},{12,20},{16,8},{20,12},{24,0},{28,4},{1,25},{... | collective-permute-start | bytes 258056 | tf_op jit(solution)/shard_map/ppermute | solution.py:349
  56.0 4.9 %collective-permute-start.31 = (f32[168,128]{1,0:T(8,128)S(1)}, f32[168,128]{1,0:T(8,128)S(1)}, u32[]{:S(2)}, u32[]{:S(2)}) collective-permute-start(f32[168,128]{1,0:T(8,128)S(1)} %constant_dynamic-update-slice_fusion.10.refs_6_), channel_id=1, source_target_pairs={{0,16},{4,20},{8,24},{12,28},{16,0},{20,4},{24,8},{28,12},{1,17},{... | collective-permute-start | bytes 258056 | tf_op jit(solution)/shard_map/ppermute | solution.py:349
  56.8 4.5 %collective-permute-start.30 = (f32[168,128]{1,0:T(8,128)S(1)}, f32[168,128]{1,0:T(8,128)S(1)}, u32[]{:S(2)}, u32[]{:S(2)}) collective-permute-start(f32[168,128]{1,0:T(8,128)S(1)} %constant_dynamic-update-slice_fusion.10.refs_6_), channel_id=1, source_target_pairs={{0,8},{4,12},{8,0},{12,4},{16,24},{20,28},{24,16},{28,20},{1,9},{5... | collective-permute-start | bytes 258056 | tf_op jit(solution)/shard_map/ppermute | solution.py:349
  57.6 3.8 %collective-permute-start.33 = (f32[168,128]{1,0:T(8,128)S(1)}, f32[168,128]{1,0:T(8,128)S(1)}, u32[]{:S(2)}, u32[]{:S(2)}) collective-permute-start(f32[168,128]{1,0:T(8,128)S(1)} %constant_dynamic-update-slice_fusion.10.refs_6_), channel_id=1, source_target_pairs={{0,4},{4,0},{8,12},{12,8},{16,20},{20,16},{24,28},{28,24},{1,5},{5... | collective-permute-start | bytes 258056 | tf_op jit(solution)/shard_map/ppermute | solution.py:349
  60.5 1.3 %collective-permute-start.36 = (f32[168,128]{1,0:T(8,128)S(1)}, f32[168,128]{1,0:T(8,128)S(1)}, u32[]{:S(2)}, u32[]{:S(2)}) collective-permute-start(f32[168,128]{1,0:T(8,128)S(1)} %collective-permute-done.32.refs_9_), channel_id=1, source_target_pairs={{0,4},{4,0},{8,12},{12,8},{16,20},{20,16},{24,28},{28,24},{1,5},{5... | collective-permute-start | bytes 258056 | tf_op jit(solution)/shard_map/ppermute | solution.py:349
  60.9 1.3 %collective-permute-start.35 = (f32[168,128]{1,0:T(8,128)S(1)}, f32[168,128]{1,0:T(8,128)S(1)}, u32[]{:S(2)}, u32[]{:S(2)}) collective-permute-start(f32[168,128]{1,0:T(8,128)S(1)} %collective-permute-done.31.refs_8_), channel_id=1, source_target_pairs={{0,4},{4,0},{8,12},{12,8},{16,20},{20,16},{24,28},{28,24},{1,5},{5... | collective-permute-start | bytes 258056 | tf_op jit(solution)/shard_map/ppermute | solution.py:349
  61.3 1.3 %collective-permute-start.34 = (f32[168,128]{1,0:T(8,128)S(1)}, f32[168,128]{1,0:T(8,128)S(1)}, u32[]{:S(2)}, u32[]{:S(2)}) collective-permute-start(f32[168,128]{1,0:T(8,128)S(1)} %collective-permute-done.30.refs_7_), channel_id=1, source_target_pairs={{0,4},{4,0},{8,12},{12,8},{16,20},{20,16},{24,28},{28,24},{1,5},{5... | collective-permute-start | bytes 258056 | tf_op jit(solution)/shard_map/ppermute | solution.py:349

commit v2 on v1

--- a/solution.py
+++ b/solution.py
@@ -25,26 +25,43 @@
     return rows == lax.broadcasted_iota(jnp.int32, (width, width), 1)
 
 
-def adjoint_terms(blocks, block_row, wide, out):
-    def step(b, _):
-        product = blocks[b] * wide[block_row[b]]
-        out[pl.ds(b, 1), :] = jnp.sum(product, axis=0, keepdims=True)
-        return 0
-
-    lax.fori_loop(0, blocks.shape[0], step, 0, unroll=8)
-
-
-def forward_sums(blocks, block_row, extra, start, sums):
+def each_block(rows, count, group, body):
+    if len(rows.shape) == 1:
+
+        def plain(b, _):
+            body(b, rows[b])
+            return 0
+
+        lax.fori_loop(0, count, plain, 0, unroll=group)
+        return
+    assert count % group == 0
+    read = lambda first: tuple(rows[pl.ds(first + i, 1), :][0, 0] for i in range(group))
+
+    def step(g, now):
+        later = read(jnp.minimum((g + 1) * group, count - group))
+        for i in range(group):
+            body(g * group + i, now[i])
+        return later
+
+    lax.fori_loop(0, count // group, step, read(0))
+
+
+def adjoint_terms(blocks, rows, wide, out):
+    def body(b, row):
+        out[pl.ds(b, 1), :] = jnp.sum(blocks[b] * wide[row], axis=0, keepdims=True)
+
+    each_block(rows, blocks.shape[0], 8, body)
+
+
+def forward_sums(blocks, rows, extra, start, sums):
     part = blocks.shape[1] // len(sums)
 
-    def step(b, _):
-        row = block_row[b]
+    def body(b, row):
         scale = extra[pl.ds(start + b, 1), :]
         for q, total in enumerate(sums):
             total[row] += blocks[b, q * part : (q + 1) * part, :] * scale
-        return 0
-
-    lax.fori_loop(0, blocks.shape[0], step, 0, unroll=4)
+
+    each_block(rows, blocks.shape[0], 4, body)
 
 
 def fill_wide(duals, wide):
@@ -97,16 +114,19 @@
 
 def first_terms(sizes, *refs):
     _, piece, tail_own = sizes
-    indices, (zeros, blocks, duals), hub_own, tail_consts = refs[:4], refs[4:7], refs[7:10], refs[10:13]
-    payload, wide, state, *scratch, sems = refs[13:]
+    indices, (zeros, blocks, duals), hub_own, tail_consts = refs[:5], refs[5:8], refs[8:11], refs[11:14]
+    payload, wide, state, tail_rows, hub_rows, *scratch, sems = refs[14:]
     copies = to_smem(indices, scratch, sems)
-    hub_row, hub_col, owner, slot_of = scratch
+    hub_row, hub_col, owner, slot_of, tail_row = scratch
     width = duals.shape[1]
     hub_n, tail_n = blocks.shape[0], owner.shape[0]
     for which, source in enumerate(tail_consts):
         state[which * tail_own : (which + 1) * tail_own, :] = source[...]
     fill_wide(duals, wide)
     wait_all(copies)
+    for source, target in ((tail_row, tail_rows), (hub_row, hub_rows)):
+        for b in range(target.shape[0]):
+            target[b : b + 1, :] = jnp.full((1, width), source[b], jnp.int32)
     adjoint_terms(blocks, hub_row, wide, payload)
     mine = lax.axis_index("rows") * piece
     for which, source in enumerate(hub_own):
@@ -160,16 +180,12 @@
     pick_rows(x.shape[0], (x, cost, upper), keys, 0, pool, where)
 
 
-def tail_terms(own_sizes, row_in, blocks, wide, *refs):
-    *own, row, sems = refs
-    copies = to_smem((row_in,), (row,), sems)
-    if own_sizes is None:
-        (out,) = own
-    else:
-        out = own.pop(-3)
+def tail_terms(own_sizes, rows, blocks, wide, *refs):
+    own = list(refs)
+    out = own.pop(-1 if own_sizes is None else -3)
+    adjoint_terms(blocks, rows, wide, out)
+    if own_sizes is not None:
         own_step(own_sizes, *own)
-    wait_all(copies)
-    adjoint_terms(blocks, row, wide, out)
 
 
 def gathered_ids(sizes, states, pieces, ids):
@@ -209,7 +225,7 @@
     refs = list(refs)
     take = lambda n: [refs.pop(0) for _ in range(n)]
     indices = take(3 if first else 2)
-    tail_blocks, hub_blocks, duals, demand = take(4)
+    hub_rows, tail_blocks, hub_blocks, duals, demand = take(5)
     pieces = take(slots)
     if first:
         states = take(slots)
@@ -269,10 +285,10 @@
         start = jnp.where(eye, (-1.0 / dual_step) * base[r : r + 1, :], 0.0)
         for q in range(PARTS):
             sums[q][r] = start[q * part : (q + 1) * part, :]
+    forward_sums(hub_blocks, hub_row if first else hub_rows, extra, tail_n, sums)
     if not first:
         wait_all(copies)
     forward_sums(tail_blocks, tail_row, extra, 0, sums)
-    forward_sums(hub_blocks, hub_row, extra, tail_n, sums)
     for r in range(base.shape[0]):
         diagonal = jnp.zeros((1, width), jnp.float32)
         for q in range(PARTS):
@@ -303,10 +319,15 @@
 
 
 def call(kernel, ins, outs, scratch, flops):
+    def shape(*sizes):
+        if isinstance(sizes[-1], int):
+            return jax.ShapeDtypeStruct(sizes, jnp.float32)
+        return jax.ShapeDtypeStruct(sizes[:-1], sizes[-1])
+
     spec = lambda items: [pl.BlockSpec(memory_space=VMEM)] * len(items)
     return pl.pallas_call(
         kernel,
-        out_shape=[jax.ShapeDtypeStruct(s, jnp.float32) for s in outs],
+        out_shape=[shape(*s) for s in outs],
         in_specs=spec(ins),
         out_specs=spec(outs),
         scratch_shapes=scratch,
@@ -364,12 +385,12 @@
     big = (row_n, width, width)
 
     (zeros,) = call(seed, (), [(8, width)], [], SEED_FLOPS)
-    payload, wide, state = call(
+    payload, wide, state, tail_rows, hub_rows = call(
         functools.partial(first_terms, (row_devs, piece, tail_own)),
-        (hub_row, hub_col, owners, tail_slot, zeros, hub_blocks, duals)
+        (hub_row, hub_col, owners, tail_slot, tail_row, zeros, hub_blocks, duals)
         + (x_hub, cost_hub, upper_hub, x_tail, cost_tail, upper_tail),
-        [(each, width), big, (state_n, width)],
-        ints(hub_n, hub_n, tail_n, tail_n),
+        [(each, width), big, (state_n, width), (tail_n, width, jnp.int32), (hub_n, width, jnp.int32)],
+        ints(hub_n, hub_n, tail_n, tail_n, tail_n),
         hub_n * work,
     )
     states = over_rows(state)
@@ -388,9 +409,9 @@
         first, last = iteration == 0, iteration == ITERS - 1
         terms, *own_new = call(
             functools.partial(tail_terms, None if first else (tail_n, hub_n, hub_devs, step_each, row_devs)),
-            (tail_row, tail_blocks, wide) + (() if first else (kept[-1], *pieces, *own)),
+            (tail_rows, tail_blocks, wide) + (() if first else (kept[-1], *pieces, *own)),
             [(tail_n, width)] + ([] if first else own_outs),
-            ints(tail_n),
+            [],
             tail_n * work,
         )
         if not first:
@@ -398,7 +419,7 @@
         parts = over_hub(payload)
         pieces = over_rows(jnp.concatenate([terms] + parts, axis=0))
         step_each = each if first else hub_n
-        ins = (tail_row, hub_row) + (hub_col,) * first + (tail_blocks, hub_blocks, duals, demand, *pieces)
+        ins = (tail_row, hub_row) + (hub_col,) * first + (hub_rows, tail_blocks, hub_blocks, duals, demand, *pieces)
         ins += (*states, *picked) if first else kept
         ins += own if last else ()
         outs = [(row_n, width)] + (own_outs if last else [(hub_n, width), big, held])

time: 65.7 us -> 65.1 us (level)
  transfers between devices with their start and end apart: 37 -> 37, of which waited for: 19 -> 20; matrix products, arithmetic and copies ran while one was open for 0% -> 0% of each run, Pallas kernels for 7% -> 7%
where the time goes in v2:
time: 65.1 us; the launch traced here: 64.8 us
  starting transfers between devices  32.2 us (49%)
  waiting for transfers between devices  17.1 us (26%)
  Pallas kernels  13.1 us (20%)
  local copies, waits for them, and re-layouts  1.43 us (2%)
  between operations  1 us (2%)
    ppermute x37, starting transfers between devices, swap(): return lax.ppermute(value, axis, [(i, i ^ mask) for i in range(count)])  32.2 us
    ppermute x37, waiting for transfers between devices, swap(): return lax.ppermute(value, axis, [(i, i ^ mask) for i in range(count)])  17.1 us
    pallas_call x9, Pallas kernels, call(): pl.pallas_call(kernel, out_shape=[shape(*s) for s in outs], in_specs=spec...  13.1 us
    unnamed x42, local copies, waits for them, and re-layouts  1.43 us
  transfers between devices with their start and end apart: 37, of which 20 were waited for; matrix products, arithmetic and copies ran while one was open for 0% of the time, Pallas kernels for 7%

profile of v2, /device:TPU:0, one launch (start us, length us, event | category | flops | bytes accessed | tf_op | source)
XLA Modules:
  0.0 64.8 jit_solution(7740475024358820441)
XLA Ops:
  0.8 0.0 copy-start.7
  0.8 0.6 copy-done.5
  1.4 0.0 copy-done.4
  1.4 0.1 copy-done.3
  1.4 0.0 copy-done.2
  1.4 0.7 %copy-done.1 = f32[24,128,128]{2,1,0:T(8,128)S(1)} copy-done((f32[24,128,128]{2,1,0:T(8,128)S(1)}, f32[24,128,128]{2,1,0:T(8,128)}, u32[]{:S(2)}) %copy-start.1) | copy-done | bytes 1572888
  2.2 1.2 %shard_map.167 = (f32[40,128]{1,0:T(8,128)S(1)}, f32[16,128,128]{2,1,0:T(8,128)S(1)}, f32[200,128]{1,0:T(8,128)S(1)}, s32[72,128]{1,0:T(8,128)S(1)}, s32[24,128]{1,0:T(8,128)S(1)}) custom-call(s32[24]{0:T(128)S(1)} %copy-done.11, s32[24]{0:T(128)S(1)} %copy-done.14, s32[72]{0:T(128)S(1)} %bitcast.1, s32[72]{0:T(128)S(1)} %copy-done.13, s32[72]{0:T(128)S(1)} %copy-done.10, ...), custom_call_target="tpu_custom_call" | custom-call | flops 786432 | tf_op jit(solution)/shard_map/pallas_call | solution.py:328
  3.4 5.1 %collective-permute-start.2 = (f32[40,128]{1,0:T(8,128)S(1)}, f32[40,128]{1,0:T(8,128)S(1)}, u32[]{:S(2)}, u32[]{:S(2)}) collective-permute-start(f32[40,128]{1,0:T(8,128)S(1)} %get-tuple-element.36), channel_id=1, source_target_pairs={{0,3},{1,2},{2,1},{3,0},{4,7},{5,6},{6,5},{7,4},{8,11},{9,10},{10,... | collective-permute-start | bytes 61448 | tf_op jit(solution)/shard_map/ppermute | solution.py:370
  8.5 0.6 collective-permute-start
  9.2 2.6 %collective-permute-start.12 = (f32[200,128]{1,0:T(8,128)S(1)}, f32[200,128]{1,0:T(8,128)S(1)}, u32[]{:S(2)}, u32[]{:S(2)}) collective-permute-start(f32[200,128]{1,0:T(8,128)S(1)} %get-tuple-element.37.refs_2_.refs_16_), channel_id=1, source_target_pairs={{0,24},{4,28},{8,16},{12,20},{16,8},{20,12},{24,0},{28,4},{1,25},{... | collective-permute-start | bytes 307208 | tf_op jit(solution)/shard_map/ppermute | solution.py:370
  11.8 0.8 %shard_map.168 = f32[72,128]{1,0:T(8,128)S(1)} custom-call(s32[72,128]{1,0:T(8,128)S(1)} %get-tuple-element.34.rows, f32[72,128,128]{2,1,0:T(8,128)S(1)} %copy-done, f32[16,128,128]{2,1,0:T(8,128)S(1)} %get-tuple-element.35.wide), custom_call_target="tpu_custom_call" | custom-call | flops 2359296 | tf_op jit(solution)/shard_map/pallas_call | solution.py:328
  12.6 0.0 collective-permute-done
  12.6 1.2 %collective-permute-start.11 = (f32[200,128]{1,0:T(8,128)S(1)}, f32[200,128]{1,0:T(8,128)S(1)}, u32[]{:S(2)}, u32[]{:S(2)}) collective-permute-start(f32[200,128]{1,0:T(8,128)S(1)} %get-tuple-element.37.refs_2_.refs_16_), channel_id=1, source_target_pairs={{0,16},{4,20},{8,24},{12,28},{16,0},{20,4},{24,8},{28,12},{1,17},{... | collective-permute-start | bytes 307208 | tf_op jit(solution)/shard_map/ppermute | solution.py:370
  13.8 0.0 collective-permute-done.1
  13.8 1.5 %collective-permute-start.10 = (f32[200,128]{1,0:T(8,128)S(1)}, f32[200,128]{1,0:T(8,128)S(1)}, u32[]{:S(2)}, u32[]{:S(2)}) collective-permute-start(f32[200,128]{1,0:T(8,128)S(1)} %get-tuple-element.37.refs_2_.refs_16_), channel_id=1, source_target_pairs={{0,8},{4,12},{8,0},{12,4},{16,24},{20,28},{24,16},{28,20},{1,9},{5... | collective-permute-start | bytes 307208 | tf_op jit(solution)/shard_map/ppermute | solution.py:370
  15.3 0.0 collective-permute-done.2
  15.3 0.9 %collective-permute-start.5 = (f32[232,128]{1,0:T(8,128)S(1)}, f32[232,128]{1,0:T(8,128)S(1)}, u32[]{:S(2)}, u32[]{:S(2)}) collective-permute-start(f32[232,128]{1,0:T(8,128)S(1)} %constant_dynamic-update-slice_fusion.refs_8_.refs_1_), channel_id=1, source_target_pairs={{0,24},{4,28},{8,16},{12,20},{16,8},{20,12},{24,0},{28,4},{1,25},{... | collective-permute-start | bytes 356360 | tf_op jit(solution)/shard_map/ppermute | solution.py:370
  16.3 0.0 collective-permute-done.13.refs_6_.refs_20_
  16.3 1.1 %collective-permute-start.4 = (f32[232,128]{1,0:T(8,128)S(1)}, f32[232,128]{1,0:T(8,128)S(1)}, u32[]{:S(2)}, u32[]{:S(2)}) collective-permute-start(f32[232,128]{1,0:T(8,128)S(1)} %constant_dynamic-update-slice_fusion.refs_8_.refs_1_), channel_id=1, source_target_pairs={{0,16},{4,20},{8,24},{12,28},{16,0},{20,4},{24,8},{28,12},{1,17},{... | collective-permute-start | bytes 356360 | tf_op jit(solution)/shard_map/ppermute | solution.py:370
  17.4 1.5 %collective-permute-start.3 = (f32[232,128]{1,0:T(8,128)S(1)}, f32[232,128]{1,0:T(8,128)S(1)}, u32[]{:S(2)}, u32[]{:S(2)}) collective-permute-start(f32[232,128]{1,0:T(8,128)S(1)} %constant_dynamic-update-slice_fusion.refs_8_.refs_1_), channel_id=1, source_target_pairs={{0,8},{4,12},{8,0},{12,4},{16,24},{20,28},{24,16},{28,20},{1,9},{5... | collective-permute-start | bytes 356360 | tf_op jit(solution)/shard_map/ppermute | solution.py:370
  18.9 0.0 collective-permute-done.11.refs_4_.refs_18_
  18.9 0.0 collective-permute-start.16
  18.9 0.7 %collective-permute-done.10.refs_3_.refs_17_ = f32[200,128]{1,0:T(8,128)S(1)} collective-permute-done((f32[200,128]{1,0:T(8,128)S(1)}, f32[200,128]{1,0:T(8,128)S(1)}, u32[]{:S(2)}, u32[]{:S(2)}) %collective-permute-start.10) | collective-permute-done | bytes 102432 | tf_op jit(solution)/shard_map/ppermute | solution.py:370
  19.6 2.9 %collective-permute-done.5.refs_11_.refs_4_ = f32[232,128]{1,0:T(8,128)S(1)} collective-permute-done((f32[232,128]{1,0:T(8,128)S(1)}, f32[232,128]{1,0:T(8,128)S(1)}, u32[]{:S(2)}, u32[]{:S(2)}) %collective-permute-start.5) | collective-permute-done | bytes 118816 | tf_op jit(solution)/shard_map/ppermute | solution.py:370
  22.5 0.6 collective-permute-done.4.refs_10_.refs_3_
  23.1 0.1 collective-permute-done.3.refs_9_.refs_2_
  23.2 0.4 collective-permute-start.8
  23.6 0.1 collective-permute-start.7
  23.7 0.4 collective-permute-start.14
  24.1 1.0 %collective-permute-done.14.refs_7_.refs_21_ = f32[200,128]{1,0:T(8,128)S(1)} collective-permute-done((f32[200,128]{1,0:T(8,128)S(1)}, f32[200,128]{1,0:T(8,128)S(1)}, u32[]{:S(2)}, u32[]{:S(2)}) %collective-permute-start.14) | collective-permute-done | bytes 102432 | tf_op jit(solution)/shard_map/ppermute | solution.py:370
  25.1 0.9 %shard_map.169 = (f32[72,128]{1,0:T(8,128)S(1)}, f32[72,128]{1,0:T(8,128)S(1)}, f32[72,128]{1,0:T(8,128)S(1)}, f32[72,128]{1,0:T(8,128)S(1)}) custom-call(s32[72]{0:T(128)S(1)} %bitcast.2, s32[72]{0:T(128)S(1)} %copy-done.13, f32[200,128]{1,0:T(8,128)S(1)} %get-tuple-element.37.refs_2_.refs_16_, f32[200,128]{1,0:T(8,128)S(1)} %collective-permute-done.10.refs_3_.refs_17_, ...), custom_call_target="tpu_custom_call" | custom-call | flops 73728 | tf_op jit(solution)/shard_map/pallas_call | solution.py:328
  26.0 2.8 %shard_map.170 = (f32[16,128]{1,0:T(8,128)S(1)}, f32[24,128]{1,0:T(8,128)S(1)}, f32[16,128,128]{2,1,0:T(8,128)S(1)}, f32[96,128]{1,0:T(8,128)S(1)}, f32[96,128]{...) custom-call(s32[72]{0:T(128)S(1)} %copy-done.10, s32[24]{0:T(128)S(1)} %copy-done.11, ...), custom_call_target="tpu_custom_call" | custom-call | flops 3145728 | tf_op jit(solution)/shard_map/pallas_call | solution.py:328
  28.8 3.7 %collective-permute-start.19 = (f32[24,128]{1,0:T(8,128)S(1)}, f32[24,128]{1,0:T(8,128)S(1)}, u32[]{:S(2)}, u32[]{:S(2)}) collective-permute-start(f32[24,128]{1,0:T(8,128)S(1)} %get-tuple-element.46), channel_id=1, source_target_pairs={{0,3},{1,2},{2,1},{3,0},{4,7},{5,6},{6,5},{7,4},{8,11},{9,10},{10,... | collective-permute-start | bytes 36872 | tf_op jit(solution)/shard_map/ppermute | solution.py:370
  32.5 0.8 %collective-permute-start.17 = (f32[24,128]{1,0:T(8,128)S(1)}, f32[24,128]{1,0:T(8,128)S(1)}, u32[]{:S(2)}, u32[]{:S(2)}) collective-permute-start(f32[24,128]{1,0:T(8,128)S(1)} %get-tuple-element.46), channel_id=1, source_target_pairs={{0,1},{1,0},{2,3},{3,2},{4,5},{5,4},{6,7},{7,6},{8,9},{9,8},{10,11... | collective-permute-start | bytes 36872 | tf_op jit(solution)/shard_map/ppermute | solution.py:370
  33.3 1.3 %shard_map.171 = (f32[72,128]{1,0:T(8,128)S(1)}, f32[64,128]{1,0:T(8,128)S(1)}, f32[32,128]{1,0:T(8,128)S(1)}) custom-call(s32[72,128]{1,0:T(8,128)S(1)} %get-tuple-element.34.rows, f32[72,128,128]{2,1,0:T(8,128)S(1)} %copy-done, f32[16,128,128]{2,1,0:T(8,128)S(1)} %get-tuple-element.43.wide, f32[16,128]{1,0:T(8,128)S(1)} %get-tuple-element.44.refs_0_.refs_19_, ...), custom_call_target="tpu_custom_call" | custom-call | flops 2359296 | tf_op jit(solution)/shard_map/pallas_call | solution.py:328
  34.6 1.7 %collective-permute-done.17 = f32[24,128]{1,0:T(8,128)S(1)} collective-permute-done((f32[24,128]{1,0:T(8,128)S(1)}, f32[24,128]{1,0:T(8,128)S(1)}, u32[]{:S(2)}, u32[]{:S(2)}) %collective-permute-start.17) | collective-permute-done | bytes 12320 | tf_op jit(solution)/shard_map/ppermute | solution.py:370
  36.3 0.8 %collective-permute-done.18 = f32[24,128]{1,0:T(8,128)S(1)} collective-permute-done((f32[24,128]{1,0:T(8,128)S(1)}, f32[24,128]{1,0:T(8,128)S(1)}, u32[]{:S(2)}, u32[]{:S(2)}) %collective-permute-start.18) | collective-permute-done | bytes 12320 | tf_op jit(solution)/shard_map/ppermute | solution.py:370
  37.1 2.2 %collective-permute-start.22 = (f32[168,128]{1,0:T(8,128)S(1)}, f32[168,128]{1,0:T(8,128)S(1)}, u32[]{:S(2)}, u32[]{:S(2)}) collective-permute-start(f32[168,128]{1,0:T(8,128)S(1)} %constant_dynamic-update-slice_fusion.5.refs_7_.refs_1_), channel_id=1, source_target_pairs={{0,24},{4,28},{8,16},{12,20},{16,8},{20,12},{24,0},{28,4},{1,25},{... | collective-permute-start | bytes 258056 | tf_op jit(solution)/shard_map/ppermute | solution.py:370
  39.3 0.5 collective-permute-start.21
  39.8 0.9 %collective-permute-start.20 = (f32[168,128]{1,0:T(8,128)S(1)}, f32[168,128]{1,0:T(8,128)S(1)}, u32[]{:S(2)}, u32[]{:S(2)}) collective-permute-start(f32[168,128]{1,0:T(8,128)S(1)} %constant_dynamic-update-slice_fusion.5.refs_7_.refs_1_), channel_id=1, source_target_pairs={{0,8},{4,12},{8,0},{12,4},{16,24},{20,28},{24,16},{28,20},{1,9},{5... | collective-permute-start | bytes 258056 | tf_op jit(solution)/shard_map/ppermute | solution.py:370
  40.6 2.7 %collective-permute-done.22.refs_10_.refs_4_ = f32[168,128]{1,0:T(8,128)S(1)} collective-permute-done((f32[168,128]{1,0:T(8,128)S(1)}, f32[168,128]{1,0:T(8,128)S(1)}, u32[]{:S(2)}, u32[]{:S(2)}) %collective-permute-start.22) | collective-permute-done | bytes 86048 | tf_op jit(solution)/shard_map/ppermute | solution.py:370
  43.4 0.6 collective-permute-done.21.refs_9_.refs_3_
  44.0 0.2 collective-permute-done.20.refs_8_.refs_2_
  44.3 0.3 collective-permute-start.24
  44.5 0.1 collective-permute-done.26.refs_14_.refs_8_
  44.7 0.6 collective-permute-done.25.refs_13_.refs_7_
  45.3 0.2 collective-permute-done.24.refs_12_.refs_6_
  45.5 2.0 %shard_map.172 = (f32[16,128]{1,0:T(8,128)S(1)}, f32[24,128]{1,0:T(8,128)S(1)}, f32[16,128,128]{2,1,0:T(8,128)S(1)}, f32[96,128]{1,0:T(8,128)S(1)}) custom-call(s32[72]{0:T(128)S(1)} %copy-done.10, s32[24]{0:T(128)S(1)} %copy-done.11, s32[24,128]{1,0:T(8,128)S(1)} %get-tuple-element.33.refs_3_.refs_2_, f32[72,128,128]{2,1,0:T(8,128)S(1)} %copy-done, ...), custom_call_target="tpu_custom_call" | custom-call | flops 3145728 | tf_op jit(solution)/shard_map/pallas_call | solution.py:328
  47.6 1.6 %collective-permute-start.29 = (f32[24,128]{1,0:T(8,128)S(1)}, f32[24,128]{1,0:T(8,128)S(1)}, u32[]{:S(2)}, u32[]{:S(2)}) collective-permute-start(f32[24,128]{1,0:T(8,128)S(1)} %get-tuple-element.56), channel_id=1, source_target_pairs={{0,3},{1,2},{2,1},{3,0},{4,7},{5,6},{6,5},{7,4},{8,11},{9,10},{10,... | collective-permute-start | bytes 36872 | tf_op jit(solution)/shard_map/ppermute | solution.py:370
  49.1 0.6 collective-permute-start.28
  49.8 2.3 %collective-permute-start.27 = (f32[24,128]{1,0:T(8,128)S(1)}, f32[24,128]{1,0:T(8,128)S(1)}, u32[]{:S(2)}, u32[]{:S(2)}) collective-permute-start(f32[24,128]{1,0:T(8,128)S(1)} %get-tuple-element.56), channel_id=1, source_target_pairs={{0,1},{1,0},{2,3},{3,2},{4,5},{5,4},{6,7},{7,6},{8,9},{9,8},{10,11... | collective-permute-start | bytes 36872 | tf_op jit(solution)/shard_map/ppermute | solution.py:370
  52.0 1.3 %shard_map.173 = (f32[72,128]{1,0:T(8,128)S(1)}, f32[64,128]{1,0:T(8,128)S(1)}, f32[32,128]{1,0:T(8,128)S(1)}) custom-call(s32[72,128]{1,0:T(8,128)S(1)} %get-tuple-element.34.rows, f32[72,128,128]{2,1,0:T(8,128)S(1)} %copy-done, f32[16,128,128]{2,1,0:T(8,128)S(1)} %get-tuple-element.52.wide, f32[16,128]{1,0:T(8,128)S(1)} %get-tuple-element.44.refs_0_.refs_19_, ...), custom_call_target="tpu_custom_call" | custom-call | flops 2359296 | tf_op jit(solution)/shard_map/pallas_call | solution.py:328
  53.4 0.5 collective-permute-done.27
  53.9 1.6 %collective-permute-start.32 = (f32[168,128]{1,0:T(8,128)S(1)}, f32[168,128]{1,0:T(8,128)S(1)}, u32[]{:S(2)}, u32[]{:S(2)}) collective-permute-start(f32[168,128]{1,0:T(8,128)S(1)} %constant_dynamic-update-slice_fusion.10.refs_7_), channel_id=1, source_target_pairs={{0,24},{4,28},{8,16},{12,20},{16,8},{20,12},{24,0},{28,4},{1,25},{... | collective-permute-start | bytes 258056 | tf_op jit(solution)/shard_map/ppermute | solution.py:370
  55.5 0.8 %collective-permute-start.31 = (f32[168,128]{1,0:T(8,128)S(1)}, f32[168,128]{1,0:T(8,128)S(1)}, u32[]{:S(2)}, u32[]{:S(2)}) collective-permute-start(f32[168,128]{1,0:T(8,128)S(1)} %constant_dynamic-update-slice_fusion.10.refs_7_), channel_id=1, source_target_pairs={{0,16},{4,20},{8,24},{12,28},{16,0},{20,4},{24,8},{28,12},{1,17},{... | collective-permute-start | bytes 258056 | tf_op jit(solution)/shard_map/ppermute | solution.py:370
  56.3 1.2 %collective-permute-start.30 = (f32[168,128]{1,0:T(8,128)S(1)}, f32[168,128]{1,0:T(8,128)S(1)}, u32[]{:S(2)}, u32[]{:S(2)}) collective-permute-start(f32[168,128]{1,0:T(8,128)S(1)} %constant_dynamic-update-slice_fusion.10.refs_7_), channel_id=1, source_target_pairs={{0,8},{4,12},{8,0},{12,4},{16,24},{20,28},{24,16},{28,20},{1,9},{5... | collective-permute-start | bytes 258056 | tf_op jit(solution)/shard_map/ppermute | solution.py:370
  57.4 2.6 %collective-permute-done.32.refs_10_ = f32[168,128]{1,0:T(8,128)S(1)} collective-permute-done((f32[168,128]{1,0:T(8,128)S(1)}, f32[168,128]{1,0:T(8,128)S(1)}, u32[]{:S(2)}, u32[]{:S(2)}) %collective-permute-start.32) | collective-permute-done | bytes 86048 | tf_op jit(solution)/shard_map/ppermute | solution.py:370
  60.0 0.6 collective-permute-done.31.refs_9_
  60.6 0.2 collective-permute-done.30.refs_8_
  60.7 0.3 collective-permute-start.34
  61.1 0.2 collective-permute-done.36.refs_14_
  61.3 0.6 collective-permute-done.35.refs_13_
  61.8 0.2 collective-permute-done.34.refs_12_
  62.0 2.8 %shard_map.174 = (f32[16,128]{1,0:T(8,128)}, f32[64,128]{1,0:T(8,128)}, f32[32,128]{1,0:T(8,128)}) custom-call(s32[72]{0:T(128)S(1)} %copy-done.10, s32[24]{0:T(128)S(1)} %copy-done.11, s32[24,128]{1,0:T(8,128)S(1)} %get-tuple-element.33.refs_3_.refs_2_, f32[72,128,128]{2,1,0:T(8,128)S(1)} %copy-done, f32[24,128,128]{2,1,0:T(8,128)S(1)} %copy-done.1, ...), custom_call_target="tpu_custom_call" | custom-call | flops 3145728 | tf_op jit(solution)/shard_map/pallas_call | solution.py:328
  (64 shorter events, 0.2 us)
Async XLA Ops:
  0.6 0.7 %copy-start.5 = (f32[32,128]{1,0:T(8,128)S(1)}, f32[32,128]{1,0:T(8,128)}, u32[]{:S(2)}) copy-start(f32[32,128]{1,0:T(8,128)} %refs_25_.1) | copy-start | bytes 49156
  0.6 0.7 %copy-start.4 = (f32[32,128]{1,0:T(8,128)S(1)}, f32[32,128]{1,0:T(8,128)}, u32[]{:S(2)}) copy-start(f32[32,128]{1,0:T(8,128)} %refs_24_.1) | copy-start | bytes 49156
  0.7 0.8 %copy-start.3 = (f32[64,128]{1,0:T(8,128)S(1)}, f32[64,128]{1,0:T(8,128)}, u32[]{:S(2)}) copy-start(f32[64,128]{1,0:T(8,128)} %refs_22_.1) | copy-start | bytes 98308
  0.7 0.8 %copy-start.2 = (f32[64,128]{1,0:T(8,128)S(1)}, f32[64,128]{1,0:T(8,128)}, u32[]{:S(2)}) copy-start(f32[64,128]{1,0:T(8,128)} %refs_21_.1) | copy-start | bytes 98308
  0.7 0.8 %copy-start.11 = (s32[24]{0:T(128)S(1)}, s32[24]{0:T(128)}, u32[]{:S(2)}) copy-start(s32[24]{0:T(128)} %refs_1_.9) | copy-start | bytes 292
  0.7 1.4 %copy-start.1 = (f32[24,128,128]{2,1,0:T(8,128)S(1)}, f32[24,128,128]{2,1,0:T(8,128)}, u32[]{:S(2)}) copy-start(f32[24,128,128]{2,1,0:T(8,128)} %refs_4_.7) | copy-start | bytes 4718596
  0.7 1.4 %copy-start.10 = (s32[72]{0:T(128)S(1)}, s32[72]{0:T(128)}, u32[]{:S(2)}) copy-start(s32[72]{0:T(128)} %refs_0_.7) | copy-start | bytes 868
  0.7 1.4 %copy-start.9 = (f32[16,128]{1,0:T(8,128)S(1)}, f32[16,128]{1,0:T(8,128)}, u32[]{:S(2)}) copy-start(f32[16,128]{1,0:T(8,128)} %refs_6_.5) | copy-start | bytes 24580
  0.7 1.4 %copy-start.8 = (f32[32,128]{1,0:T(8,128)S(1)}, f32[32,128]{1,0:T(8,128)}, u32[]{:S(2)}) copy-start(f32[32,128]{1,0:T(8,128)} %refs_12_.3) | copy-start | bytes 49156
  0.7 1.4 %copy-start.6 = (f32[64,128]{1,0:T(8,128)S(1)}, f32[64,128]{1,0:T(8,128)}, u32[]{:S(2)}) copy-start(f32[64,128]{1,0:T(8,128)} %refs_9_.3) | copy-start | bytes 98308
  0.7 1.4 %copy-start.14 = (s32[24]{0:T(128)S(1)}, s32[24]{0:T(128)}, u32[]{:S(2)}) copy-start(s32[24]{0:T(128)} %refs_2_.1) | copy-start | bytes 292
  0.7 1.4 %copy-start.13 = (s32[72]{0:T(128)S(1)}, s32[72]{0:T(128)}, u32[]{:S(2)}) copy-start(s32[72]{0:T(128)} %refs_1_.6) | copy-start | bytes 868
  0.8 1.4 %copy-start.12 = (s32[72,1]{0,1:T(1,128)S(1)}, s32[72,1]{0,1:T(1,128)}, u32[]{:S(2)}) copy-start(s32[72,1]{0,1:T(1,128)} %param.17) | copy-start | bytes 868
  0.8 11.0 %copy-start = (f32[72,128,128]{2,1,0:T(8,128)S(1)}, f32[72,128,128]{2,1,0:T(8,128)}, u32[]{:S(2)}) copy-start(f32[72,128,128]{2,1,0:T(8,128)} %refs_3_.5) | copy-start | bytes 14155780
  0.8 25.2 %copy-start.7 = (f32[16,128]{1,0:T(8,128)S(1)}, f32[16,128]{1,0:T(8,128)}, u32[]{:S(2)}) copy-start(f32[16,128]{1,0:T(8,128)} %refs_6_.7) | copy-start | bytes 24580
  3.4 12.0 %collective-permute-start.2 = (f32[40,128]{1,0:T(8,128)S(1)}, f32[40,128]{1,0:T(8,128)S(1)}, u32[]{:S(2)}, u32[]{:S(2)}) collective-permute-start(f32[40,128]{1,0:T(8,128)S(1)} %get-tuple-element.36), channel_id=1, source_target_pairs={{0,3},{1,2},{2,1},{3,0},{4,7},{5,6},{6,5},{7,4},{8,11},{9,10},{10,... | collective-permute-start | bytes 61448 | tf_op jit(solution)/shard_map/ppermute | solution.py:370
  8.5 5.3 %collective-permute-start.1 = (f32[40,128]{1,0:T(8,128)S(1)}, f32[40,128]{1,0:T(8,128)S(1)}, u32[]{:S(2)}, u32[]{:S(2)}) collective-permute-start(f32[40,128]{1,0:T(8,128)S(1)} %get-tuple-element.36), channel_id=1, source_target_pairs={{0,2},{1,3},{2,0},{3,1},{4,6},{5,7},{6,4},{7,5},{8,10},{9,11},{10,... | collective-permute-start | bytes 61448 | tf_op jit(solution)/shard_map/ppermute | solution.py:370
  8.5 4.1 %collective-permute-start = (f32[40,128]{1,0:T(8,128)S(1)}, f32[40,128]{1,0:T(8,128)S(1)}, u32[]{:S(2)}, u32[]{:S(2)}) collective-permute-start(f32[40,128]{1,0:T(8,128)S(1)} %get-tuple-element.36), channel_id=1, source_target_pairs={{0,1},{1,0},{2,3},{3,2},{4,5},{5,4},{6,7},{7,6},{8,9},{9,8},{10,11... | collective-permute-start | bytes 61448 | tf_op jit(solution)/shard_map/ppermute | solution.py:370
  9.2 7.1 %collective-permute-start.13 = (f32[200,128]{1,0:T(8,128)S(1)}, f32[200,128]{1,0:T(8,128)S(1)}, u32[]{:S(2)}, u32[]{:S(2)}) collective-permute-start(f32[200,128]{1,0:T(8,128)S(1)} %get-tuple-element.37.refs_2_.refs_16_), channel_id=1, source_target_pairs={{0,4},{4,0},{8,12},{12,8},{16,20},{20,16},{24,28},{28,24},{1,5},{5... | collective-permute-start | bytes 307208 | tf_op jit(solution)/shard_map/ppermute | solution.py:370
  9.2 8.2 %collective-permute-start.12 = (f32[200,128]{1,0:T(8,128)S(1)}, f32[200,128]{1,0:T(8,128)S(1)}, u32[]{:S(2)}, u32[]{:S(2)}) collective-permute-start(f32[200,128]{1,0:T(8,128)S(1)} %get-tuple-element.37.refs_2_.refs_16_), channel_id=1, source_target_pairs={{0,24},{4,28},{8,16},{12,20},{16,8},{20,12},{24,0},{28,4},{1,25},{... | collective-permute-start | bytes 307208 | tf_op jit(solution)/shard_map/ppermute | solution.py:370
  12.6 6.3 %collective-permute-start.11 = (f32[200,128]{1,0:T(8,128)S(1)}, f32[200,128]{1,0:T(8,128)S(1)}, u32[]{:S(2)}, u32[]{:S(2)}) collective-permute-start(f32[200,128]{1,0:T(8,128)S(1)} %get-tuple-element.37.refs_2_.refs_16_), channel_id=1, source_target_pairs={{0,16},{4,20},{8,24},{12,28},{16,0},{20,4},{24,8},{28,12},{1,17},{... | collective-permute-start | bytes 307208 | tf_op jit(solution)/shard_map/ppermute | solution.py:370
  13.8 5.8 %collective-permute-start.10 = (f32[200,128]{1,0:T(8,128)S(1)}, f32[200,128]{1,0:T(8,128)S(1)}, u32[]{:S(2)}, u32[]{:S(2)}) collective-permute-start(f32[200,128]{1,0:T(8,128)S(1)} %get-tuple-element.37.refs_2_.refs_16_), channel_id=1, source_target_pairs={{0,8},{4,12},{8,0},{12,4},{16,24},{20,28},{24,16},{28,20},{1,9},{5... | collective-permute-start | bytes 307208 | tf_op jit(solution)/shard_map/ppermute | solution.py:370
  15.3 7.1 %collective-permute-start.5 = (f32[232,128]{1,0:T(8,128)S(1)}, f32[232,128]{1,0:T(8,128)S(1)}, u32[]{:S(2)}, u32[]{:S(2)}) collective-permute-start(f32[232,128]{1,0:T(8,128)S(1)} %constant_dynamic-update-slice_fusion.refs_8_.refs_1_), channel_id=1, source_target_pairs={{0,24},{4,28},{8,16},{12,20},{16,8},{20,12},{24,0},{28,4},{1,25},{... | collective-permute-start | bytes 356360 | tf_op jit(solution)/shard_map/ppermute | solution.py:370
  16.3 6.8 %collective-permute-start.4 = (f32[232,128]{1,0:T(8,128)S(1)}, f32[232,128]{1,0:T(8,128)S(1)}, u32[]{:S(2)}, u32[]{:S(2)}) collective-permute-start(f32[232,128]{1,0:T(8,128)S(1)} %constant_dynamic-update-slice_fusion.refs_8_.refs_1_), channel_id=1, source_target_pairs={{0,16},{4,20},{8,24},{12,28},{16,0},{20,4},{24,8},{28,12},{1,17},{... | collective-permute-start | bytes 356360 | tf_op jit(solution)/shard_map/ppermute | solution.py:370
  17.4 5.8 %collective-permute-start.3 = (f32[232,128]{1,0:T(8,128)S(1)}, f32[232,128]{1,0:T(8,128)S(1)}, u32[]{:S(2)}, u32[]{:S(2)}) collective-permute-start(f32[232,128]{1,0:T(8,128)S(1)} %constant_dynamic-update-slice_fusion.refs_8_.refs_1_), channel_id=1, source_target_pairs={{0,8},{4,12},{8,0},{12,4},{16,24},{20,28},{24,16},{28,20},{1,9},{5... | collective-permute-start | bytes 356360 | tf_op jit(solution)/shard_map/ppermute | solution.py:370
  18.9 4.7 %collective-permute-start.16 = (f32[200,128]{1,0:T(8,128)S(1)}, f32[200,128]{1,0:T(8,128)S(1)}, u32[]{:S(2)}, u32[]{:S(2)}) collective-permute-start(f32[200,128]{1,0:T(8,128)S(1)} %collective-permute-done.12.refs_5_.refs_19_), channel_id=1, source_target_pairs={{0,4},{4,0},{8,12},{12,8},{16,20},{20,16},{24,28},{28,24},{1,5},{5... | collective-permute-start | bytes 307208 | tf_op jit(solution)/shard_map/ppermute | solution.py:370
  19.6 4.1 %collective-permute-start.15 = (f32[200,128]{1,0:T(8,128)S(1)}, f32[200,128]{1,0:T(8,128)S(1)}, u32[]{:S(2)}, u32[]{:S(2)}) collective-permute-start(f32[200,128]{1,0:T(8,128)S(1)} %collective-permute-done.11.refs_4_.refs_18_), channel_id=1, source_target_pairs={{0,4},{4,0},{8,12},{12,8},{16,20},{20,16},{24,28},{28,24},{1,5},{5... | collective-permute-start | bytes 307208 | tf_op jit(solution)/shard_map/ppermute | solution.py:370
  22.5 3.5 %collective-permute-start.6 = (f32[232,128]{1,0:T(8,128)S(1)}, f32[232,128]{1,0:T(8,128)S(1)}, u32[]{:S(2)}, u32[]{:S(2)}) collective-permute-start(f32[232,128]{1,0:T(8,128)S(1)} %constant_dynamic-update-slice_fusion.refs_8_.refs_1_), channel_id=1, source_target_pairs={{0,4},{4,0},{8,12},{12,8},{16,20},{20,16},{24,28},{28,24},{1,5},{5... | collective-permute-start | bytes 356360 | tf_op jit(solution)/shard_map/ppermute | solution.py:370
  23.1 2.9 %collective-permute-start.9 = (f32[232,128]{1,0:T(8,128)S(1)}, f32[232,128]{1,0:T(8,128)S(1)}, u32[]{:S(2)}, u32[]{:S(2)}) collective-permute-start(f32[232,128]{1,0:T(8,128)S(1)} %collective-permute-done.5.refs_11_.refs_4_), channel_id=1, source_target_pairs={{0,4},{4,0},{8,12},{12,8},{16,20},{20,16},{24,28},{28,24},{1,5},{5... | collective-permute-start | bytes 356360 | tf_op jit(solution)/shard_map/ppermute | solution.py:370
  23.2 2.8 %collective-permute-start.8 = (f32[232,128]{1,0:T(8,128)S(1)}, f32[232,128]{1,0:T(8,128)S(1)}, u32[]{:S(2)}, u32[]{:S(2)}) collective-permute-start(f32[232,128]{1,0:T(8,128)S(1)} %collective-permute-done.4.refs_10_.refs_3_), channel_id=1, source_target_pairs={{0,4},{4,0},{8,12},{12,8},{16,20},{20,16},{24,28},{28,24},{1,5},{5... | collective-permute-start | bytes 356360 | tf_op jit(solution)/shard_map/ppermute | solution.py:370
  23.6 2.4 %collective-permute-start.7 = (f32[232,128]{1,0:T(8,128)S(1)}, f32[232,128]{1,0:T(8,128)S(1)}, u32[]{:S(2)}, u32[]{:S(2)}) collective-permute-start(f32[232,128]{1,0:T(8,128)S(1)} %collective-permute-done.3.refs_9_.refs_2_), channel_id=1, source_target_pairs={{0,4},{4,0},{8,12},{12,8},{16,20},{20,16},{24,28},{28,24},{1,5},{5... | collective-permute-start | bytes 356360 | tf_op jit(solution)/shard_map/ppermute | solution.py:370
  23.7 1.4 %collective-permute-start.14 = (f32[200,128]{1,0:T(8,128)S(1)}, f32[200,128]{1,0:T(8,128)S(1)}, u32[]{:S(2)}, u32[]{:S(2)}) collective-permute-start(f32[200,128]{1,0:T(8,128)S(1)} %collective-permute-done.10.refs_3_.refs_17_), channel_id=1, source_target_pairs={{0,4},{4,0},{8,12},{12,8},{16,20},{20,16},{24,28},{28,24},{1,5},{5... | collective-permute-start | bytes 307208 | tf_op jit(solution)/shard_map/ppermute | solution.py:370
  28.8 8.3 %collective-permute-start.19 = (f32[24,128]{1,0:T(8,128)S(1)}, f32[24,128]{1,0:T(8,128)S(1)}, u32[]{:S(2)}, u32[]{:S(2)}) collective-permute-start(f32[24,128]{1,0:T(8,128)S(1)} %get-tuple-element.46), channel_id=1, source_target_pairs={{0,3},{1,2},{2,1},{3,0},{4,7},{5,6},{6,5},{7,4},{8,11},{9,10},{10,... | collective-permute-start | bytes 36872 | tf_op jit(solution)/shard_map/ppermute | solution.py:370
  32.5 4.6 %collective-permute-start.18 = (f32[24,128]{1,0:T(8,128)S(1)}, f32[24,128]{1,0:T(8,128)S(1)}, u32[]{:S(2)}, u32[]{:S(2)}) collective-permute-start(f32[24,128]{1,0:T(8,128)S(1)} %get-tuple-element.46), channel_id=1, source_target_pairs={{0,2},{1,3},{2,0},{3,1},{4,6},{5,7},{6,4},{7,5},{8,10},{9,11},{10,... | collective-permute-start | bytes 36872 | tf_op jit(solution)/shard_map/ppermute | solution.py:370
  32.5 3.8 %collective-permute-start.17 = (f32[24,128]{1,0:T(8,128)S(1)}, f32[24,128]{1,0:T(8,128)S(1)}, u32[]{:S(2)}, u32[]{:S(2)}) collective-permute-start(f32[24,128]{1,0:T(8,128)S(1)} %get-tuple-element.46), channel_id=1, source_target_pairs={{0,1},{1,0},{2,3},{3,2},{4,5},{5,4},{6,7},{7,6},{8,9},{9,8},{10,11... | collective-permute-start | bytes 36872 | tf_op jit(solution)/shard_map/ppermute | solution.py:370
  37.1 6.3 %collective-permute-start.22 = (f32[168,128]{1,0:T(8,128)S(1)}, f32[168,128]{1,0:T(8,128)S(1)}, u32[]{:S(2)}, u32[]{:S(2)}) collective-permute-start(f32[168,128]{1,0:T(8,128)S(1)} %constant_dynamic-update-slice_fusion.5.refs_7_.refs_1_), channel_id=1, source_target_pairs={{0,24},{4,28},{8,16},{12,20},{16,8},{20,12},{24,0},{28,4},{1,25},{... | collective-permute-start | bytes 258056 | tf_op jit(solution)/shard_map/ppermute | solution.py:370
  39.3 4.8 %collective-permute-start.21 = (f32[168,128]{1,0:T(8,128)S(1)}, f32[168,128]{1,0:T(8,128)S(1)}, u32[]{:S(2)}, u32[]{:S(2)}) collective-permute-start(f32[168,128]{1,0:T(8,128)S(1)} %constant_dynamic-update-slice_fusion.5.refs_7_.refs_1_), channel_id=1, source_target_pairs={{0,16},{4,20},{8,24},{12,28},{16,0},{20,4},{24,8},{28,12},{1,17},{... | collective-permute-start | bytes 258056 | tf_op jit(solution)/shard_map/ppermute | solution.py:370
  39.8 4.5 %collective-permute-start.20 = (f32[168,128]{1,0:T(8,128)S(1)}, f32[168,128]{1,0:T(8,128)S(1)}, u32[]{:S(2)}, u32[]{:S(2)}) collective-permute-start(f32[168,128]{1,0:T(8,128)S(1)} %constant_dynamic-update-slice_fusion.5.refs_7_.refs_1_), channel_id=1, source_target_pairs={{0,8},{4,12},{8,0},{12,4},{16,24},{20,28},{24,16},{28,20},{1,9},{5... | collective-permute-start | bytes 258056 | tf_op jit(solution)/shard_map/ppermute | solution.py:370
  40.6 3.9 %collective-permute-start.23 = (f32[168,128]{1,0:T(8,128)S(1)}, f32[168,128]{1,0:T(8,128)S(1)}, u32[]{:S(2)}, u32[]{:S(2)}) collective-permute-start(f32[168,128]{1,0:T(8,128)S(1)} %constant_dynamic-update-slice_fusion.5.refs_7_.refs_1_), channel_id=1, source_target_pairs={{0,4},{4,0},{8,12},{12,8},{16,20},{20,16},{24,28},{28,24},{1,5},{5... | collective-permute-start | bytes 258056 | tf_op jit(solution)/shard_map/ppermute | solution.py:370
  43.4 1.3 %collective-permute-start.26 = (f32[168,128]{1,0:T(8,128)S(1)}, f32[168,128]{1,0:T(8,128)S(1)}, u32[]{:S(2)}, u32[]{:S(2)}) collective-permute-start(f32[168,128]{1,0:T(8,128)S(1)} %collective-permute-done.22.refs_10_.refs_4_), channel_id=1, source_target_pairs={{0,4},{4,0},{8,12},{12,8},{16,20},{20,16},{24,28},{28,24},{1,5},{5... | collective-permute-start | bytes 258056 | tf_op jit(solution)/shard_map/ppermute | solution.py:370
  44.0 1.3 %collective-permute-start.25 = (f32[168,128]{1,0:T(8,128)S(1)}, f32[168,128]{1,0:T(8,128)S(1)}, u32[]{:S(2)}, u32[]{:S(2)}) collective-permute-start(f32[168,128]{1,0:T(8,128)S(1)} %collective-permute-done.21.refs_9_.refs_3_), channel_id=1, source_target_pairs={{0,4},{4,0},{8,12},{12,8},{16,20},{20,16},{24,28},{28,24},{1,5},{5... | collective-permute-start | bytes 258056 | tf_op jit(solution)/shard_map/ppermute | solution.py:370
  44.3 1.3 %collective-permute-start.24 = (f32[168,128]{1,0:T(8,128)S(1)}, f32[168,128]{1,0:T(8,128)S(1)}, u32[]{:S(2)}, u32[]{:S(2)}) collective-permute-start(f32[168,128]{1,0:T(8,128)S(1)} %collective-permute-done.20.refs_8_.refs_2_), channel_id=1, source_target_pairs={{0,4},{4,0},{8,12},{12,8},{16,20},{20,16},{24,28},{28,24},{1,5},{5... | collective-permute-start | bytes 258056 | tf_op jit(solution)/shard_map/ppermute | solution.py:370
  47.6 6.3 %collective-permute-start.29 = (f32[24,128]{1,0:T(8,128)S(1)}, f32[24,128]{1,0:T(8,128)S(1)}, u32[]{:S(2)}, u32[]{:S(2)}) collective-permute-start(f32[24,128]{1,0:T(8,128)S(1)} %get-tuple-element.56), channel_id=1, source_target_pairs={{0,3},{1,2},{2,1},{3,0},{4,7},{5,6},{6,5},{7,4},{8,11},{9,10},{10,... | collective-permute-start | bytes 36872 | tf_op jit(solution)/shard_map/ppermute | solution.py:370
  49.1 4.7 %collective-permute-start.28 = (f32[24,128]{1,0:T(8,128)S(1)}, f32[24,128]{1,0:T(8,128)S(1)}, u32[]{:S(2)}, u32[]{:S(2)}) collective-permute-start(f32[24,128]{1,0:T(8,128)S(1)} %get-tuple-element.56), channel_id=1, source_target_pairs={{0,2},{1,3},{2,0},{3,1},{4,6},{5,7},{6,4},{7,5},{8,10},{9,11},{10,... | collective-permute-start | bytes 36872 | tf_op jit(solution)/shard_map/ppermute | solution.py:370
  49.8 4.1 %collective-permute-start.27 = (f32[24,128]{1,0:T(8,128)S(1)}, f32[24,128]{1,0:T(8,128)S(1)}, u32[]{:S(2)}, u32[]{:S(2)}) collective-permute-start(f32[24,128]{1,0:T(8,128)S(1)} %get-tuple-element.56), channel_id=1, source_target_pairs={{0,1},{1,0},{2,3},{3,2},{4,5},{5,4},{6,7},{7,6},{8,9},{9,8},{10,11... | collective-permute-start | bytes 36872 | tf_op jit(solution)/shard_map/ppermute | solution.py:370
  53.9 6.1 %collective-permute-start.32 = (f32[168,128]{1,0:T(8,128)S(1)}, f32[168,128]{1,0:T(8,128)S(1)}, u32[]{:S(2)}, u32[]{:S(2)}) collective-permute-start(f32[168,128]{1,0:T(8,128)S(1)} %constant_dynamic-update-slice_fusion.10.refs_7_), channel_id=1, source_target_pairs={{0,24},{4,28},{8,16},{12,20},{16,8},{20,12},{24,0},{28,4},{1,25},{... | collective-permute-start | bytes 258056 | tf_op jit(solution)/shard_map/ppermute | solution.py:370
  55.5 5.1 %collective-permute-start.31 = (f32[168,128]{1,0:T(8,128)S(1)}, f32[168,128]{1,0:T(8,128)S(1)}, u32[]{:S(2)}, u32[]{:S(2)}) collective-permute-start(f32[168,128]{1,0:T(8,128)S(1)} %constant_dynamic-update-slice_fusion.10.refs_7_), channel_id=1, source_target_pairs={{0,16},{4,20},{8,24},{12,28},{16,0},{20,4},{24,8},{28,12},{1,17},{... | collective-permute-start | bytes 258056 | tf_op jit(solution)/shard_map/ppermute | solution.py:370
  56.3 4.5 %collective-permute-start.30 = (f32[168,128]{1,0:T(8,128)S(1)}, f32[168,128]{1,0:T(8,128)S(1)}, u32[]{:S(2)}, u32[]{:S(2)}) collective-permute-start(f32[168,128]{1,0:T(8,128)S(1)} %constant_dynamic-update-slice_fusion.10.refs_7_), channel_id=1, source_target_pairs={{0,8},{4,12},{8,0},{12,4},{16,24},{20,28},{24,16},{28,20},{1,9},{5... | collective-permute-start | bytes 258056 | tf_op jit(solution)/shard_map/ppermute | solution.py:370
  57.4 3.7 %collective-permute-start.33 = (f32[168,128]{1,0:T(8,128)S(1)}, f32[168,128]{1,0:T(8,128)S(1)}, u32[]{:S(2)}, u32[]{:S(2)}) collective-permute-start(f32[168,128]{1,0:T(8,128)S(1)} %constant_dynamic-update-slice_fusion.10.refs_7_), channel_id=1, source_target_pairs={{0,4},{4,0},{8,12},{12,8},{16,20},{20,16},{24,28},{28,24},{1,5},{5... | collective-permute-start | bytes 258056 | tf_op jit(solution)/shard_map/ppermute | solution.py:370
  60.0 1.3 %collective-permute-start.36 = (f32[168,128]{1,0:T(8,128)S(1)}, f32[168,128]{1,0:T(8,128)S(1)}, u32[]{:S(2)}, u32[]{:S(2)}) collective-permute-start(f32[168,128]{1,0:T(8,128)S(1)} %collective-permute-done.32.refs_10_), channel_id=1, source_target_pairs={{0,4},{4,0},{8,12},{12,8},{16,20},{20,16},{24,28},{28,24},{1,5},{5... | collective-permute-start | bytes 258056 | tf_op jit(solution)/shard_map/ppermute | solution.py:370
  60.6 1.3 %collective-permute-start.35 = (f32[168,128]{1,0:T(8,128)S(1)}, f32[168,128]{1,0:T(8,128)S(1)}, u32[]{:S(2)}, u32[]{:S(2)}) collective-permute-start(f32[168,128]{1,0:T(8,128)S(1)} %collective-permute-done.31.refs_9_), channel_id=1, source_target_pairs={{0,4},{4,0},{8,12},{12,8},{16,20},{20,16},{24,28},{28,24},{1,5},{5... | collective-permute-start | bytes 258056 | tf_op jit(solution)/shard_map/ppermute | solution.py:370
  60.7 1.3 %collective-permute-start.34 = (f32[168,128]{1,0:T(8,128)S(1)}, f32[168,128]{1,0:T(8,128)S(1)}, u32[]{:S(2)}, u32[]{:S(2)}) collective-permute-start(f32[168,128]{1,0:T(8,128)S(1)} %collective-permute-done.30.refs_8_), channel_id=1, source_target_pairs={{0,4},{4,0},{8,12},{12,8},{16,20},{20,16},{24,28},{28,24},{1,5},{5... | collective-permute-start | bytes 258056 | tf_op jit(solution)/shard_map/ppermute | solution.py:370

commit v3 on v2

--- a/solution.py
+++ b/solution.py
@@ -90,9 +90,10 @@
         match = [keys == ids[slot * tiles + t : slot * tiles + t + 1, :] for t in range(tiles)]
         match = match[0] if tiles == 1 else jnp.concatenate(match, axis=1)
         match = jnp.where(match[:, :count], 1.0, 0.0).astype(jnp.bfloat16)
-        for part in split_bf16(values, split):
-            term = jnp.dot(match, part, preferred_element_type=jnp.float32)
-            image = term if image is None else image + term
+        term = jnp.dot(match, jnp.concatenate(split_bf16(values, split), axis=1), preferred_element_type=jnp.float32)
+        image = term if image is None else image + term
+    width = keys.shape[1]
+    image = sum(image[:, i * width : (i + 1) * width] for i in range(split))
     return image
 
 

time: 65.1 us -> 64.5 us (level)
  Pallas kernels: 13.1 us -> 12.3 us
    pallas_call x9, Pallas kernels: 13.1 us -> 12.3 us  [call(): pl.pallas_call(kernel, out_shape=[shape(*s) for s in outs], in_specs=spec...]
  transfers between devices with their start and end apart: 37 -> 37, of which waited for: 20 -> 20; matrix products, arithmetic and copies ran while one was open for 0% -> 0% of each run, Pallas kernels for 7% -> 6%
where the time goes in v3:
time: 64.5 us; the launch traced here: 64.2 us
  starting transfers between devices  32.2 us (50%)
  waiting for transfers between devices  17.3 us (27%)
  Pallas kernels  12.3 us (19%)
  local copies, waits for them, and re-layouts  1.43 us (2%)
  between operations  1 us (2%)
    ppermute x37, starting transfers between devices, swap(): return lax.ppermute(value, axis, [(i, i ^ mask) for i in range(count)])  32.2 us
    ppermute x37, waiting for transfers between devices, swap(): return lax.ppermute(value, axis, [(i, i ^ mask) for i in range(count)])  17.3 us
    pallas_call x9, Pallas kernels, call(): pl.pallas_call(kernel, out_shape=[shape(*s) for s in outs], in_specs=spec...  12.3 us
    unnamed x42, local copies, waits for them, and re-layouts  1.43 us
  transfers between devices with their start and end apart: 37, of which 20 were waited for; matrix products, arithmetic and copies ran while one was open for 0% of the time, Pallas kernels for 6%

profile of v3, /device:TPU:0, one launch (start us, length us, event | category | flops | bytes accessed | tf_op | source)
XLA Modules:
  0.0 64.2 jit_solution(963358283100212295)
XLA Ops:
  0.8 0.0 copy-start.7
  0.8 0.6 copy-done.5
  1.4 0.0 copy-done.4
  1.4 0.1 copy-done.3
  1.4 0.0 copy-done.2
  1.4 0.7 %copy-done.1 = f32[24,128,128]{2,1,0:T(8,128)S(1)} copy-done((f32[24,128,128]{2,1,0:T(8,128)S(1)}, f32[24,128,128]{2,1,0:T(8,128)}, u32[]{:S(2)}) %copy-start.1) | copy-done | bytes 1572888
  2.2 1.2 %shard_map.167 = (f32[40,128]{1,0:T(8,128)S(1)}, f32[16,128,128]{2,1,0:T(8,128)S(1)}, f32[200,128]{1,0:T(8,128)S(1)}, s32[72,128]{1,0:T(8,128)S(1)}, s32[24,128]{1,0:T(8,128)S(1)}) custom-call(s32[24]{0:T(128)S(1)} %copy-done.11, s32[24]{0:T(128)S(1)} %copy-done.14, s32[72]{0:T(128)S(1)} %bitcast.1, s32[72]{0:T(128)S(1)} %copy-done.13, s32[72]{0:T(128)S(1)} %copy-done.10, ...), custom_call_target="tpu_custom_call" | custom-call | flops 786432 | tf_op jit(solution)/shard_map/pallas_call | solution.py:329
  3.4 5.1 %collective-permute-start.2 = (f32[40,128]{1,0:T(8,128)S(1)}, f32[40,128]{1,0:T(8,128)S(1)}, u32[]{:S(2)}, u32[]{:S(2)}) collective-permute-start(f32[40,128]{1,0:T(8,128)S(1)} %get-tuple-element.36), channel_id=1, source_target_pairs={{0,3},{1,2},{2,1},{3,0},{4,7},{5,6},{6,5},{7,4},{8,11},{9,10},{10,... | collective-permute-start | bytes 61448 | tf_op jit(solution)/shard_map/ppermute | solution.py:371
  8.5 0.6 collective-permute-start
  9.2 2.6 %collective-permute-start.12 = (f32[200,128]{1,0:T(8,128)S(1)}, f32[200,128]{1,0:T(8,128)S(1)}, u32[]{:S(2)}, u32[]{:S(2)}) collective-permute-start(f32[200,128]{1,0:T(8,128)S(1)} %get-tuple-element.37.refs_2_.refs_16_), channel_id=1, source_target_pairs={{0,24},{4,28},{8,16},{12,20},{16,8},{20,12},{24,0},{28,4},{1,25},{... | collective-permute-start | bytes 307208 | tf_op jit(solution)/shard_map/ppermute | solution.py:371
  11.8 0.8 %shard_map.168 = f32[72,128]{1,0:T(8,128)S(1)} custom-call(s32[72,128]{1,0:T(8,128)S(1)} %get-tuple-element.34.rows, f32[72,128,128]{2,1,0:T(8,128)S(1)} %copy-done, f32[16,128,128]{2,1,0:T(8,128)S(1)} %get-tuple-element.35.wide), custom_call_target="tpu_custom_call" | custom-call | flops 2359296 | tf_op jit(solution)/shard_map/pallas_call | solution.py:329
  12.6 0.0 collective-permute-done
  12.6 1.2 %collective-permute-start.11 = (f32[200,128]{1,0:T(8,128)S(1)}, f32[200,128]{1,0:T(8,128)S(1)}, u32[]{:S(2)}, u32[]{:S(2)}) collective-permute-start(f32[200,128]{1,0:T(8,128)S(1)} %get-tuple-element.37.refs_2_.refs_16_), channel_id=1, source_target_pairs={{0,16},{4,20},{8,24},{12,28},{16,0},{20,4},{24,8},{28,12},{1,17},{... | collective-permute-start | bytes 307208 | tf_op jit(solution)/shard_map/ppermute | solution.py:371
  13.8 0.0 collective-permute-done.1
  13.8 1.5 %collective-permute-start.10 = (f32[200,128]{1,0:T(8,128)S(1)}, f32[200,128]{1,0:T(8,128)S(1)}, u32[]{:S(2)}, u32[]{:S(2)}) collective-permute-start(f32[200,128]{1,0:T(8,128)S(1)} %get-tuple-element.37.refs_2_.refs_16_), channel_id=1, source_target_pairs={{0,8},{4,12},{8,0},{12,4},{16,24},{20,28},{24,16},{28,20},{1,9},{5... | collective-permute-start | bytes 307208 | tf_op jit(solution)/shard_map/ppermute | solution.py:371
  15.3 0.0 collective-permute-done.2
  15.3 0.9 %collective-permute-start.5 = (f32[232,128]{1,0:T(8,128)S(1)}, f32[232,128]{1,0:T(8,128)S(1)}, u32[]{:S(2)}, u32[]{:S(2)}) collective-permute-start(f32[232,128]{1,0:T(8,128)S(1)} %constant_dynamic-update-slice_fusion.refs_8_.refs_1_), channel_id=1, source_target_pairs={{0,24},{4,28},{8,16},{12,20},{16,8},{20,12},{24,0},{28,4},{1,25},{... | collective-permute-start | bytes 356360 | tf_op jit(solution)/shard_map/ppermute | solution.py:371
  16.3 0.0 collective-permute-done.13.refs_6_.refs_20_
  16.3 1.1 %collective-permute-start.4 = (f32[232,128]{1,0:T(8,128)S(1)}, f32[232,128]{1,0:T(8,128)S(1)}, u32[]{:S(2)}, u32[]{:S(2)}) collective-permute-start(f32[232,128]{1,0:T(8,128)S(1)} %constant_dynamic-update-slice_fusion.refs_8_.refs_1_), channel_id=1, source_target_pairs={{0,16},{4,20},{8,24},{12,28},{16,0},{20,4},{24,8},{28,12},{1,17},{... | collective-permute-start | bytes 356360 | tf_op jit(solution)/shard_map/ppermute | solution.py:371
  17.4 1.5 %collective-permute-start.3 = (f32[232,128]{1,0:T(8,128)S(1)}, f32[232,128]{1,0:T(8,128)S(1)}, u32[]{:S(2)}, u32[]{:S(2)}) collective-permute-start(f32[232,128]{1,0:T(8,128)S(1)} %constant_dynamic-update-slice_fusion.refs_8_.refs_1_), channel_id=1, source_target_pairs={{0,8},{4,12},{8,0},{12,4},{16,24},{20,28},{24,16},{28,20},{1,9},{5... | collective-permute-start | bytes 356360 | tf_op jit(solution)/shard_map/ppermute | solution.py:371
  18.9 0.0 collective-permute-done.11.refs_4_.refs_18_
  18.9 0.0 collective-permute-start.16
  18.9 0.7 %collective-permute-done.10.refs_3_.refs_17_ = f32[200,128]{1,0:T(8,128)S(1)} collective-permute-done((f32[200,128]{1,0:T(8,128)S(1)}, f32[200,128]{1,0:T(8,128)S(1)}, u32[]{:S(2)}, u32[]{:S(2)}) %collective-permute-start.10) | collective-permute-done | bytes 102432 | tf_op jit(solution)/shard_map/ppermute | solution.py:371
  19.6 2.9 %collective-permute-done.5.refs_11_.refs_4_ = f32[232,128]{1,0:T(8,128)S(1)} collective-permute-done((f32[232,128]{1,0:T(8,128)S(1)}, f32[232,128]{1,0:T(8,128)S(1)}, u32[]{:S(2)}, u32[]{:S(2)}) %collective-permute-start.5) | collective-permute-done | bytes 118816 | tf_op jit(solution)/shard_map/ppermute | solution.py:371
  22.5 0.6 %collective-permute-done.4.refs_10_.refs_3_ = f32[232,128]{1,0:T(8,128)S(1)} collective-permute-done((f32[232,128]{1,0:T(8,128)S(1)}, f32[232,128]{1,0:T(8,128)S(1)}, u32[]{:S(2)}, u32[]{:S(2)}) %collective-permute-start.4) | collective-permute-done | bytes 118816 | tf_op jit(solution)/shard_map/ppermute | solution.py:371
  23.1 0.1 collective-permute-done.3.refs_9_.refs_2_
  23.2 0.4 collective-permute-start.8
  23.6 0.1 collective-permute-start.7
  23.7 0.4 collective-permute-start.14
  24.1 1.0 %collective-permute-done.14.refs_7_.refs_21_ = f32[200,128]{1,0:T(8,128)S(1)} collective-permute-done((f32[200,128]{1,0:T(8,128)S(1)}, f32[200,128]{1,0:T(8,128)S(1)}, u32[]{:S(2)}, u32[]{:S(2)}) %collective-permute-start.14) | collective-permute-done | bytes 102432 | tf_op jit(solution)/shard_map/ppermute | solution.py:371
  25.1 0.9 %shard_map.169 = (f32[72,128]{1,0:T(8,128)S(1)}, f32[72,128]{1,0:T(8,128)S(1)}, f32[72,128]{1,0:T(8,128)S(1)}, f32[72,128]{1,0:T(8,128)S(1)}) custom-call(s32[72]{0:T(128)S(1)} %bitcast.2, s32[72]{0:T(128)S(1)} %copy-done.13, f32[200,128]{1,0:T(8,128)S(1)} %get-tuple-element.37.refs_2_.refs_16_, f32[200,128]{1,0:T(8,128)S(1)} %collective-permute-done.10.refs_3_.refs_17_, ...), custom_call_target="tpu_custom_call" | custom-call | flops 73728 | tf_op jit(solution)/shard_map/pallas_call | solution.py:329
  26.0 2.7 %shard_map.170 = (f32[16,128]{1,0:T(8,128)S(1)}, f32[24,128]{1,0:T(8,128)S(1)}, f32[16,128,128]{2,1,0:T(8,128)S(1)}, f32[96,128]{1,0:T(8,128)S(1)}, f32[96,128]{...) custom-call(s32[72]{0:T(128)S(1)} %copy-done.10, s32[24]{0:T(128)S(1)} %copy-done.11, ...), custom_call_target="tpu_custom_call" | custom-call | flops 3145728 | tf_op jit(solution)/shard_map/pallas_call | solution.py:329
  28.7 3.7 %collective-permute-start.19 = (f32[24,128]{1,0:T(8,128)S(1)}, f32[24,128]{1,0:T(8,128)S(1)}, u32[]{:S(2)}, u32[]{:S(2)}) collective-permute-start(f32[24,128]{1,0:T(8,128)S(1)} %get-tuple-element.46), channel_id=1, source_target_pairs={{0,3},{1,2},{2,1},{3,0},{4,7},{5,6},{6,5},{7,4},{8,11},{9,10},{10,... | collective-permute-start | bytes 36872 | tf_op jit(solution)/shard_map/ppermute | solution.py:371
  32.4 0.8 %collective-permute-start.17 = (f32[24,128]{1,0:T(8,128)S(1)}, f32[24,128]{1,0:T(8,128)S(1)}, u32[]{:S(2)}, u32[]{:S(2)}) collective-permute-start(f32[24,128]{1,0:T(8,128)S(1)} %get-tuple-element.46), channel_id=1, source_target_pairs={{0,1},{1,0},{2,3},{3,2},{4,5},{5,4},{6,7},{7,6},{8,9},{9,8},{10,11... | collective-permute-start | bytes 36872 | tf_op jit(solution)/shard_map/ppermute | solution.py:371
  33.1 1.2 %shard_map.171 = (f32[72,128]{1,0:T(8,128)S(1)}, f32[64,128]{1,0:T(8,128)S(1)}, f32[32,128]{1,0:T(8,128)S(1)}) custom-call(s32[72,128]{1,0:T(8,128)S(1)} %get-tuple-element.34.rows, f32[72,128,128]{2,1,0:T(8,128)S(1)} %copy-done, f32[16,128,128]{2,1,0:T(8,128)S(1)} %get-tuple-element.43.wide, f32[16,128]{1,0:T(8,128)S(1)} %get-tuple-element.44.refs_0_.refs_19_, ...), custom_call_target="tpu_custom_call" | custom-call | flops 2359296 | tf_op jit(solution)/shard_map/pallas_call | solution.py:329
  34.4 1.8 %collective-permute-done.17 = f32[24,128]{1,0:T(8,128)S(1)} collective-permute-done((f32[24,128]{1,0:T(8,128)S(1)}, f32[24,128]{1,0:T(8,128)S(1)}, u32[]{:S(2)}, u32[]{:S(2)}) %collective-permute-start.17) | collective-permute-done | bytes 12320 | tf_op jit(solution)/shard_map/ppermute | solution.py:371
  36.2 0.8 %collective-permute-done.18 = f32[24,128]{1,0:T(8,128)S(1)} collective-permute-done((f32[24,128]{1,0:T(8,128)S(1)}, f32[24,128]{1,0:T(8,128)S(1)}, u32[]{:S(2)}, u32[]{:S(2)}) %collective-permute-start.18) | collective-permute-done | bytes 12320 | tf_op jit(solution)/shard_map/ppermute | solution.py:371
  37.0 2.2 %collective-permute-start.22 = (f32[168,128]{1,0:T(8,128)S(1)}, f32[168,128]{1,0:T(8,128)S(1)}, u32[]{:S(2)}, u32[]{:S(2)}) collective-permute-start(f32[168,128]{1,0:T(8,128)S(1)} %constant_dynamic-update-slice_fusion.5.refs_7_.refs_1_), channel_id=1, source_target_pairs={{0,24},{4,28},{8,16},{12,20},{16,8},{20,12},{24,0},{28,4},{1,25},{... | collective-permute-start | bytes 258056 | tf_op jit(solution)/shard_map/ppermute | solution.py:371
  39.2 0.5 collective-permute-start.21
  39.7 0.9 %collective-permute-start.20 = (f32[168,128]{1,0:T(8,128)S(1)}, f32[168,128]{1,0:T(8,128)S(1)}, u32[]{:S(2)}, u32[]{:S(2)}) collective-permute-start(f32[168,128]{1,0:T(8,128)S(1)} %constant_dynamic-update-slice_fusion.5.refs_7_.refs_1_), channel_id=1, source_target_pairs={{0,8},{4,12},{8,0},{12,4},{16,24},{20,28},{24,16},{28,20},{1,9},{5... | collective-permute-start | bytes 258056 | tf_op jit(solution)/shard_map/ppermute | solution.py:371
  40.5 2.7 %collective-permute-done.22.refs_10_.refs_4_ = f32[168,128]{1,0:T(8,128)S(1)} collective-permute-done((f32[168,128]{1,0:T(8,128)S(1)}, f32[168,128]{1,0:T(8,128)S(1)}, u32[]{:S(2)}, u32[]{:S(2)}) %collective-permute-start.22) | collective-permute-done | bytes 86048 | tf_op jit(solution)/shard_map/ppermute | solution.py:371
  43.3 0.6 collective-permute-done.21.refs_9_.refs_3_
  43.9 0.2 collective-permute-done.20.refs_8_.refs_2_
  44.1 0.3 collective-permute-start.24
  44.4 0.1 collective-permute-done.26.refs_14_.refs_8_
  44.6 0.6 collective-permute-done.25.refs_13_.refs_7_
  45.2 0.2 collective-permute-done.24.refs_12_.refs_6_
  45.4 1.9 %shard_map.172 = (f32[16,128]{1,0:T(8,128)S(1)}, f32[24,128]{1,0:T(8,128)S(1)}, f32[16,128,128]{2,1,0:T(8,128)S(1)}, f32[96,128]{1,0:T(8,128)S(1)}) custom-call(s32[72]{0:T(128)S(1)} %copy-done.10, s32[24]{0:T(128)S(1)} %copy-done.11, s32[24,128]{1,0:T(8,128)S(1)} %get-tuple-element.33.refs_3_.refs_2_, f32[72,128,128]{2,1,0:T(8,128)S(1)} %copy-done, ...), custom_call_target="tpu_custom_call" | custom-call | flops 3145728 | tf_op jit(solution)/shard_map/pallas_call | solution.py:329
  47.4 1.5 %collective-permute-start.29 = (f32[24,128]{1,0:T(8,128)S(1)}, f32[24,128]{1,0:T(8,128)S(1)}, u32[]{:S(2)}, u32[]{:S(2)}) collective-permute-start(f32[24,128]{1,0:T(8,128)S(1)} %get-tuple-element.56), channel_id=1, source_target_pairs={{0,3},{1,2},{2,1},{3,0},{4,7},{5,6},{6,5},{7,4},{8,11},{9,10},{10,... | collective-permute-start | bytes 36872 | tf_op jit(solution)/shard_map/ppermute | solution.py:371
  48.9 0.6 collective-permute-start.28
  49.5 2.3 %collective-permute-start.27 = (f32[24,128]{1,0:T(8,128)S(1)}, f32[24,128]{1,0:T(8,128)S(1)}, u32[]{:S(2)}, u32[]{:S(2)}) collective-permute-start(f32[24,128]{1,0:T(8,128)S(1)} %get-tuple-element.56), channel_id=1, source_target_pairs={{0,1},{1,0},{2,3},{3,2},{4,5},{5,4},{6,7},{7,6},{8,9},{9,8},{10,11... | collective-permute-start | bytes 36872 | tf_op jit(solution)/shard_map/ppermute | solution.py:371
  51.8 1.2 %shard_map.173 = (f32[72,128]{1,0:T(8,128)S(1)}, f32[64,128]{1,0:T(8,128)S(1)}, f32[32,128]{1,0:T(8,128)S(1)}) custom-call(s32[72,128]{1,0:T(8,128)S(1)} %get-tuple-element.34.rows, f32[72,128,128]{2,1,0:T(8,128)S(1)} %copy-done, f32[16,128,128]{2,1,0:T(8,128)S(1)} %get-tuple-element.52.wide, f32[16,128]{1,0:T(8,128)S(1)} %get-tuple-element.44.refs_0_.refs_19_, ...), custom_call_target="tpu_custom_call" | custom-call | flops 2359296 | tf_op jit(solution)/shard_map/pallas_call | solution.py:329
  53.1 0.6 collective-permute-done.27
  53.7 1.6 %collective-permute-start.32 = (f32[168,128]{1,0:T(8,128)S(1)}, f32[168,128]{1,0:T(8,128)S(1)}, u32[]{:S(2)}, u32[]{:S(2)}) collective-permute-start(f32[168,128]{1,0:T(8,128)S(1)} %constant_dynamic-update-slice_fusion.10.refs_7_), channel_id=1, source_target_pairs={{0,24},{4,28},{8,16},{12,20},{16,8},{20,12},{24,0},{28,4},{1,25},{... | collective-permute-start | bytes 258056 | tf_op jit(solution)/shard_map/ppermute | solution.py:371
  55.2 0.8 %collective-permute-start.31 = (f32[168,128]{1,0:T(8,128)S(1)}, f32[168,128]{1,0:T(8,128)S(1)}, u32[]{:S(2)}, u32[]{:S(2)}) collective-permute-start(f32[168,128]{1,0:T(8,128)S(1)} %constant_dynamic-update-slice_fusion.10.refs_7_), channel_id=1, source_target_pairs={{0,16},{4,20},{8,24},{12,28},{16,0},{20,4},{24,8},{28,12},{1,17},{... | collective-permute-start | bytes 258056 | tf_op jit(solution)/shard_map/ppermute | solution.py:371
  56.0 1.2 %collective-permute-start.30 = (f32[168,128]{1,0:T(8,128)S(1)}, f32[168,128]{1,0:T(8,128)S(1)}, u32[]{:S(2)}, u32[]{:S(2)}) collective-permute-start(f32[168,128]{1,0:T(8,128)S(1)} %constant_dynamic-update-slice_fusion.10.refs_7_), channel_id=1, source_target_pairs={{0,8},{4,12},{8,0},{12,4},{16,24},{20,28},{24,16},{28,20},{1,9},{5... | collective-permute-start | bytes 258056 | tf_op jit(solution)/shard_map/ppermute | solution.py:371
  57.2 2.6 %collective-permute-done.32.refs_10_ = f32[168,128]{1,0:T(8,128)S(1)} collective-permute-done((f32[168,128]{1,0:T(8,128)S(1)}, f32[168,128]{1,0:T(8,128)S(1)}, u32[]{:S(2)}, u32[]{:S(2)}) %collective-permute-start.32) | collective-permute-done | bytes 86048 | tf_op jit(solution)/shard_map/ppermute | solution.py:371
  59.8 0.6 collective-permute-done.31.refs_9_
  60.3 0.2 collective-permute-done.30.refs_8_
  60.5 0.3 collective-permute-start.34
  60.9 0.2 collective-permute-done.36.refs_14_
  61.1 0.6 collective-permute-done.35.refs_13_
  61.6 0.2 collective-permute-done.34.refs_12_
  61.8 2.4 %shard_map.174 = (f32[16,128]{1,0:T(8,128)}, f32[64,128]{1,0:T(8,128)}, f32[32,128]{1,0:T(8,128)}) custom-call(s32[72]{0:T(128)S(1)} %copy-done.10, s32[24]{0:T(128)S(1)} %copy-done.11, s32[24,128]{1,0:T(8,128)S(1)} %get-tuple-element.33.refs_3_.refs_2_, f32[72,128,128]{2,1,0:T(8,128)S(1)} %copy-done, f32[24,128,128]{2,1,0:T(8,128)S(1)} %copy-done.1, ...), custom_call_target="tpu_custom_call" | custom-call | flops 3145728 | tf_op jit(solution)/shard_map/pallas_call | solution.py:329
  (64 shorter events, 0.2 us)
Async XLA Ops:
  0.6 0.7 %copy-start.5 = (f32[32,128]{1,0:T(8,128)S(1)}, f32[32,128]{1,0:T(8,128)}, u32[]{:S(2)}) copy-start(f32[32,128]{1,0:T(8,128)} %refs_25_.1) | copy-start | bytes 49156
  0.6 0.7 %copy-start.4 = (f32[32,128]{1,0:T(8,128)S(1)}, f32[32,128]{1,0:T(8,128)}, u32[]{:S(2)}) copy-start(f32[32,128]{1,0:T(8,128)} %refs_24_.1) | copy-start | bytes 49156
  0.7 0.8 %copy-start.3 = (f32[64,128]{1,0:T(8,128)S(1)}, f32[64,128]{1,0:T(8,128)}, u32[]{:S(2)}) copy-start(f32[64,128]{1,0:T(8,128)} %refs_22_.1) | copy-start | bytes 98308
  0.7 0.8 %copy-start.2 = (f32[64,128]{1,0:T(8,128)S(1)}, f32[64,128]{1,0:T(8,128)}, u32[]{:S(2)}) copy-start(f32[64,128]{1,0:T(8,128)} %refs_21_.1) | copy-start | bytes 98308
  0.7 0.8 %copy-start.11 = (s32[24]{0:T(128)S(1)}, s32[24]{0:T(128)}, u32[]{:S(2)}) copy-start(s32[24]{0:T(128)} %refs_1_.9) | copy-start | bytes 292
  0.7 1.4 %copy-start.1 = (f32[24,128,128]{2,1,0:T(8,128)S(1)}, f32[24,128,128]{2,1,0:T(8,128)}, u32[]{:S(2)}) copy-start(f32[24,128,128]{2,1,0:T(8,128)} %refs_4_.7) | copy-start | bytes 4718596
  0.7 1.4 %copy-start.10 = (s32[72]{0:T(128)S(1)}, s32[72]{0:T(128)}, u32[]{:S(2)}) copy-start(s32[72]{0:T(128)} %refs_0_.7) | copy-start | bytes 868
  0.7 1.4 %copy-start.9 = (f32[16,128]{1,0:T(8,128)S(1)}, f32[16,128]{1,0:T(8,128)}, u32[]{:S(2)}) copy-start(f32[16,128]{1,0:T(8,128)} %refs_6_.5) | copy-start | bytes 24580
  0.7 1.4 %copy-start.8 = (f32[32,128]{1,0:T(8,128)S(1)}, f32[32,128]{1,0:T(8,128)}, u32[]{:S(2)}) copy-start(f32[32,128]{1,0:T(8,128)} %refs_12_.3) | copy-start | bytes 49156
  0.7 1.4 %copy-start.6 = (f32[64,128]{1,0:T(8,128)S(1)}, f32[64,128]{1,0:T(8,128)}, u32[]{:S(2)}) copy-start(f32[64,128]{1,0:T(8,128)} %refs_9_.3) | copy-start | bytes 98308
  0.7 1.4 %copy-start.14 = (s32[24]{0:T(128)S(1)}, s32[24]{0:T(128)}, u32[]{:S(2)}) copy-start(s32[24]{0:T(128)} %refs_2_.1) | copy-start | bytes 292
  0.7 1.4 %copy-start.13 = (s32[72]{0:T(128)S(1)}, s32[72]{0:T(128)}, u32[]{:S(2)}) copy-start(s32[72]{0:T(128)} %refs_1_.6) | copy-start | bytes 868
  0.8 1.4 %copy-start.12 = (s32[72,1]{0,1:T(1,128)S(1)}, s32[72,1]{0,1:T(1,128)}, u32[]{:S(2)}) copy-start(s32[72,1]{0,1:T(1,128)} %param.17) | copy-start | bytes 868
  0.8 11.0 %copy-start = (f32[72,128,128]{2,1,0:T(8,128)S(1)}, f32[72,128,128]{2,1,0:T(8,128)}, u32[]{:S(2)}) copy-start(f32[72,128,128]{2,1,0:T(8,128)} %refs_3_.5) | copy-start | bytes 14155780
  0.8 25.2 %copy-start.7 = (f32[16,128]{1,0:T(8,128)S(1)}, f32[16,128]{1,0:T(8,128)}, u32[]{:S(2)}) copy-start(f32[16,128]{1,0:T(8,128)} %refs_6_.7) | copy-start | bytes 24580
  3.4 12.0 %collective-permute-start.2 = (f32[40,128]{1,0:T(8,128)S(1)}, f32[40,128]{1,0:T(8,128)S(1)}, u32[]{:S(2)}, u32[]{:S(2)}) collective-permute-start(f32[40,128]{1,0:T(8,128)S(1)} %get-tuple-element.36), channel_id=1, source_target_pairs={{0,3},{1,2},{2,1},{3,0},{4,7},{5,6},{6,5},{7,4},{8,11},{9,10},{10,... | collective-permute-start | bytes 61448 | tf_op jit(solution)/shard_map/ppermute | solution.py:371
  8.5 5.3 %collective-permute-start.1 = (f32[40,128]{1,0:T(8,128)S(1)}, f32[40,128]{1,0:T(8,128)S(1)}, u32[]{:S(2)}, u32[]{:S(2)}) collective-permute-start(f32[40,128]{1,0:T(8,128)S(1)} %get-tuple-element.36), channel_id=1, source_target_pairs={{0,2},{1,3},{2,0},{3,1},{4,6},{5,7},{6,4},{7,5},{8,10},{9,11},{10,... | collective-permute-start | bytes 61448 | tf_op jit(solution)/shard_map/ppermute | solution.py:371
  8.5 4.1 %collective-permute-start = (f32[40,128]{1,0:T(8,128)S(1)}, f32[40,128]{1,0:T(8,128)S(1)}, u32[]{:S(2)}, u32[]{:S(2)}) collective-permute-start(f32[40,128]{1,0:T(8,128)S(1)} %get-tuple-element.36), channel_id=1, source_target_pairs={{0,1},{1,0},{2,3},{3,2},{4,5},{5,4},{6,7},{7,6},{8,9},{9,8},{10,11... | collective-permute-start | bytes 61448 | tf_op jit(solution)/shard_map/ppermute | solution.py:371
  9.2 7.1 %collective-permute-start.13 = (f32[200,128]{1,0:T(8,128)S(1)}, f32[200,128]{1,0:T(8,128)S(1)}, u32[]{:S(2)}, u32[]{:S(2)}) collective-permute-start(f32[200,128]{1,0:T(8,128)S(1)} %get-tuple-element.37.refs_2_.refs_16_), channel_id=1, source_target_pairs={{0,4},{4,0},{8,12},{12,8},{16,20},{20,16},{24,28},{28,24},{1,5},{5... | collective-permute-start | bytes 307208 | tf_op jit(solution)/shard_map/ppermute | solution.py:371
  9.2 8.2 %collective-permute-start.12 = (f32[200,128]{1,0:T(8,128)S(1)}, f32[200,128]{1,0:T(8,128)S(1)}, u32[]{:S(2)}, u32[]{:S(2)}) collective-permute-start(f32[200,128]{1,0:T(8,128)S(1)} %get-tuple-element.37.refs_2_.refs_16_), channel_id=1, source_target_pairs={{0,24},{4,28},{8,16},{12,20},{16,8},{20,12},{24,0},{28,4},{1,25},{... | collective-permute-start | bytes 307208 | tf_op jit(solution)/shard_map/ppermute | solution.py:371
  12.6 6.3 %collective-permute-start.11 = (f32[200,128]{1,0:T(8,128)S(1)}, f32[200,128]{1,0:T(8,128)S(1)}, u32[]{:S(2)}, u32[]{:S(2)}) collective-permute-start(f32[200,128]{1,0:T(8,128)S(1)} %get-tuple-element.37.refs_2_.refs_16_), channel_id=1, source_target_pairs={{0,16},{4,20},{8,24},{12,28},{16,0},{20,4},{24,8},{28,12},{1,17},{... | collective-permute-start | bytes 307208 | tf_op jit(solution)/shard_map/ppermute | solution.py:371
  13.8 5.8 %collective-permute-start.10 = (f32[200,128]{1,0:T(8,128)S(1)}, f32[200,128]{1,0:T(8,128)S(1)}, u32[]{:S(2)}, u32[]{:S(2)}) collective-permute-start(f32[200,128]{1,0:T(8,128)S(1)} %get-tuple-element.37.refs_2_.refs_16_), channel_id=1, source_target_pairs={{0,8},{4,12},{8,0},{12,4},{16,24},{20,28},{24,16},{28,20},{1,9},{5... | collective-permute-start | bytes 307208 | tf_op jit(solution)/shard_map/ppermute | solution.py:371
  15.3 7.1 %collective-permute-start.5 = (f32[232,128]{1,0:T(8,128)S(1)}, f32[232,128]{1,0:T(8,128)S(1)}, u32[]{:S(2)}, u32[]{:S(2)}) collective-permute-start(f32[232,128]{1,0:T(8,128)S(1)} %constant_dynamic-update-slice_fusion.refs_8_.refs_1_), channel_id=1, source_target_pairs={{0,24},{4,28},{8,16},{12,20},{16,8},{20,12},{24,0},{28,4},{1,25},{... | collective-permute-start | bytes 356360 | tf_op jit(solution)/shard_map/ppermute | solution.py:371
  16.3 6.8 %collective-permute-start.4 = (f32[232,128]{1,0:T(8,128)S(1)}, f32[232,128]{1,0:T(8,128)S(1)}, u32[]{:S(2)}, u32[]{:S(2)}) collective-permute-start(f32[232,128]{1,0:T(8,128)S(1)} %constant_dynamic-update-slice_fusion.refs_8_.refs_1_), channel_id=1, source_target_pairs={{0,16},{4,20},{8,24},{12,28},{16,0},{20,4},{24,8},{28,12},{1,17},{... | collective-permute-start | bytes 356360 | tf_op jit(solution)/shard_map/ppermute | solution.py:371
  17.4 5.8 %collective-permute-start.3 = (f32[232,128]{1,0:T(8,128)S(1)}, f32[232,128]{1,0:T(8,128)S(1)}, u32[]{:S(2)}, u32[]{:S(2)}) collective-permute-start(f32[232,128]{1,0:T(8,128)S(1)} %constant_dynamic-update-slice_fusion.refs_8_.refs_1_), channel_id=1, source_target_pairs={{0,8},{4,12},{8,0},{12,4},{16,24},{20,28},{24,16},{28,20},{1,9},{5... | collective-permute-start | bytes 356360 | tf_op jit(solution)/shard_map/ppermute | solution.py:371
  18.9 4.7 %collective-permute-start.16 = (f32[200,128]{1,0:T(8,128)S(1)}, f32[200,128]{1,0:T(8,128)S(1)}, u32[]{:S(2)}, u32[]{:S(2)}) collective-permute-start(f32[200,128]{1,0:T(8,128)S(1)} %collective-permute-done.12.refs_5_.refs_19_), channel_id=1, source_target_pairs={{0,4},{4,0},{8,12},{12,8},{16,20},{20,16},{24,28},{28,24},{1,5},{5... | collective-permute-start | bytes 307208 | tf_op jit(solution)/shard_map/ppermute | solution.py:371
  19.6 4.1 %collective-permute-start.15 = (f32[200,128]{1,0:T(8,128)S(1)}, f32[200,128]{1,0:T(8,128)S(1)}, u32[]{:S(2)}, u32[]{:S(2)}) collective-permute-start(f32[200,128]{1,0:T(8,128)S(1)} %collective-permute-done.11.refs_4_.refs_18_), channel_id=1, source_target_pairs={{0,4},{4,0},{8,12},{12,8},{16,20},{20,16},{24,28},{28,24},{1,5},{5... | collective-permute-start | bytes 307208 | tf_op jit(solution)/shard_map/ppermute | solution.py:371
  22.5 3.5 %collective-permute-start.6 = (f32[232,128]{1,0:T(8,128)S(1)}, f32[232,128]{1,0:T(8,128)S(1)}, u32[]{:S(2)}, u32[]{:S(2)}) collective-permute-start(f32[232,128]{1,0:T(8,128)S(1)} %constant_dynamic-update-slice_fusion.refs_8_.refs_1_), channel_id=1, source_target_pairs={{0,4},{4,0},{8,12},{12,8},{16,20},{20,16},{24,28},{28,24},{1,5},{5... | collective-permute-start | bytes 356360 | tf_op jit(solution)/shard_map/ppermute | solution.py:371
  23.1 2.9 %collective-permute-start.9 = (f32[232,128]{1,0:T(8,128)S(1)}, f32[232,128]{1,0:T(8,128)S(1)}, u32[]{:S(2)}, u32[]{:S(2)}) collective-permute-start(f32[232,128]{1,0:T(8,128)S(1)} %collective-permute-done.5.refs_11_.refs_4_), channel_id=1, source_target_pairs={{0,4},{4,0},{8,12},{12,8},{16,20},{20,16},{24,28},{28,24},{1,5},{5... | collective-permute-start | bytes 356360 | tf_op jit(solution)/shard_map/ppermute | solution.py:371
  23.2 2.8 %collective-permute-start.8 = (f32[232,128]{1,0:T(8,128)S(1)}, f32[232,128]{1,0:T(8,128)S(1)}, u32[]{:S(2)}, u32[]{:S(2)}) collective-permute-start(f32[232,128]{1,0:T(8,128)S(1)} %collective-permute-done.4.refs_10_.refs_3_), channel_id=1, source_target_pairs={{0,4},{4,0},{8,12},{12,8},{16,20},{20,16},{24,28},{28,24},{1,5},{5... | collective-permute-start | bytes 356360 | tf_op jit(solution)/shard_map/ppermute | solution.py:371
  23.6 2.4 %collective-permute-start.7 = (f32[232,128]{1,0:T(8,128)S(1)}, f32[232,128]{1,0:T(8,128)S(1)}, u32[]{:S(2)}, u32[]{:S(2)}) collective-permute-start(f32[232,128]{1,0:T(8,128)S(1)} %collective-permute-done.3.refs_9_.refs_2_), channel_id=1, source_target_pairs={{0,4},{4,0},{8,12},{12,8},{16,20},{20,16},{24,28},{28,24},{1,5},{5... | collective-permute-start | bytes 356360 | tf_op jit(solution)/shard_map/ppermute | solution.py:371
  23.7 1.4 %collective-permute-start.14 = (f32[200,128]{1,0:T(8,128)S(1)}, f32[200,128]{1,0:T(8,128)S(1)}, u32[]{:S(2)}, u32[]{:S(2)}) collective-permute-start(f32[200,128]{1,0:T(8,128)S(1)} %collective-permute-done.10.refs_3_.refs_17_), channel_id=1, source_target_pairs={{0,4},{4,0},{8,12},{12,8},{16,20},{20,16},{24,28},{28,24},{1,5},{5... | collective-permute-start | bytes 307208 | tf_op jit(solution)/shard_map/ppermute | solution.py:371
  28.7 8.3 %collective-permute-start.19 = (f32[24,128]{1,0:T(8,128)S(1)}, f32[24,128]{1,0:T(8,128)S(1)}, u32[]{:S(2)}, u32[]{:S(2)}) collective-permute-start(f32[24,128]{1,0:T(8,128)S(1)} %get-tuple-element.46), channel_id=1, source_target_pairs={{0,3},{1,2},{2,1},{3,0},{4,7},{5,6},{6,5},{7,4},{8,11},{9,10},{10,... | collective-permute-start | bytes 36872 | tf_op jit(solution)/shard_map/ppermute | solution.py:371
  32.4 4.6 %collective-permute-start.18 = (f32[24,128]{1,0:T(8,128)S(1)}, f32[24,128]{1,0:T(8,128)S(1)}, u32[]{:S(2)}, u32[]{:S(2)}) collective-permute-start(f32[24,128]{1,0:T(8,128)S(1)} %get-tuple-element.46), channel_id=1, source_target_pairs={{0,2},{1,3},{2,0},{3,1},{4,6},{5,7},{6,4},{7,5},{8,10},{9,11},{10,... | collective-permute-start | bytes 36872 | tf_op jit(solution)/shard_map/ppermute | solution.py:371
  32.4 3.8 %collective-permute-start.17 = (f32[24,128]{1,0:T(8,128)S(1)}, f32[24,128]{1,0:T(8,128)S(1)}, u32[]{:S(2)}, u32[]{:S(2)}) collective-permute-start(f32[24,128]{1,0:T(8,128)S(1)} %get-tuple-element.46), channel_id=1, source_target_pairs={{0,1},{1,0},{2,3},{3,2},{4,5},{5,4},{6,7},{7,6},{8,9},{9,8},{10,11... | collective-permute-start | bytes 36872 | tf_op jit(solution)/shard_map/ppermute | solution.py:371
  37.0 6.3 %collective-permute-start.22 = (f32[168,128]{1,0:T(8,128)S(1)}, f32[168,128]{1,0:T(8,128)S(1)}, u32[]{:S(2)}, u32[]{:S(2)}) collective-permute-start(f32[168,128]{1,0:T(8,128)S(1)} %constant_dynamic-update-slice_fusion.5.refs_7_.refs_1_), channel_id=1, source_target_pairs={{0,24},{4,28},{8,16},{12,20},{16,8},{20,12},{24,0},{28,4},{1,25},{... | collective-permute-start | bytes 258056 | tf_op jit(solution)/shard_map/ppermute | solution.py:371
  39.2 4.8 %collective-permute-start.21 = (f32[168,128]{1,0:T(8,128)S(1)}, f32[168,128]{1,0:T(8,128)S(1)}, u32[]{:S(2)}, u32[]{:S(2)}) collective-permute-start(f32[168,128]{1,0:T(8,128)S(1)} %constant_dynamic-update-slice_fusion.5.refs_7_.refs_1_), channel_id=1, source_target_pairs={{0,16},{4,20},{8,24},{12,28},{16,0},{20,4},{24,8},{28,12},{1,17},{... | collective-permute-start | bytes 258056 | tf_op jit(solution)/shard_map/ppermute | solution.py:371
  39.7 4.5 %collective-permute-start.20 = (f32[168,128]{1,0:T(8,128)S(1)}, f32[168,128]{1,0:T(8,128)S(1)}, u32[]{:S(2)}, u32[]{:S(2)}) collective-permute-start(f32[168,128]{1,0:T(8,128)S(1)} %constant_dynamic-update-slice_fusion.5.refs_7_.refs_1_), channel_id=1, source_target_pairs={{0,8},{4,12},{8,0},{12,4},{16,24},{20,28},{24,16},{28,20},{1,9},{5... | collective-permute-start | bytes 258056 | tf_op jit(solution)/shard_map/ppermute | solution.py:371
  40.5 3.9 %collective-permute-start.23 = (f32[168,128]{1,0:T(8,128)S(1)}, f32[168,128]{1,0:T(8,128)S(1)}, u32[]{:S(2)}, u32[]{:S(2)}) collective-permute-start(f32[168,128]{1,0:T(8,128)S(1)} %constant_dynamic-update-slice_fusion.5.refs_7_.refs_1_), channel_id=1, source_target_pairs={{0,4},{4,0},{8,12},{12,8},{16,20},{20,16},{24,28},{28,24},{1,5},{5... | collective-permute-start | bytes 258056 | tf_op jit(solution)/shard_map/ppermute | solution.py:371
  43.3 1.3 %collective-permute-start.26 = (f32[168,128]{1,0:T(8,128)S(1)}, f32[168,128]{1,0:T(8,128)S(1)}, u32[]{:S(2)}, u32[]{:S(2)}) collective-permute-start(f32[168,128]{1,0:T(8,128)S(1)} %collective-permute-done.22.refs_10_.refs_4_), channel_id=1, source_target_pairs={{0,4},{4,0},{8,12},{12,8},{16,20},{20,16},{24,28},{28,24},{1,5},{5... | collective-permute-start | bytes 258056 | tf_op jit(solution)/shard_map/ppermute | solution.py:371
  43.9 1.3 %collective-permute-start.25 = (f32[168,128]{1,0:T(8,128)S(1)}, f32[168,128]{1,0:T(8,128)S(1)}, u32[]{:S(2)}, u32[]{:S(2)}) collective-permute-start(f32[168,128]{1,0:T(8,128)S(1)} %collective-permute-done.21.refs_9_.refs_3_), channel_id=1, source_target_pairs={{0,4},{4,0},{8,12},{12,8},{16,20},{20,16},{24,28},{28,24},{1,5},{5... | collective-permute-start | bytes 258056 | tf_op jit(solution)/shard_map/ppermute | solution.py:371
  44.1 1.3 %collective-permute-start.24 = (f32[168,128]{1,0:T(8,128)S(1)}, f32[168,128]{1,0:T(8,128)S(1)}, u32[]{:S(2)}, u32[]{:S(2)}) collective-permute-start(f32[168,128]{1,0:T(8,128)S(1)} %collective-permute-done.20.refs_8_.refs_2_), channel_id=1, source_target_pairs={{0,4},{4,0},{8,12},{12,8},{16,20},{20,16},{24,28},{28,24},{1,5},{5... | collective-permute-start | bytes 258056 | tf_op jit(solution)/shard_map/ppermute | solution.py:371
  47.4 6.3 %collective-permute-start.29 = (f32[24,128]{1,0:T(8,128)S(1)}, f32[24,128]{1,0:T(8,128)S(1)}, u32[]{:S(2)}, u32[]{:S(2)}) collective-permute-start(f32[24,128]{1,0:T(8,128)S(1)} %get-tuple-element.56), channel_id=1, source_target_pairs={{0,3},{1,2},{2,1},{3,0},{4,7},{5,6},{6,5},{7,4},{8,11},{9,10},{10,... | collective-permute-start | bytes 36872 | tf_op jit(solution)/shard_map/ppermute | solution.py:371
  48.9 4.7 %collective-permute-start.28 = (f32[24,128]{1,0:T(8,128)S(1)}, f32[24,128]{1,0:T(8,128)S(1)}, u32[]{:S(2)}, u32[]{:S(2)}) collective-permute-start(f32[24,128]{1,0:T(8,128)S(1)} %get-tuple-element.56), channel_id=1, source_target_pairs={{0,2},{1,3},{2,0},{3,1},{4,6},{5,7},{6,4},{7,5},{8,10},{9,11},{10,... | collective-permute-start | bytes 36872 | tf_op jit(solution)/shard_map/ppermute | solution.py:371
  49.5 4.1 %collective-permute-start.27 = (f32[24,128]{1,0:T(8,128)S(1)}, f32[24,128]{1,0:T(8,128)S(1)}, u32[]{:S(2)}, u32[]{:S(2)}) collective-permute-start(f32[24,128]{1,0:T(8,128)S(1)} %get-tuple-element.56), channel_id=1, source_target_pairs={{0,1},{1,0},{2,3},{3,2},{4,5},{5,4},{6,7},{7,6},{8,9},{9,8},{10,11... | collective-permute-start | bytes 36872 | tf_op jit(solution)/shard_map/ppermute | solution.py:371
  53.7 6.1 %collective-permute-start.32 = (f32[168,128]{1,0:T(8,128)S(1)}, f32[168,128]{1,0:T(8,128)S(1)}, u32[]{:S(2)}, u32[]{:S(2)}) collective-permute-start(f32[168,128]{1,0:T(8,128)S(1)} %constant_dynamic-update-slice_fusion.10.refs_7_), channel_id=1, source_target_pairs={{0,24},{4,28},{8,16},{12,20},{16,8},{20,12},{24,0},{28,4},{1,25},{... | collective-permute-start | bytes 258056 | tf_op jit(solution)/shard_map/ppermute | solution.py:371
  55.2 5.1 %collective-permute-start.31 = (f32[168,128]{1,0:T(8,128)S(1)}, f32[168,128]{1,0:T(8,128)S(1)}, u32[]{:S(2)}, u32[]{:S(2)}) collective-permute-start(f32[168,128]{1,0:T(8,128)S(1)} %constant_dynamic-update-slice_fusion.10.refs_7_), channel_id=1, source_target_pairs={{0,16},{4,20},{8,24},{12,28},{16,0},{20,4},{24,8},{28,12},{1,17},{... | collective-permute-start | bytes 258056 | tf_op jit(solution)/shard_map/ppermute | solution.py:371
  56.0 4.5 %collective-permute-start.30 = (f32[168,128]{1,0:T(8,128)S(1)}, f32[168,128]{1,0:T(8,128)S(1)}, u32[]{:S(2)}, u32[]{:S(2)}) collective-permute-start(f32[168,128]{1,0:T(8,128)S(1)} %constant_dynamic-update-slice_fusion.10.refs_7_), channel_id=1, source_target_pairs={{0,8},{4,12},{8,0},{12,4},{16,24},{20,28},{24,16},{28,20},{1,9},{5... | collective-permute-start | bytes 258056 | tf_op jit(solution)/shard_map/ppermute | solution.py:371
  57.2 3.7 %collective-permute-start.33 = (f32[168,128]{1,0:T(8,128)S(1)}, f32[168,128]{1,0:T(8,128)S(1)}, u32[]{:S(2)}, u32[]{:S(2)}) collective-permute-start(f32[168,128]{1,0:T(8,128)S(1)} %constant_dynamic-update-slice_fusion.10.refs_7_), channel_id=1, source_target_pairs={{0,4},{4,0},{8,12},{12,8},{16,20},{20,16},{24,28},{28,24},{1,5},{5... | collective-permute-start | bytes 258056 | tf_op jit(solution)/shard_map/ppermute | solution.py:371
  59.8 1.3 %collective-permute-start.36 = (f32[168,128]{1,0:T(8,128)S(1)}, f32[168,128]{1,0:T(8,128)S(1)}, u32[]{:S(2)}, u32[]{:S(2)}) collective-permute-start(f32[168,128]{1,0:T(8,128)S(1)} %collective-permute-done.32.refs_10_), channel_id=1, source_target_pairs={{0,4},{4,0},{8,12},{12,8},{16,20},{20,16},{24,28},{28,24},{1,5},{5... | collective-permute-start | bytes 258056 | tf_op jit(solution)/shard_map/ppermute | solution.py:371
  60.3 1.3 %collective-permute-start.35 = (f32[168,128]{1,0:T(8,128)S(1)}, f32[168,128]{1,0:T(8,128)S(1)}, u32[]{:S(2)}, u32[]{:S(2)}) collective-permute-start(f32[168,128]{1,0:T(8,128)S(1)} %collective-permute-done.31.refs_9_), channel_id=1, source_target_pairs={{0,4},{4,0},{8,12},{12,8},{16,20},{20,16},{24,28},{28,24},{1,5},{5... | collective-permute-start | bytes 258056 | tf_op jit(solution)/shard_map/ppermute | solution.py:371
  60.5 1.3 %collective-permute-start.34 = (f32[168,128]{1,0:T(8,128)S(1)}, f32[168,128]{1,0:T(8,128)S(1)}, u32[]{:S(2)}, u32[]{:S(2)}) collective-permute-start(f32[168,128]{1,0:T(8,128)S(1)} %collective-permute-done.30.refs_8_), channel_id=1, source_target_pairs={{0,4},{4,0},{8,12},{12,8},{16,20},{20,16},{24,28},{28,24},{1,5},{5... | collective-permute-start | bytes 258056 | tf_op jit(solution)/shard_map/ppermute | solution.py:371
